TPU v7x, 512 devices: a 8x2x16 block of a 8x8x16 slice. The times are simulated.
512 devices in a mesh: grp: 2 (over y), ha: 16 (over z), wa: 8 (over x), ta: 2 (over core).
Axes of the slice: x: 8, y: 2, z: 16, core: 2. Of those that a mesh axis runs over, the one named last changes fastest.
The devices are a block of a 8x8x16 slice.
Arguments:
- frames: bfloat16 [8, 96, 64, 1024], P(('grp', 'ta'), None, 'ha', 'wa'), parts along dimension 0, may hold values from -14 to 14
- cache_in: bfloat16 [4, 96, 64, 1024], P('grp', None, 'ha', 'wa'), parts along dimension 0, may hold values from -4 to 4
- cache_mid: bfloat16 [4, 96, 64, 1024], P('grp', None, 'ha', 'wa'), parts along dimension 0, may hold values from -4 to 4
- gain_in: float32 [96], replicated, may hold values from 0.25 to 1.75
- gain_mid: float32 [96], replicated, may hold values from 0.25 to 1.75
- weight_in: bfloat16 [3, 3, 96, 288], replicated, may hold values from -0.125 to 0.125
- bias_in: float32 [96], replicated, may hold values from -3 to 3
- weight_mid: bfloat16 [3, 3, 96, 288], replicated, may hold values from -0.125 to 0.125
- bias_mid: float32 [96], replicated, may hold values from -3 to 3
- cotangent: bfloat16 [8, 96, 64, 1024], P(('grp', 'ta'), None, 'ha', 'wa'), parts along dimension 0, may hold values from -6 to 6
Outputs:
- decoded: bfloat16 [8, 96, 64, 1024], P(('grp', 'ta'), None, 'ha', 'wa'), parts along dimension 0
- input_grad: float32 [8, 96, 64, 1024], P(('grp', 'ta'), None, 'ha', 'wa'), parts along dimension 0
There are 2 independent parts, one for each index of `grp`. A program takes and returns all parts, laid end to end along the dimension named above; an argument that names none is the same for every part. Nothing has to cross between parts.
All inputs are finite; a program needn't handle non-finite values.
Results may differ from a plain program's by a relative error of at most 0.006.
Values may be sent and summed in bfloat16 or wider, within the bound.
No kernel may reach another device: no remote copies, remote signals or barrier semaphores. Data moves between devices by JAX's collectives and lax.ppermute only.
A program may use at most 64 MiB of HBM per device.

v0:
```python
import jax
import jax.numpy as jnp
from jax import lax
from jax.sharding import PartitionSpec as P

epsilon = 1e-06


def passed_along(value, axis, steps):
    count = lax.axis_size(axis)
    leading, last = (max(0, -steps), min(count, count - steps))
    return lax.ppermute(value, axis, [(source, source + steps) for source in range(leading, last)])


def extended_2(array, sides, width):
    for axis, dim in sides:
        peers, length = (lax.axis_size(axis), array.shape[dim])
        up = [(i, (i + 1) % peers) for i in range(peers - 1)]
        down = [(j, i) for i, j in up]
        last = lax.slice_in_dim(array, length - width, length, axis=dim)
        leading = lax.slice_in_dim(array, 0, width, axis=dim)
        before = lax.ppermute(last, axis, up)
        after = lax.ppermute(leading, axis, down)
        array = jnp.concatenate([before, array, after], axis=dim)
    return array


def activate(values, gain):
    values = values.astype(jnp.float32)
    mean_square = jnp.mean(values * values, axis=1, keepdims=True)
    scaled = values * lax.rsqrt(mean_square + epsilon) * gain[None, :, None, None]
    return jax.nn.silu(scaled)


def act_back(values, gain, upstream):
    values = values.astype(jnp.float32)
    mean_square = jnp.mean(values * values, axis=1, keepdims=True)
    inverse = lax.rsqrt(mean_square + epsilon)
    gains = gain[None, :, None, None]
    scaled = values * inverse * gains
    sigmoid_part = jax.nn.sigmoid(scaled)
    weighted = gains * upstream * sigmoid_part * (1.0 + scaled * (1.0 - sigmoid_part))
    return inverse * weighted - values * inverse**3 * jnp.mean(
        weighted * values, axis=1, keepdims=True
    )


def flipped(weight):
    channels = weight.shape[2]
    five = weight.reshape(3, 3, channels, 3, channels)[::-1, ::-1, :, ::-1, :]
    return jnp.transpose(five, (0, 1, 4, 3, 2)).reshape(3, 3, channels, 3 * channels)


def convolve(padded, weight):
    count_frames = padded.shape[0] - 2
    height = padded.shape[2] - 2
    width = padded.shape[3] - 2
    stacked = jnp.concatenate(
        [padded[time_tap : time_tap + count_frames] for time_tap in range(3)], 1
    )
    summed = jnp.zeros((count_frames, weight.shape[2], height, width), jnp.float32)
    for row_tap in range(3):
        for col_tap in range(3):
            summed = summed + jnp.einsum(
                "ok,fkhw->fohw",
                weight[row_tap, col_tap],
                stacked[:, :, row_tap : row_tap + height, col_tap : col_tap + width],
                preferred_element_type=jnp.float32,
            )
    return summed


def earlier(values):
    return passed_along(values, "ta", 1)


def following(values):
    return passed_along(values, "ta", -1)


def inside_window(height, width):
    rows = lax.axis_index("ha") * height + jnp.arange(-1, height + 1, dtype=jnp.int32)
    cols = lax.axis_index("wa") * width + jnp.arange(-1, width + 1, dtype=jnp.int32)
    row_ok = (rows >= 0) & (rows < height * lax.axis_size("ha"))
    col_ok = (cols >= 0) & (cols < width * lax.axis_size("wa"))
    return (row_ok[:, None] & col_ok[None, :])[None, None]


def per_device(
    frames,
    cache_in,
    cache_mid,
    gain_in,
    gain_mid,
    weight_in,
    bias_in,
    weight_mid,
    bias_mid,
    cotangent,
):
    at_start = lax.axis_index("ta") == 0
    count_frames = frames.shape[0]
    height = frames.shape[2]
    width = frames.shape[3]
    stacked_inputs = jnp.concatenate(
        [earlier(frames), frames, cache_in, cache_mid, cotangent, following(cotangent)], 0
    )
    extended = extended_2(stacked_inputs, (("ha", 2), ("wa", 3)), 2)
    raw_part = extended[: count_frames + 2]
    cache_in_wide = extended[count_frames + 2 : count_frames + 4]
    cache_mid_cycle = extended[count_frames + 4 : count_frames + 6, :, 1:-1, 1:-1]
    padded_grad = extended[count_frames + 6 :]
    activated = activate(raw_part, gain_in).astype(jnp.bfloat16)
    padded_in = jnp.concatenate(
        [jnp.where(at_start, cache_in_wide, activated[:2]), activated[2:]], 0
    )
    hidden_cycle = (convolve(padded_in, weight_in) + bias_in[None, :, None, None]).astype(
        jnp.bfloat16
    )
    window_mask = inside_window(height, width)
    zero_mid = jnp.zeros((), jnp.bfloat16)
    active_cycle = jnp.where(
        window_mask, activate(hidden_cycle, gain_mid).astype(jnp.bfloat16), zero_mid
    )
    arrived_cycle = earlier(active_cycle)
    padded_mid = jnp.concatenate(
        [jnp.where(at_start, cache_mid_cycle, arrived_cycle), active_cycle], 0
    )
    residual = convolve(padded_mid, weight_mid) + bias_mid[None, :, None, None]
    decoded = (frames.astype(jnp.float32) + residual).astype(jnp.bfloat16)
    back_cycle = convolve(padded_grad, flipped(weight_mid))
    d_cycle = jnp.where(
        window_mask, act_back(hidden_cycle, gain_mid, back_cycle).astype(jnp.bfloat16), zero_mid
    )
    padded_back = jnp.concatenate([d_cycle, following(d_cycle)], 0)
    back_in = convolve(padded_back, flipped(weight_in))
    input_grad = cotangent.astype(jnp.float32) + act_back(frames, gain_in, back_in)
    return (decoded, input_grad)


def solution(mesh):
    placed = (
        P(("grp", "ta"), None, "ha", "wa"),
        P("grp", None, "ha", "wa"),
        P("grp", None, "ha", "wa"),
        P(),
        P(),
        P(),
        P(),
        P(),
        P(),
        P(("grp", "ta"), None, "ha", "wa"),
    )
    return jax.shard_map(
        per_device,
        mesh=mesh,
        in_specs=placed,
        out_specs=(P(("grp", "ta"), None, "ha", "wa"), P(("grp", "ta"), None, "ha", "wa")),
        check_vma=False,
    )
```

profile of v0, /device:TPU:65, one launch (start us, length us, event | category | flops | bytes accessed | tf_op | source)
XLA Modules:
  0.0 118.9 jit_solution(6275039867199575277)
XLA Ops:
  0.6 1.1 copy.93
  1.7 1.3 %collective-permute-start = (bf16[2,96,4,128]{1,3,2,0:T(8,128)(2,1)S(1)}, bf16[2,96,4,128]{1,3,2,0:T(8,128)(2,1)S(1)}, u32[]{:S(2)}, u32[]{:S(2)}) collective-permute-start(bf16[2,96,4,128]{1,3,2,0:T(8,128)(2,1)S(1)} %copy.93), channel_id=1, source_target_pairs={{0,1},{2,3},{4,5},{6,7},{8,9},{10,11},{12,13},{14,15},{16,17},{18,... | collective-permute-start | bytes 589832 | tf_op jit(solution)/shard_map/ppermute | solution.py:12
  3.1 1.1 copy.98
  4.2 43.4 %collective-permute-start.1 = (bf16[2,96,4,128]{1,3,2,0:T(8,128)(2,1)S(1)}, bf16[2,96,4,128]{1,3,2,0:T(8,128)(2,1)S(1)}, u32[]{:S(2)}, u32[]{:S(2)}) collective-permute-start(bf16[2,96,4,128]{1,3,2,0:T(8,128)(2,1)S(1)} %copy.98), channel_id=1, source_target_pairs={{1,0},{3,2},{5,4},{7,6},{9,8},{11,10},{13,12},{15,14},{17,16},{19,... | collective-permute-start | bytes 589832 | tf_op jit(solution)/shard_map/ppermute | solution.py:12
  47.6 1.1 copy.96
  48.7 1.1 copy.97
  50.2 1.1 copy.99
  51.3 2.3 %collective-permute-start.2 = (bf16[12,96,2,128]{3,1,2,0:T(8,128)(2,1)}, bf16[12,96,2,128]{3,1,2,0:T(8,128)(2,1)}, u32[]{:S(2)}, u32[]{:S(2)}) collective-permute-start(bf16[12,96,2,128]{3,1,2,0:T(8,128)(2,1)} %copy.99), channel_id=1, source_target_pairs={{0,16},{16,32},{32,48},{48,64},{64,80},{80,96},{96,112},{112,128},... | collective-permute-start | bytes 1769480 | tf_op jit(solution)/shard_map/ppermute | solution.py:22
  53.5 1.1 copy.100
  54.6 1.3 %collective-permute-start.3 = (bf16[12,96,2,128]{3,1,2,0:T(8,128)(2,1)}, bf16[12,96,2,128]{3,1,2,0:T(8,128)(2,1)}, u32[]{:S(2)}, u32[]{:S(2)}) collective-permute-start(bf16[12,96,2,128]{3,1,2,0:T(8,128)(2,1)} %copy.100), channel_id=1, source_target_pairs={{16,0},{32,16},{48,32},{64,48},{80,64},{96,80},{112,96},{128,112},... | collective-permute-start | bytes 1769480 | tf_op jit(solution)/shard_map/ppermute | solution.py:23
  55.9 1.4 %copy.113 = bf16[3,3,96,288]{2,3,1,0:T(8,128)(2,1)S(1)} copy(bf16[3,3,96,288]{3,2,1,0:T(8,128)(2,1)} %param.17) | data formatting | bytes 995328 | tf_op args[7]
  57.4 1.2 copy.124
  58.6 0.9 reverse_bitcast_fusion.1
  59.5 6.2 %collective-permute-done.2 = bf16[12,96,2,128]{3,1,2,0:T(8,128)(2,1)} collective-permute-done((bf16[12,96,2,128]{3,1,2,0:T(8,128)(2,1)}, bf16[12,96,2,128]{3,1,2,0:T(8,128)(2,1)}, u32[]{:S(2)}, u32[]{:S(2)}) %collective-permute-start.2) | collective-permute-done | bytes 589856 | tf_op jit(solution)/shard_map/ppermute | solution.py:22
  65.7 1.4 %copy.101 = bf16[12,96,2,128]{1,3,2,0:T(8,128)(2,1)S(1)} copy(bf16[12,96,2,128]{3,1,2,0:T(8,128)(2,1)} %collective-permute-done.2) | data formatting | bytes 1179648 | tf_op jit(solution)/shard_map/ppermute | solution.py:22
  67.1 4.7 %collective-permute-done.3 = bf16[12,96,2,128]{3,1,2,0:T(8,128)(2,1)} collective-permute-done((bf16[12,96,2,128]{3,1,2,0:T(8,128)(2,1)}, bf16[12,96,2,128]{3,1,2,0:T(8,128)(2,1)}, u32[]{:S(2)}, u32[]{:S(2)}) %collective-permute-start.3) | collective-permute-done | bytes 589856 | tf_op jit(solution)/shard_map/ppermute | solution.py:23
  71.8 1.4 %copy.102 = bf16[12,96,2,128]{1,3,2,0:T(8,128)(2,1)S(1)} copy(bf16[12,96,2,128]{3,1,2,0:T(8,128)(2,1)} %collective-permute-done.3) | data formatting | bytes 1179648 | tf_op jit(solution)/shard_map/ppermute | solution.py:23
  73.4 1.4 %collective-permute-start.4 = (bf16[12,96,8,2]{1,3,2,0:T(2,128)(2,1)S(1)}, bf16[12,96,8,2]{1,3,2,0:T(2,128)(2,1)S(1)}, u32[]{:S(2)}, u32[]{:S(2)}) collective-permute-start(bf16[12,96,8,2]{1,3,2,0:T(2,128)(2,1)S(1)} %get-tuple-element.8), channel_id=1, source_target_pairs={{0,2},{2,4},{4,6},{6,8},{8,10},{10,12},{12,14},{1,3},{3,5},{5,7},{... | collective-permute-start | bytes 110600 | tf_op jit(solution)/shard_map/ppermute | solution.py:22
  74.8 1.5 %collective-permute-start.5 = (bf16[12,96,8,2]{1,3,2,0:T(2,128)(2,1)S(1)}, bf16[12,96,8,2]{1,3,2,0:T(2,128)(2,1)S(1)}, u32[]{:S(2)}, u32[]{:S(2)}) collective-permute-start(bf16[12,96,8,2]{1,3,2,0:T(2,128)(2,1)S(1)} %get-tuple-element.9), channel_id=1, source_target_pairs={{2,0},{4,2},{6,4},{8,6},{10,8},{12,10},{14,12},{3,1},{5,3},{7,5},{... | collective-permute-start | bytes 110600 | tf_op jit(solution)/shard_map/ppermute | solution.py:23
  76.3 0.9 reverse_bitcast_fusion
  77.2 2.2 %copy.114 = bf16[3,3,96,3,96]{2,4,3,1,0:T(8,128)(2,1)} copy(bf16[3,3,96,3,96]{4,2,3,1,0:T(8,128)(2,1)} %reverse_bitcast_fusion.1) | data formatting | bytes 995328 | tf_op jit(solution)/shard_map/transpose | solution.py:51
  79.4 2.2 %copy.125 = bf16[3,3,96,3,96]{2,4,3,1,0:T(8,128)(2,1)} copy(bf16[3,3,96,3,96]{4,2,3,1,0:T(8,128)(2,1)} %reverse_bitcast_fusion) | data formatting | bytes 995328 | tf_op jit(solution)/shard_map/transpose | solution.py:51
  81.6 4.1 %fusion.8 = bf16[2,288,8,132]{1,3,2,0:T(8,128)(2,1)S(1)} fusion(bf16[12,96,8,2]{1,3,2,0:T(2,128)(2,1)S(1)} %collective-permute-done.5, bf16[12,96,8,2]{1,3,2,0:T(2,128)(2,1)S(1)} %collective-permute-done.4, bf16[12,96,2,128]{1,3,2,0:T(8,128)(2,1)S(1)} %copy.102, bf16[12,96,4,128]{1,3,2,0:T(8,128)(2,1)S(1)} %constant_dynamic-update-slice_fusion, ...), kind=kLoop, calls=%fused_computation.12 | loop fusion | flops 18247680 | bytes 3649536 | tf_op jit(solution)/shard_map/concatenate | solution.py:58
  85.8 0.6 fusion.29
  86.4 0.6 fusion.31
  87.0 0.6 fusion.33
  87.6 0.6 fusion.35
  88.2 0.6 fusion.37
  88.8 0.6 fusion.39
  89.4 0.6 fusion.41
  90.0 0.6 fusion.43
  90.6 1.7 %pad_maximum_fusion = bf16[12,96,8,132]{1,3,2,0:T(8,128)(2,1)S(1)} fusion(bf16[12,96,8,2]{1,3,2,0:T(2,128)(2,1)S(1)} %collective-permute-done.5, bf16[12,96,2,128]{1,3,2,0:T(8,128)(2,1)S(1)} %copy.102, bf16[12,96,4,128]{1,3,2,0:T(8,128)(2,1)S(1)} %constant_dynamic-update-slice_fusion, bf16[12,96,2,128]{1,3,2,0:T(8,128)(2,1)S(1)} %copy.101, ...), kind=kLoop, calls=%fused_computation | loop fusion | flops 12165120 | bytes 4866048 | tf_op jit(solution)/shard_map/concatenate | solution.py:24
  92.3 1.2 fusion
  93.5 1.1 fusion.7
  94.9 0.8 fusion.11
  95.9 0.5 fusion.56
  96.4 0.5 convolution_add_fusion.8
  96.9 0.5 convolution_add_fusion.7
  97.5 0.5 convolution_add_fusion.6
  98.0 0.5 convolution_add_fusion.5
  98.5 0.5 convolution_add_fusion.4
  99.0 0.5 convolution_add_fusion.3
  99.5 0.5 convolution_add_fusion.2
  100.2 0.8 multiply_reduce_fusion.1
  101.0 1.3 %multiply_reduce_fusion = (f32[2,6,130]{2,1,0:T(8,128)S(1)}, f32[2,96,6,130]{1,3,2,0:T(8,128)S(1)}) fusion(f32[2,96,6,130]{1,3,2,0:T(8,128)S(1)} %get-tuple-element.21, f32[96]{0:T(128)S(1)} %copy-done.8, f32[2,6,130]{2,1,0:T(8,128)S(1)} %get-tuple-element.17, f32[2,6,130,96]{3,2,1,0:T(8,128)S(1)} %fusion.29, f32[2,6,130,96]{3,2,1,0:T(8,128)S(1)} %fusion.31, ...), kind=kOutput, calls=%fused_computation.110 | convolution fusion | flops 89405160 | bytes 9470048 | tf_op jit(solution)/shard_map/ok,fkhw->fohw/dot_general | solution.py:64
  102.3 1.0 fusion.114
  103.4 2.5 %collective-permute-start.7 = (bf16[2,96,6,130]{1,3,2,0:T(8,128)(2,1)S(1)}, bf16[2,96,6,130]{1,3,2,0:T(8,128)(2,1)S(1)}, u32[]{:S(2)}, u32[]{:S(2)}) collective-permute-start(bf16[2,96,6,130]{1,3,2,0:T(8,128)(2,1)S(1)} %get-tuple-element.14), channel_id=1, source_target_pairs={{1,0},{3,2},{5,4},{7,6},{9,8},{11,10},{13,12},{15,14},{17,16},{19,... | collective-permute-start | bytes 898568 | tf_op jit(solution)/shard_map/ppermute | solution.py:12
  106.0 1.6 %collective-permute-start.6 = (bf16[2,96,6,130]{1,3,2,0:T(8,128)(2,1)S(1)}, bf16[2,96,6,130]{1,3,2,0:T(8,128)(2,1)S(1)}, u32[]{:S(2)}, u32[]{:S(2)}) collective-permute-start(bf16[2,96,6,130]{1,3,2,0:T(8,128)(2,1)S(1)} %get-tuple-element.15), channel_id=1, source_target_pairs={{0,1},{2,3},{4,5},{6,7},{8,9},{10,11},{12,13},{14,15},{16,17},{18,... | collective-permute-start | bytes 898568 | tf_op jit(solution)/shard_map/ppermute | solution.py:12
  107.6 0.6 fusion.28
  108.6 0.4 fusion.82
  109.3 0.4 fusion.86
  109.7 0.4 fusion.88
  110.9 0.4 fusion.94
  111.5 0.6 fusion.47
  112.1 0.5 copy-done.4
  113.0 0.4 fusion.103
  113.4 0.4 fusion.105
  114.1 0.4 fusion.109
  114.5 0.4 fusion.111
  114.9 0.4 fusion.97
  115.7 0.7 fusion.127
  116.7 1.0 copy.145
  117.7 0.5 fusion.79
  118.2 0.8 copy.144
  (56 shorter events, 4.5 us)
Async XLA Ops:
  1.7 48.1 %collective-permute-start = (bf16[2,96,4,128]{1,3,2,0:T(8,128)(2,1)S(1)}, bf16[2,96,4,128]{1,3,2,0:T(8,128)(2,1)S(1)}, u32[]{:S(2)}, u32[]{:S(2)}) collective-permute-start(bf16[2,96,4,128]{1,3,2,0:T(8,128)(2,1)S(1)} %copy.93), channel_id=1, source_target_pairs={{0,1},{2,3},{4,5},{6,7},{8,9},{10,11},{12,13},{14,15},{16,17},{18,... | collective-permute-start | bytes 589832 | tf_op jit(solution)/shard_map/ppermute | solution.py:12
  4.2 45.8 %collective-permute-start.1 = (bf16[2,96,4,128]{1,3,2,0:T(8,128)(2,1)S(1)}, bf16[2,96,4,128]{1,3,2,0:T(8,128)(2,1)S(1)}, u32[]{:S(2)}, u32[]{:S(2)}) collective-permute-start(bf16[2,96,4,128]{1,3,2,0:T(8,128)(2,1)S(1)} %copy.98), channel_id=1, source_target_pairs={{1,0},{3,2},{5,4},{7,6},{9,8},{11,10},{13,12},{15,14},{17,16},{19,... | collective-permute-start | bytes 589832 | tf_op jit(solution)/shard_map/ppermute | solution.py:12
  51.3 6.1 %copy-start.2 = (bf16[3,3,96,288]{3,2,1,0:T(8,128)(2,1)S(1)}, bf16[3,3,96,288]{3,2,1,0:T(8,128)(2,1)}, u32[]{:S(2)}) copy-start(bf16[3,3,96,288]{3,2,1,0:T(8,128)(2,1)} %param.15) | copy-start | bytes 1492996
  51.3 14.4 %collective-permute-start.2 = (bf16[12,96,2,128]{3,1,2,0:T(8,128)(2,1)}, bf16[12,96,2,128]{3,1,2,0:T(8,128)(2,1)}, u32[]{:S(2)}, u32[]{:S(2)}) collective-permute-start(bf16[12,96,2,128]{3,1,2,0:T(8,128)(2,1)} %copy.99), channel_id=1, source_target_pairs={{0,16},{16,32},{32,48},{48,64},{64,80},{80,96},{96,112},{112,128},... | collective-permute-start | bytes 1769480 | tf_op jit(solution)/shard_map/ppermute | solution.py:22
  54.6 17.2 %collective-permute-start.3 = (bf16[12,96,2,128]{3,1,2,0:T(8,128)(2,1)}, bf16[12,96,2,128]{3,1,2,0:T(8,128)(2,1)}, u32[]{:S(2)}, u32[]{:S(2)}) collective-permute-start(bf16[12,96,2,128]{3,1,2,0:T(8,128)(2,1)} %copy.100), channel_id=1, source_target_pairs={{16,0},{32,16},{48,32},{64,48},{80,64},{96,80},{112,96},{128,112},... | collective-permute-start | bytes 1769480 | tf_op jit(solution)/shard_map/ppermute | solution.py:23
  73.3 3.1 %copy-start.1 = (bf16[3,3,96,288]{2,3,1,0:T(8,128)(2,1)S(1)}, bf16[3,3,96,288]{2,3,1,0:T(8,128)(2,1)}, u32[]{:S(2)}) copy-start(bf16[3,3,96,288]{2,3,1,0:T(8,128)(2,1)} %copy.124) | copy-start | bytes 1492996
  73.4 8.2 %collective-permute-start.4 = (bf16[12,96,8,2]{1,3,2,0:T(2,128)(2,1)S(1)}, bf16[12,96,8,2]{1,3,2,0:T(2,128)(2,1)S(1)}, u32[]{:S(2)}, u32[]{:S(2)}) collective-permute-start(bf16[12,96,8,2]{1,3,2,0:T(2,128)(2,1)S(1)} %get-tuple-element.8), channel_id=1, source_target_pairs={{0,2},{2,4},{4,6},{6,8},{8,10},{10,12},{12,14},{1,3},{3,5},{5,7},{... | collective-permute-start | bytes 110600 | tf_op jit(solution)/shard_map/ppermute | solution.py:22
  74.8 6.8 %collective-permute-start.5 = (bf16[12,96,8,2]{1,3,2,0:T(2,128)(2,1)S(1)}, bf16[12,96,8,2]{1,3,2,0:T(2,128)(2,1)S(1)}, u32[]{:S(2)}, u32[]{:S(2)}) collective-permute-start(bf16[12,96,8,2]{1,3,2,0:T(2,128)(2,1)S(1)} %get-tuple-element.9), channel_id=1, source_target_pairs={{2,0},{4,2},{6,4},{8,6},{10,8},{12,10},{14,12},{3,1},{5,3},{7,5},{... | collective-permute-start | bytes 110600 | tf_op jit(solution)/shard_map/ppermute | solution.py:23
  81.6 4.2 %copy-start.6 = (bf16[3,3,96,3,96]{2,4,3,1,0:T(8,128)(2,1)S(1)}, bf16[3,3,96,3,96]{2,4,3,1,0:T(8,128)(2,1)}, u32[]{:S(2)}) copy-start(bf16[3,3,96,3,96]{2,4,3,1,0:T(8,128)(2,1)} %copy.114) | copy-start | bytes 1492996
  90.6 2.9 %copy-start.9 = (f32[96]{0:T(128)S(1)}, f32[96]{0:T(128)}, u32[]{:S(2)}) copy-start(f32[96]{0:T(128)} %param.13) | copy-start | bytes 1156
  94.8 1.1 copy-start.3
  99.5 0.7 copy-start.11
  100.2 0.9 copy-start.8
  102.3 3.6 %copy-start = (bf16[2,96,4,128]{3,2,1,0:T(4,128)(2,1)S(1)}, bf16[2,96,4,128]{3,2,1,0:T(4,128)(2,1)}, u32[]{:S(2)}) copy-start(bf16[2,96,4,128]{3,2,1,0:T(4,128)(2,1)} %param.10) | copy-start | bytes 589828
  103.4 4.8 %copy-start.5 = (bf16[3,3,96,3,96]{2,4,3,1,0:T(8,128)(2,1)S(1)}, bf16[3,3,96,3,96]{2,4,3,1,0:T(8,128)(2,1)}, u32[]{:S(2)}) copy-start(bf16[3,3,96,3,96]{2,4,3,1,0:T(8,128)(2,1)} %copy.125) | copy-start | bytes 1492996
  103.4 4.2 %collective-permute-start.7 = (bf16[2,96,6,130]{1,3,2,0:T(8,128)(2,1)S(1)}, bf16[2,96,6,130]{1,3,2,0:T(8,128)(2,1)S(1)}, u32[]{:S(2)}, u32[]{:S(2)}) collective-permute-start(bf16[2,96,6,130]{1,3,2,0:T(8,128)(2,1)S(1)} %get-tuple-element.14), channel_id=1, source_target_pairs={{1,0},{3,2},{5,4},{7,6},{9,8},{11,10},{13,12},{15,14},{17,16},{19,... | collective-permute-start | bytes 898568 | tf_op jit(solution)/shard_map/ppermute | solution.py:12
  106.0 5.3 %collective-permute-start.6 = (bf16[2,96,6,130]{1,3,2,0:T(8,128)(2,1)S(1)}, bf16[2,96,6,130]{1,3,2,0:T(8,128)(2,1)S(1)}, u32[]{:S(2)}, u32[]{:S(2)}) collective-permute-start(bf16[2,96,6,130]{1,3,2,0:T(8,128)(2,1)S(1)} %get-tuple-element.15), channel_id=1, source_target_pairs={{0,1},{2,3},{4,5},{6,7},{8,9},{10,11},{12,13},{14,15},{16,17},{18,... | collective-permute-start | bytes 898568 | tf_op jit(solution)/shard_map/ppermute | solution.py:12
  111.5 1.1 copy-start.4
  115.7 0.9 copy-start.7
  116.4 1.3 %copy-start.10 = (f32[96]{0:T(128)S(1)}, f32[96]{0:T(128)}, u32[]{:S(2)}) copy-start(f32[96]{0:T(128)} %param.18) | copy-start | bytes 1156
where the time goes:
time: 120 us; the launch traced here: 119 us
  starting transfers between devices  55.2 us (46%)
  local copies, waits for them, and re-layouts  21.4 us (18%)
  matrix products  18.2 us (15%)
  other arithmetic  12.1 us (10%)
  waiting for transfers between devices  10.9 us (9%)
    ppermute x4, starting transfers between devices, passed_along(): lax.ppermute(value, axis, [(source, source + steps) for source in range(l...  48.8 us
    dot_general x36, matrix products, convolve(): jnp.einsum('ok,fkhw->fohw', weight[row_tap, col_tap], stacked[:, :, row_t...  18.2 us
    unnamed x37, local copies, waits for them, and re-layouts  10.1 us
    concatenate x4, other arithmetic, convolve(): jnp.concatenate([padded[time_tap:time_tap + count_frames] for time_tap in...  6.25 us
    ppermute x2, waiting for transfers between devices, extended_2(): before = lax.ppermute(last, axis, up)  6.17 us
    transpose x4, local copies, waits for them, and re-layouts, flipped(): jnp.transpose(five, (0, 1, 4, 3, 2)).reshape(3, 3, channels, 3 * channels)  6.16 us
    ppermute x2, waiting for transfers between devices, extended_2(): after = lax.ppermute(leading, axis, down)  4.68 us
    ppermute x2, starting transfers between devices, extended_2(): before = lax.ppermute(last, axis, up)  3.69 us
  transfers between devices with their start and end apart: 8, of which 2 were waited for; matrix products, arithmetic and copies ran while one was open for 16% of the time, Pallas kernels for 0%

commit v1 on v0

v1 whole, which is shorter than its diff:
```python
import jax
import jax.numpy as jnp
from jax import lax
from jax.experimental import pallas as pl
from jax.experimental.pallas import tpu as pltpu
from jax.sharding import PartitionSpec as P

epsilon = 1e-06
f32 = jnp.float32
bf16 = jnp.bfloat16


def lanes_of(shape):
    return lax.broadcasted_iota(jnp.int32, shape, len(shape) - 1)


def act(v, g):
    r = lax.rsqrt(jnp.mean(v * v, axis=0, keepdims=True) + epsilon)
    z = v * r * g
    return z * jax.nn.sigmoid(z)


def act_and_back(v, g, d):
    r = lax.rsqrt(jnp.mean(v * v, axis=0, keepdims=True) + epsilon)
    vr = v * r
    z = vr * g
    s = jax.nn.sigmoid(z)
    q = g * d * s * (1.0 + z * (1.0 - s))
    back = r * q - vr * (r * r) * jnp.mean(q * v, axis=0, keepdims=True)
    return z * s, back


def pack_body(fr, ct, ci, cm, m1, m2, oc, sw, ed, scr):
    channels = m1.shape[1]
    rows = 4
    flat = channels * rows
    ta = lax.axis_index("ta")
    sources = [
        fr[0:flat, :], fr[flat:, :], ct[0:flat, :], ct[flat:, :],
        ci[pl.ds(ta * flat, flat), :], cm[pl.ds(ta * flat, flat), :],
        ci[pl.ds((1 - ta) * flat, flat), :], cm[pl.ds((1 - ta) * flat, flat), :],
    ]
    for s, source in enumerate(sources):
        scr[s] = source.astype(f32)
    k = lax.broadcasted_iota(jnp.int32, (rows * 128, 128), 0)
    j = lanes_of((rows * 128, 128))
    column = jnp.where(j % 4 == 0, 1, jnp.where(j % 4 == 1, 0, jnp.where(j % 4 == 2, 127, 126)))
    chosen = (j < 4 * rows) & (k // 128 == j // 4) & (k % 128 == column)
    chosen = jnp.where(chosen, 1.0, 0.0).astype(bf16)
    edges = jnp.zeros((channels, 128), f32)
    for s in range(6):
        tiles = [scr[s, pl.ds(r, channels, stride=rows), :].astype(bf16) for r in range(rows)]
        part = jnp.dot(jnp.concatenate(tiles, axis=1), chosen, preferred_element_type=f32)
        edges = edges + (pltpu.roll(part, 4 * rows * s, 1) if s else part)

        @pl.when(ta == 0)
        def _():
            for i in range(2):
                m1[2 * s + i] = tiles[2 + i]
                m2[2 * s + i] = tiles[i]
                if s < 4:
                    sw[2 * s + i] = tiles[2 + i]
                    sw[8 + 2 * s + i] = tiles[i]

        @pl.when(ta == 1)
        def _():
            for i in range(2):
                m1[2 * s + i] = tiles[i]
                m2[2 * s + i] = tiles[2 + i]
                if s < 4:
                    sw[2 * s + i] = tiles[i]
                    sw[8 + 2 * s + i] = tiles[2 + i]

    for s in range(2):
        for r in range(rows):
            oc[s, r] = scr[6 + s, pl.ds(r, channels, stride=rows), :].astype(bf16)
    ed[...] = edges.astype(bf16)


def main_body(
    m1, m2, oc, sp, z1, z2, w1, w2, w1f, w2f, vec, keep, send,
    A, C, M, D, HID, PA, PC, EA, EC,
):
    channels = m1.shape[1]
    tile = (channels, 128)
    ta = lax.axis_index("ta")
    ha = lax.axis_index("ha")
    wa = lax.axis_index("wa")
    first_row = (ta == 1) | (ha > 0)
    last_row = (ta == 0) | (ha < lax.axis_size("ha") - 1)
    left_col = wa > 0
    right_col = wa < lax.axis_size("wa") - 1
    other = 1 - ta
    zb = 4 * ta
    mb = 4 - 4 * ta
    lane = lanes_of(tile)
    column = lane % 4
    gin = jnp.broadcast_to(vec[:, 0:1], tile)
    gmid = jnp.broadcast_to(vec[:, 1:2], tile)
    bin_ = jnp.broadcast_to(vec[:, 2:3], tile)
    bmid = jnp.broadcast_to(vec[:, 3:4], tile)
    zero = jnp.zeros(tile, bf16)

    for i in range(2):
        for r in range(2):
            for src, at, frame, row in (
                (m2, 2 * i + r, 2 * ta + i, 2 + r),
                (m1, 2 * i + r, 2 * ta + i, mb + r),
                (z1, 2 * i + r, 2 * ta + i, zb + r),
                (sp, 2 * i + r, 2 * other + i, 2 + r),
                (sp, 8 + 2 * i + r, 2 * other + i, mb + r),
                (z2, 2 * i + r, 2 * other + i, zb + r),
            ):
                A[2 + frame, row] = act(src[at].astype(f32), gin).astype(bf16)
                C[frame, row] = src[at + 4]
    for r in range(2):
        A[ta, 2 + r] = m2[8 + r]
        A[ta, mb + r] = m1[8 + r]
        A[ta, zb + r] = z1[8 + r]
        A[other, zb + r] = z2[8 + r]
        M[ta, 1 + r] = m2[10 + r]
    M[ta, 3 - 3 * ta] = m1[10 + ta]
    M[ta, 3 * ta] = z1[11 - ta]
    M[other, 3 * ta] = z2[11 - ta]
    for r in range(4):
        A[other, r + 2 - 2 * ta] = oc[0, r]
    for k in range(3):
        M[other, k + 1 - ta] = oc[1, k + ta]
    for e in range(6):
        C[4, e] = zero
        C[5, e] = zero
    for e in range(4):
        D[4, e] = zero
        D[5, e] = zero

    own, par, zo, zp = (t[...].astype(f32) for t in (m2.at[12], sp.at[16], z1.at[12], z2.at[12]))

    def placed(t, slot, start, rows_from, rows, to):
        moved = pltpu.roll(t, (start + 4 * to - 16 * slot - 4 * rows_from) % 128, 1)
        low = start + 4 * to
        return jnp.where((lane >= low) & (lane < low + 4 * rows), moved, 0.0)

    def group(first, swapped):
        mine = yours = 0.0
        for i in range(2):
            mine += placed(own, first + i, 32 * i, 0, 4, 2 - 2 * ta)
            mine += placed(zo, first + i, 32 * i, 2 - 2 * ta, 2, 4 * ta)
            yours += placed(par, first + i, 32 * i, 0, 4, 2 - 2 * ta)
            yours += placed(zp, first + i, 32 * i, 2 - 2 * ta, 2, 4 * ta)
        g0 = jnp.where(ta == 0, mine, yours)
        g1 = jnp.where(ta == 0, yours, mine)
        return g0 + pltpu.roll(g1, 64, 1)

    def caches(slot):
        out = placed(own, slot, 32 * ta, 0, 4, 2 - 2 * ta)
        out += placed(zo, slot, 32 * ta, 2 - 2 * ta, 2, 4 * ta)
        out += placed(par, slot, 32 * other, 0, 4, 2 - 2 * ta)
        return out + placed(zp, slot, 32 * other, 2 - 2 * ta, 2, 4 * ta)

    def edge_products(w, low, high):
        pieces = []
        for t in range(3):
            for a in range(3):
                s = 32 * t + 4 * a
                if s == 0:
                    pieces.append(low.astype(bf16))
                    continue
                moved = pltpu.roll(low, 128 - s, 1)
                beyond = 0.0 if high is None else pltpu.roll(high, 128 - s, 1)
                pieces.append(jnp.where(lane < 128 - s, moved, beyond).astype(bf16))
        p = jnp.dot(w[...], jnp.concatenate(pieces, axis=0), preferred_element_type=f32)
        p0, p1, p2 = (p[b * channels : (b + 1) * channels] for b in range(3))
        across = jnp.where(column == 2, p0, p2)
        own_part = jnp.where(column == 2, pltpu.roll(p0, 127, 1), pltpu.roll(p2, 1, 1)) + p1
        return across, own_part

    act_edges = pltpu.roll(act(group(0, True), gin), 64, 1)
    cin_edges = caches(4)
    across, own_part = edge_products(
        w1, jnp.where(lane < 64, cin_edges, act_edges), jnp.where(lane < 64, act_edges, 0.0)
    )
    PA[...] = across
    EA[...] = own_part
    across, own_part = edge_products(w2f, group(2, True), None)
    PC[...] = across
    EC[...] = own_part
    cmid_edges = pltpu.roll(caches(5), 124, 1)

    def products(w, ref, f, row):
        cols = []
        for i in range(2):
            cols.append(
                jnp.concatenate(
                    [ref[f + t, row + i + a] for t in range(3) for a in range(3)], axis=0
                )
            )
        p = jnp.dot(w[...], jnp.concatenate(cols, axis=1), preferred_element_type=f32)
        return [
            [p[b * channels : (b + 1) * channels, 128 * i : 128 * (i + 1)] for b in range(3)]
            for i in range(2)
        ]

    def shifted_sum(p, edge_ref, q):
        back = pltpu.roll(edge_ref[...], lax.rem(256 - (q + 2), 128), 1)
        out = p[1] + jnp.where(lane == 0, back, pltpu.roll(p[0], 1, 1))
        return out + jnp.where(lane == 127, back, pltpu.roll(p[2], 127, 1))

    def to_edges(p, edge_ref, q):
        moved = pltpu.roll(jnp.where(lane == 0, p[2], p[0]), q + 2, 1)
        here = (lane == q + 1) | (lane == q + 2)
        edge_ref[...] = edge_ref[...] + jnp.where(here, moved, 0.0)

    def first_layer(f, carry):
        for pair in range(2):
            pf = products(w1, A, f, 2 * pair)
            pb = products(w2f, C, f, 2 * pair)
            for i in range(2):
                e = 2 * pair + i
                q = f * 32 + e * 4
                hidden = (shifted_sum(pf[i], PA, q) + bin_).astype(bf16).astype(f32)
                back = shifted_sum(pb[i], PC, q)
                to_edges(pf[i], EA, q)
                to_edges(pb[i], EC, q)
                a, d = act_and_back(hidden, gmid, back)
                if e == 0:
                    a = jnp.where(first_row, a, 0.0)
                    d = jnp.where(first_row, d, 0.0)
                if e == 3:
                    a = jnp.where(last_row, a, 0.0)
                    d = jnp.where(last_row, d, 0.0)
                M[2 + f, e] = a.astype(bf16)
                D[f, e] = d.astype(bf16)
        return carry

    lax.fori_loop(0, 4, first_layer, 0)

    hidden = (EA[...] + bin_).astype(bf16).astype(f32)
    a, d = act_and_back(hidden, gmid, EC[...])
    row = (lane % 32) // 4
    inside = ((column == 2) & left_col) | ((column == 1) & right_col)
    inside = inside & (row < 4) & ((row > 0) | first_row) & ((row < 3) | last_row)
    a = jnp.where(inside, a, 0.0).astype(bf16).astype(f32)
    d = jnp.where(inside, d, 0.0).astype(bf16).astype(f32)
    a = pltpu.roll(a, 64, 1)
    low = jnp.where(lane < 64, cmid_edges, a)
    across, _ = edge_products(w2, low, jnp.where(lane < 64, a, 0.0))
    PA[...] = across
    across, _ = edge_products(w1f, d, None)
    PC[...] = across

    def second_layer(f, mine, slot):
        pf = products(w2, M, f, 0)
        pb = products(w1f, D, f, 0)
        for i in range(2):
            q = f * 32 + i * 4
            frame = mine[2 * slot + i].astype(f32)
            cot = mine[4 + 2 * slot + i].astype(f32)
            decoded = frame + (shifted_sum(pf[i], PA, q) + bmid)
            _, back = act_and_back(frame, gin, shifted_sum(pb[i], PC, q))
            yield i, decoded.astype(bf16).astype(f32), cot + back

    def second(slot, carry):
        for i, decoded, grad in second_layer(2 * ta + slot, m2, slot):
            keep[0, slot, i] = decoded
            keep[1, slot, i] = grad
        for i, decoded, grad in second_layer(2 * other + slot, sp, slot):
            send[0, slot, i] = decoded
            send[1, slot, i] = grad
        return carry

    lax.fori_loop(0, 2, second, 0)


def assemble_body(keep, got, dec, grad, scr):
    channels = keep.shape[3]
    flat = 4 * channels
    ta = lax.axis_index("ta")

    def write(at_keep, at_got):
        for f in range(2):
            for i in range(2):
                for src, r in ((keep, at_keep + i), (got, at_got + i)):
                    scr[pl.ds(f * flat + r, channels, stride=4), :] = src[0, f, i]
                    grad[pl.ds(f * flat + r, channels, stride=4), :] = src[1, f, i]

    @pl.when(ta == 0)
    def _():
        write(0, 2)

    @pl.when(ta == 1)
    def _():
        write(2, 0)

    dec[...] = scr[...].astype(bf16)


def forward_weights(weight):
    c = weight.shape[2]
    five = weight.reshape(3, 3, c, 3, c)
    return jnp.transpose(five, (1, 2, 3, 0, 4)).reshape(3 * c, 9 * c)


def flipped_weights(weight):
    c = weight.shape[2]
    five = weight.reshape(3, 3, c, 3, c)[::-1, ::-1, :, ::-1, :]
    return jnp.transpose(five, (1, 4, 3, 0, 2)).reshape(3 * c, 9 * c)


def per_device(
    frames, cache_in, cache_mid, gain_in, gain_mid,
    weight_in, bias_in, weight_mid, bias_mid, cotangent,
):
    n, c, height, width = frames.shape
    flat = lambda v: v.reshape(n * c * height, width)
    tile = (c, width)
    m1, m2, oc, sw, ed = pl.pallas_call(
        pack_body,
        out_shape=(
            jax.ShapeDtypeStruct((13,) + tile, bf16),
            jax.ShapeDtypeStruct((13,) + tile, bf16),
            jax.ShapeDtypeStruct((2, 4) + tile, bf16),
            jax.ShapeDtypeStruct((17,) + tile, bf16),
            jax.ShapeDtypeStruct(tile, bf16),
        ),
        scratch_shapes=[pltpu.VMEM((8, c * height, width), f32)],
        name="pack",
    )(flat(frames), flat(cotangent), flat(cache_in), flat(cache_mid))

    wide = lax.axis_size("wa")
    high = lax.axis_size("ha")
    from_left = lax.ppermute(ed, "wa", [(i, i + 1) for i in range(wide - 1)])
    from_right = lax.ppermute(ed, "wa", [(i + 1, i) for i in range(wide - 1)])
    edge = jnp.where(lanes_of(tile) % 4 >= 2, from_left, from_right)
    m1 = m1.at[12].set(edge)
    m2 = m2.at[12].set(edge)
    sw = sw.at[16].set(edge)
    one = [(2 * i, 2 * i + 2) for i in range(high - 1)]
    one += [(2 * i + 3, 2 * i + 1) for i in range(high - 1)]
    two = [(2 * i + 2, 2 * i + 1) for i in range(high - 1)]
    two += [(2 * i + 1, 2 * i + 2) for i in range(high - 1)]
    z1 = lax.ppermute(m1, ("ha", "ta"), one)
    z2 = lax.ppermute(m2, ("ha", "ta"), two)
    sp = lax.ppermute(sw, "ta", [(0, 1), (1, 0)])

    w1, w2 = forward_weights(weight_in), forward_weights(weight_mid)
    w1f, w2f = flipped_weights(weight_in), flipped_weights(weight_mid)
    vec = jnp.stack([gain_in, gain_mid, bias_in, bias_mid], axis=1)
    half = jax.ShapeDtypeStruct((2, 2, 2) + tile, f32)
    keep, send = pl.pallas_call(
        main_body,
        out_shape=(half, half),
        scratch_shapes=[
            pltpu.VMEM((6, 6) + tile, bf16),
            pltpu.VMEM((6, 6) + tile, bf16),
            pltpu.VMEM((6, 4) + tile, bf16),
            pltpu.VMEM((6, 4) + tile, bf16),
            pltpu.VMEM((4, 4) + tile, bf16),
            pltpu.VMEM(tile, f32),
            pltpu.VMEM(tile, f32),
            pltpu.VMEM(tile, f32),
            pltpu.VMEM(tile, f32),
        ],
        name="block",
    )(m1, m2, oc, sp, z1, z2, w1, w2, w1f, w2f, vec)

    got = lax.ppermute(send, "ta", [(0, 1), (1, 0)])
    decoded, grad = pl.pallas_call(
        assemble_body,
        out_shape=(
            jax.ShapeDtypeStruct((n * c * height, width), bf16),
            jax.ShapeDtypeStruct((n * c * height, width), f32),
        ),
        scratch_shapes=[pltpu.VMEM((n * c * height, width), f32)],
        name="assemble",
    )(keep, got)
    return decoded.reshape(frames.shape), grad.reshape(frames.shape)


def solution(mesh):
    split = P(("grp", "ta"), None, "ha", "wa")
    cache = P("grp", None, "ha", "wa")
    return jax.shard_map(
        per_device,
        mesh=mesh,
        in_specs=(split, cache, cache, P(), P(), P(), P(), P(), P(), split),
        out_specs=(split, split),
        check_vma=False,
    )
```

time: 120 us -> 91.2 us (0.76)
  matrix products: 18.2 us -> 0 us
  Pallas kernels: 0 us -> 16.3 us
  other arithmetic: 12.1 us -> 0.63 us
  local copies, waits for them, and re-layouts: 21.4 us -> 12.7 us
  waiting for transfers between devices: 10.9 us -> 2.65 us
  starting transfers between devices: 55.2 us -> 57.7 us
    dot_general x36 -> x0, matrix products: 18.2 us -> none  [convolve(): jnp.einsum('ok,fkhw->fohw', weight[row_tap, col_tap], stacked[:, :, row_t...]
    pallas_call x0 -> x3, Pallas kernels: none -> 16.3 us  [the longest x1 10.6 us: per_device(): pl.pallas_call(main_body, out_shape=(half, half), scratch_shapes=[pltpu.V...]
    ppermute x8 -> x6, waiting for transfers between devices: 10.9 us -> 2.65 us  [the longest x1 1.54 us: per_device(): got = lax.ppermute(send, 'ta', [(0, 1), (1, 0)])]
    concatenate x5 -> x0, other arithmetic: 7.94 us -> none  [the longest x4 6.25 us: convolve(): jnp.concatenate([padded[time_tap:time_tap + count_frames] for time_tap in...]
    unnamed x37 -> x22, local copies, waits for them, and re-layouts: 10.1 us -> 3.81 us
    reshape x0 -> x4, local copies, waits for them, and re-layouts: none -> 5.19 us  [the longest x2 2.6 us: flipped_weights(): return jnp.transpose(five, (1, 4, 3, 0, 2)).reshape(3 * c, 9 * c)]
    transpose x4 -> x6, local copies, waits for them, and re-layouts: 6.16 us -> 2.31 us  [the longest x2 1.3 us: forward_weights(): return jnp.transpose(five, (1, 2, 3, 0, 4)).reshape(3 * c, 9 * c)]
    ppermute x2 -> x0, local copies, waits for them, and re-layouts: 2.88 us -> none  [the longest x1 1.44 us: extended_2(): after = lax.ppermute(leading, axis, down)]
  transfers between devices with their start and end apart: 8 -> 6, of which waited for: 2 -> 2; matrix products, arithmetic and copies ran while one was open for 16% -> 11% of each run, Pallas kernels for 0% -> 0%
where the time goes in v1:
time: 91.2 us; the launch traced here: 90.8 us
  starting transfers between devices  57.7 us (63%)
  Pallas kernels  16.3 us (18%)
  local copies, waits for them, and re-layouts  12.7 us (14%)
  waiting for transfers between devices  2.65 us (3%)
    ppermute x1, starting transfers between devices, per_device(): sp = lax.ppermute(sw, 'ta', [(0, 1), (1, 0)])  43.7 us
    pallas_call x1, Pallas kernels, per_device(): pl.pallas_call(main_body, out_shape=(half, half), scratch_shapes=[pltpu.V...  10.6 us
    ppermute x1, starting transfers between devices, per_device(): from_left = lax.ppermute(ed, 'wa', [(i, i + 1) for i in range(wide - 1)])  4.74 us
    ppermute x1, starting transfers between devices, per_device(): got = lax.ppermute(send, 'ta', [(0, 1), (1, 0)])  4.7 us
    unnamed x22, local copies, waits for them, and re-layouts  3.81 us
    pallas_call x1, Pallas kernels, per_device(): pl.pallas_call(pack_body, out_shape=(jax.ShapeDtypeStruct((13,) + tile, b...  3.74 us
    reshape x2, local copies, waits for them, and re-layouts, flipped_weights(): return jnp.transpose(five, (1, 4, 3, 0, 2)).reshape(3 * c, 9 * c)  2.6 us
    reshape x2, local copies, waits for them, and re-layouts, forward_weights(): return jnp.transpose(five, (1, 2, 3, 0, 4)).reshape(3 * c, 9 * c)  2.59 us
  transfers between devices with their start and end apart: 6, of which 2 were waited for; matrix products, arithmetic and copies ran while one was open for 11% of the time, Pallas kernels for 0%

profile of v1, /device:TPU:65, one launch (start us, length us, event | category | flops | bytes accessed | tf_op | source)
XLA Modules:
  0.0 90.8 jit_solution(14644572372558224306)
XLA Ops:
  0.6 0.0 copy-start
  0.6 3.7 %pack.1 = (bf16[13,96,128]{2,1,0:T(8,128)(2,1)}, bf16[13,96,128]{2,1,0:T(8,128)(2,1)}, bf16[2,4,96,128]{3,2,1,0:T(8,128)(2,1)}, bf16[17,96,128]{2,1,0:T(8,128)(2,1)}, bf16[96,128]{1,0:T(8,128)(2,1)}) custom-call(bf16[768,128]{1,0:T(8,128)(2,1)} %bitcast.27, bf16[768,128]{1,0:T(8,128)(2,1)} %bitcast.28, bf16[768,128]{1,0:T(8,128)(2,1)} %bitcast.29, ...), custom_call_target="tpu_custom_call" | custom-call | tf_op jit(solution)/shard_map/pack/pallas_call | solution.py:316
  4.4 1.3 %collective-permute-start.1 = (bf16[96,128]{1,0:T(8,128)(2,1)}, bf16[96,128]{1,0:T(8,128)(2,1)S(1)}, u32[]{:S(2)}, u32[]{:S(2)}) collective-permute-start(bf16[96,128]{1,0:T(8,128)(2,1)} %get-tuple-element.48), channel_id=1, source_target_pairs={{2,0},{4,2},{6,4},{8,6},{10,8},{12,10},{14,12},{3,1},{5,3},{7,5},{... | collective-permute-start | bytes 73736 | tf_op jit(solution)/shard_map/ppermute | solution.py:332
  5.7 4.7 %collective-permute-start = (bf16[96,128]{1,0:T(8,128)(2,1)}, bf16[96,128]{1,0:T(8,128)(2,1)S(1)}, u32[]{:S(2)}, u32[]{:S(2)}) collective-permute-start(bf16[96,128]{1,0:T(8,128)(2,1)} %get-tuple-element.48), channel_id=1, source_target_pairs={{0,2},{2,4},{4,6},{6,8},{8,10},{10,12},{12,14},{1,3},{3,5},{5,7},{... | collective-permute-start | bytes 73736 | tf_op jit(solution)/shard_map/ppermute | solution.py:331
  10.5 0.0 collective-permute-done.1
  10.5 1.1 %collective-permute-done = bf16[96,128]{1,0:T(8,128)(2,1)S(1)} collective-permute-done((bf16[96,128]{1,0:T(8,128)(2,1)}, bf16[96,128]{1,0:T(8,128)(2,1)S(1)}, u32[]{:S(2)}, u32[]{:S(2)}) %collective-permute-start) | collective-permute-done | bytes 24608 | tf_op jit(solution)/shard_map/ppermute | solution.py:331
  11.6 0.6 constant_dynamic-update-slice_fusion.2
  12.2 43.7 %collective-permute-start.2 = (bf16[17,96,128]{2,1,0:T(8,128)(2,1)}, bf16[17,96,128]{2,1,0:T(8,128)(2,1)S(1)}, u32[]{:S(2)}, u32[]{:S(2)}) collective-permute-start(bf16[17,96,128]{2,1,0:T(8,128)(2,1)} %get-tuple-element.56), channel_id=1, source_target_pairs={{0,1},{1,0},{2,3},{3,2},{4,5},{5,4},{6,7},{7,6},{8,9},{9,8},{10,11... | collective-permute-start | bytes 1253384 | tf_op jit(solution)/shard_map/ppermute | solution.py:343
  55.9 0.0 copy-start.9
  55.9 0.6 constant_dynamic-update-slice_fusion
  56.6 1.9 %collective-permute-start.4 = (bf16[13,96,128]{2,1,0:T(8,128)(2,1)}, bf16[13,96,128]{2,1,0:T(8,128)(2,1)S(1)}, u32[]{:S(2)}, u32[]{:S(2)}) collective-permute-start(bf16[13,96,128]{2,1,0:T(8,128)(2,1)} %get-tuple-element.58.m2), channel_id=1, source_target_pairs={{16,1},{32,17},{48,33},{64,49},{80,65},{96,81},{112,97},{128,113},... | collective-permute-start | bytes 958472 | tf_op jit(solution)/shard_map/ppermute | solution.py:342
  58.5 1.3 %collective-permute-start.3 = (bf16[13,96,128]{2,1,0:T(8,128)(2,1)}, bf16[13,96,128]{2,1,0:T(8,128)(2,1)S(1)}, u32[]{:S(2)}, u32[]{:S(2)}) collective-permute-start(bf16[13,96,128]{2,1,0:T(8,128)(2,1)} %get-tuple-element.59.m1), channel_id=1, source_target_pairs={{0,16},{16,32},{32,48},{48,64},{64,80},{80,96},{96,112},{112,128},... | collective-permute-start | bytes 958472 | tf_op jit(solution)/shard_map/ppermute | solution.py:341
  59.8 0.0 copy-start.6
  59.8 0.0 copy-start.7
  59.9 0.0 copy-start.8
  59.9 0.0 copy-done.9
  59.9 0.6 copy-done.6
  60.5 0.0 copy-done.7
  60.5 0.0 copy-done.8
  60.5 0.7 copy.36.vec
  61.3 0.0 copy-done
  61.3 0.0 copy-start.1
  61.3 0.4 copy.30
  61.6 0.7 copy-done.1
  62.3 0.4 copy.32
  62.8 0.5 copy.35
  63.2 1.3 %reshape.132.w2f = bf16[288,864]{1,0:T(8,128)(2,1)} reshape(bf16[3,96,3,3,96]{4,3,2,1,0:T(4,128)(2,1)S(1)} %copy.35) | data formatting | bytes 995328 | tf_op jit(solution)/shard_map/reshape | solution.py:306
  64.6 0.5 copy.34
  65.0 1.3 %reshape.131.w1f = bf16[288,864]{1,0:T(8,128)(2,1)} reshape(bf16[3,96,3,3,96]{4,3,2,1,0:T(4,128)(2,1)S(1)} %copy.34) | data formatting | bytes 995328 | tf_op jit(solution)/shard_map/reshape | solution.py:306
  66.3 0.7 copy.33
  67.0 1.3 %reshape.130.w2 = bf16[288,864]{1,0:T(8,128)(2,1)} reshape(bf16[3,96,3,3,96]{4,3,2,1,0:T(4,128)(2,1)S(1)} %copy.33) | data formatting | bytes 995328 | tf_op jit(solution)/shard_map/reshape | solution.py:300
  68.3 0.7 copy.31
  69.0 1.3 %reshape.128.w1 = bf16[288,864]{1,0:T(8,128)(2,1)} reshape(bf16[3,96,3,3,96]{4,3,2,1,0:T(4,128)(2,1)S(1)} %copy.31) | data formatting | bytes 995328 | tf_op jit(solution)/shard_map/reshape | solution.py:300
  70.3 0.0 collective-permute-done.4.z2
  70.3 0.0 copy-start.4
  70.3 0.0 collective-permute-done.3.z1
  70.3 0.0 copy-start.5
  70.3 0.0 collective-permute-done.2.sp
  70.3 0.0 copy-start.2
  70.3 0.7 copy-done.4
  71.0 0.1 copy-done.5
  71.1 0.1 copy-done.2
  71.2 10.6 %block.1 = (f32[2,2,2,96,128]{4,3,2,1,0:T(8,128)}, f32[2,2,2,96,128]{4,3,2,1,0:T(8,128)}) custom-call(bf16[13,96,128]{2,1,0:T(8,128)(2,1)} %get-tuple-element.59.m1, bf16[13,96,128]{2,1,0:T(8,128)(2,1)} %get-tuple-element.58.m2, bf16[2,4,96,128]{3,2,1,0:T(8,128)(2,1)} %get-tuple-element.50.oc, bf16[17,96,128]{2,1,0:T(8,128)(2,1)} %copy-done.2, ...), custom_call_target="tpu_custom_call" | custom-call | tf_op jit(solution)/shard_map/block/pallas_call | solution.py:349
  81.8 4.7 %collective-permute-start.5 = (f32[2,2,2,96,128]{4,3,2,1,0:T(8,128)}, f32[2,2,2,96,128]{4,3,2,1,0:T(8,128)S(1)}, u32[]{:S(2)}, u32[]{:S(2)}) collective-permute-start(f32[2,2,2,96,128]{4,3,2,1,0:T(8,128)} %get-tuple-element.53), channel_id=1, source_target_pairs={{0,1},{1,0},{2,3},{3,2},{4,5},{5,4},{6,7},{7,6},{8,9},{9,8},{10,11... | collective-permute-start | bytes 1179656 | tf_op jit(solution)/shard_map/ppermute | solution.py:366
  86.5 1.5 %collective-permute-done.5.got = f32[2,2,2,96,128]{4,3,2,1,0:T(8,128)S(1)} collective-permute-done((f32[2,2,2,96,128]{4,3,2,1,0:T(8,128)}, f32[2,2,2,96,128]{4,3,2,1,0:T(8,128)S(1)}, u32[]{:S(2)}, u32[]{:S(2)}) %collective-permute-start.5) | collective-permute-done | bytes 393248 | tf_op jit(solution)/shard_map/ppermute | solution.py:366
  88.0 0.0 copy-start.3
  88.0 0.7 copy-done.3
  88.8 2.0 %assemble.1 = (bf16[768,128]{1,0:T(8,128)(2,1)}, f32[768,128]{1,0:T(8,128)}) custom-call(f32[2,2,2,96,128]{4,3,2,1,0:T(8,128)} %get-tuple-element.52.keep, f32[2,2,2,96,128]{4,3,2,1,0:T(8,128)} %copy-done.3), custom_call_target="tpu_custom_call" | custom-call | tf_op jit(solution)/shard_map/assemble/pallas_call | solution.py:367
  (5 shorter events, 0.1 us)
Async XLA Ops:
  0.6 60.6 %copy-start = (bf16[3,3,96,288]{3,2,1,0:T(8,128)(2,1)S(1)}, bf16[3,3,96,288]{3,2,1,0:T(8,128)(2,1)}, u32[]{:S(2)}) copy-start(bf16[3,3,96,288]{3,2,1,0:T(8,128)(2,1)} %param.21) | copy-start | bytes 1492996
  4.4 6.1 %collective-permute-start.1 = (bf16[96,128]{1,0:T(8,128)(2,1)}, bf16[96,128]{1,0:T(8,128)(2,1)S(1)}, u32[]{:S(2)}, u32[]{:S(2)}) collective-permute-start(bf16[96,128]{1,0:T(8,128)(2,1)} %get-tuple-element.48), channel_id=1, source_target_pairs={{2,0},{4,2},{6,4},{8,6},{10,8},{12,10},{14,12},{3,1},{5,3},{7,5},{... | collective-permute-start | bytes 73736 | tf_op jit(solution)/shard_map/ppermute | solution.py:332
  5.7 5.9 %collective-permute-start = (bf16[96,128]{1,0:T(8,128)(2,1)}, bf16[96,128]{1,0:T(8,128)(2,1)S(1)}, u32[]{:S(2)}, u32[]{:S(2)}) collective-permute-start(bf16[96,128]{1,0:T(8,128)(2,1)} %get-tuple-element.48), channel_id=1, source_target_pairs={{0,2},{2,4},{4,6},{6,8},{8,10},{10,12},{12,14},{1,3},{3,5},{5,7},{... | collective-permute-start | bytes 73736 | tf_op jit(solution)/shard_map/ppermute | solution.py:331
  12.2 58.1 %collective-permute-start.2 = (bf16[17,96,128]{2,1,0:T(8,128)(2,1)}, bf16[17,96,128]{2,1,0:T(8,128)(2,1)S(1)}, u32[]{:S(2)}, u32[]{:S(2)}) collective-permute-start(bf16[17,96,128]{2,1,0:T(8,128)(2,1)} %get-tuple-element.56), channel_id=1, source_target_pairs={{0,1},{1,0},{2,3},{3,2},{4,5},{5,4},{6,7},{7,6},{8,9},{9,8},{10,11... | collective-permute-start | bytes 1253384 | tf_op jit(solution)/shard_map/ppermute | solution.py:343
  55.9 3.9 %copy-start.9 = (f32[96]{0:T(128)S(1)}, f32[96]{0:T(128)}, u32[]{:S(2)}) copy-start(f32[96]{0:T(128)} %param.19) | copy-start | bytes 1156
  56.6 13.7 %collective-permute-start.4 = (bf16[13,96,128]{2,1,0:T(8,128)(2,1)}, bf16[13,96,128]{2,1,0:T(8,128)(2,1)S(1)}, u32[]{:S(2)}, u32[]{:S(2)}) collective-permute-start(bf16[13,96,128]{2,1,0:T(8,128)(2,1)} %get-tuple-element.58.m2), channel_id=1, source_target_pairs={{16,1},{32,17},{48,33},{64,49},{80,65},{96,81},{112,97},{128,113},... | collective-permute-start | bytes 958472 | tf_op jit(solution)/shard_map/ppermute | solution.py:342
  58.5 11.8 %collective-permute-start.3 = (bf16[13,96,128]{2,1,0:T(8,128)(2,1)}, bf16[13,96,128]{2,1,0:T(8,128)(2,1)S(1)}, u32[]{:S(2)}, u32[]{:S(2)}) collective-permute-start(bf16[13,96,128]{2,1,0:T(8,128)(2,1)} %get-tuple-element.59.m1), channel_id=1, source_target_pairs={{0,16},{16,32},{32,48},{48,64},{64,80},{80,96},{96,112},{112,128},... | collective-permute-start | bytes 958472 | tf_op jit(solution)/shard_map/ppermute | solution.py:341
  59.8 0.7 copy-start.6
  59.8 0.7 copy-start.7
  59.9 0.7 copy-start.8
  61.3 1.1 %copy-start.1 = (bf16[3,3,96,288]{3,2,1,0:T(8,128)(2,1)S(1)}, bf16[3,3,96,288]{3,2,1,0:T(8,128)(2,1)}, u32[]{:S(2)}) copy-start(bf16[3,3,96,288]{3,2,1,0:T(8,128)(2,1)} %param.23) | copy-start | bytes 1492996
  70.3 0.7 copy-start.4
  70.3 0.8 copy-start.5
  70.3 0.9 %copy-start.2 = (bf16[17,96,128]{2,1,0:T(8,128)(2,1)}, bf16[17,96,128]{2,1,0:T(8,128)(2,1)S(1)}, u32[]{:S(2)}) copy-start(bf16[17,96,128]{2,1,0:T(8,128)(2,1)S(1)} %collective-permute-done.2.sp) | copy-start | bytes 1253380
  81.8 6.2 %collective-permute-start.5 = (f32[2,2,2,96,128]{4,3,2,1,0:T(8,128)}, f32[2,2,2,96,128]{4,3,2,1,0:T(8,128)S(1)}, u32[]{:S(2)}, u32[]{:S(2)}) collective-permute-start(f32[2,2,2,96,128]{4,3,2,1,0:T(8,128)} %get-tuple-element.53), channel_id=1, source_target_pairs={{0,1},{1,0},{2,3},{3,2},{4,5},{5,4},{6,7},{7,6},{8,9},{9,8},{10,11... | collective-permute-start | bytes 1179656 | tf_op jit(solution)/shard_map/ppermute | solution.py:366
  88.0 0.8 copy-start.3

commit v2 on v1

--- a/solution.py
+++ b/solution.py
@@ -8,6 +8,16 @@
 epsilon = 1e-06
 f32 = jnp.float32
 bf16 = jnp.bfloat16
+VM = pl.BlockSpec(memory_space=pltpu.VMEM)
+HB = pl.BlockSpec(memory_space=pltpu.HBM)
+
+
+def near(*values):
+    return [pltpu.with_memory_space_constraint(v, pltpu.VMEM) for v in values]
+
+
+def far(*values):
+    return [pltpu.with_memory_space_constraint(v, pltpu.HBM) for v in values]
 
 
 def lanes_of(shape):
@@ -30,24 +40,29 @@
     return z * s, back
 
 
-def pack_body(fr, ct, ci, cm, m1, m2, oc, sw, ed, scr):
+def pack_body(fr_far, ct_far, ci_far, cm_far, m1, m2, oc, sw, ed, scr, inp, sems):
+    copies = [
+        pltpu.make_async_copy(source, inp.at[i], sems.at[i])
+        for i, source in enumerate((fr_far, ct_far, ci_far, cm_far))
+    ]
+    for copy in copies:
+        copy.start()
     channels = m1.shape[1]
     rows = 4
     flat = channels * rows
     ta = lax.axis_index("ta")
-    sources = [
-        fr[0:flat, :], fr[flat:, :], ct[0:flat, :], ct[flat:, :],
-        ci[pl.ds(ta * flat, flat), :], cm[pl.ds(ta * flat, flat), :],
-        ci[pl.ds((1 - ta) * flat, flat), :], cm[pl.ds((1 - ta) * flat, flat), :],
-    ]
-    for s, source in enumerate(sources):
-        scr[s] = source.astype(f32)
+    starts = [(0, 0), (0, flat), (1, 0), (1, flat), (2, ta * flat), (3, ta * flat)]
+    starts += [(2, (1 - ta) * flat), (3, (1 - ta) * flat)]
     k = lax.broadcasted_iota(jnp.int32, (rows * 128, 128), 0)
     j = lanes_of((rows * 128, 128))
     column = jnp.where(j % 4 == 0, 1, jnp.where(j % 4 == 1, 0, jnp.where(j % 4 == 2, 127, 126)))
     chosen = (j < 4 * rows) & (k // 128 == j // 4) & (k % 128 == column)
     chosen = jnp.where(chosen, 1.0, 0.0).astype(bf16)
     edges = jnp.zeros((channels, 128), f32)
+    for s, (array, start) in enumerate(starts):
+        if s in (0, 2, 4, 5):
+            copies[array].wait()
+        scr[s] = inp[array, pl.ds(start, flat), :].astype(f32)
     for s in range(6):
         tiles = [scr[s, pl.ds(r, channels, stride=rows), :].astype(bf16) for r in range(rows)]
         part = jnp.dot(jnp.concatenate(tiles, axis=1), chosen, preferred_element_type=f32)
@@ -77,9 +92,47 @@
     ed[...] = edges.astype(bf16)
 
 
+def merge_body(first, second, m1_in, m2_in, sw_in, m1, m2, sw):
+    even = lax.rem(lax.axis_index("wa"), 2) == 0
+    a, b = first[...].astype(f32), second[...].astype(f32)
+    inner = lanes_of(a.shape) % 4 >= 2
+    edge = jnp.where(inner == even, b, a).astype(bf16)
+    m1[12] = edge
+    m2[12] = edge
+    sw[16] = edge
+
+
+def weights_body(
+    far_in, far_mid, gi, gm, bi, bm, after, w1, w2, w1f, w2f, vec, win, wmid, sems
+):
+    copies = [
+        pltpu.make_async_copy(far_in, win, sems.at[0]),
+        pltpu.make_async_copy(far_mid, wmid, sems.at[1]),
+    ]
+    for copy in copies:
+        copy.start()
+    channels = w1.shape[0] // 3
+    for k, row in enumerate((gi, gm, bi, bm)):
+        vec[k] = jnp.transpose(jnp.broadcast_to(row[...], (128, channels)))
+    for copy, src, plain, turned in zip(copies, (win, wmid), (w1, w2), (w1f, w2f)):
+        copy.wait()
+        plain[...] = jnp.concatenate([src[a].astype(f32) for a in range(3)], axis=1).astype(bf16)
+        for b in range(3):
+            flat = [
+                jnp.transpose(src[2 - a, (2 - b) * channels : (3 - b) * channels, :].astype(f32))
+                for a in range(3)
+            ]
+            blocks = [
+                flat[a][(2 - t) * channels : (3 - t) * channels] for t in range(3) for a in range(3)
+            ]
+            turned[b * channels : (b + 1) * channels, :] = jnp.concatenate(blocks, axis=1).astype(
+                bf16
+            )
+
+
 def main_body(
     m1, m2, oc, sp, z1, z2, w1, w2, w1f, w2f, vec, keep, send,
-    A, C, M, D, HID, PA, PC, EA, EC,
+    A, C, M, D, PA, PC, EA, EC,
 ):
     channels = m1.shape[1]
     tile = (channels, 128)
@@ -95,11 +148,7 @@
     mb = 4 - 4 * ta
     lane = lanes_of(tile)
     column = lane % 4
-    gin = jnp.broadcast_to(vec[:, 0:1], tile)
-    gmid = jnp.broadcast_to(vec[:, 1:2], tile)
-    bin_ = jnp.broadcast_to(vec[:, 2:3], tile)
-    bmid = jnp.broadcast_to(vec[:, 3:4], tile)
-    zero = jnp.zeros(tile, bf16)
+    gin, gmid, bin_, bmid = (vec[k] for k in range(4))
 
     for i in range(2):
         for r in range(2):
@@ -126,12 +175,10 @@
         A[other, r + 2 - 2 * ta] = oc[0, r]
     for k in range(3):
         M[other, k + 1 - ta] = oc[1, k + ta]
-    for e in range(6):
-        C[4, e] = zero
-        C[5, e] = zero
+
     for e in range(4):
-        D[4, e] = zero
-        D[5, e] = zero
+        D[4, e] = jnp.zeros(tile, bf16)
+        D[5, e] = jnp.zeros(tile, bf16)
 
     own, par, zo, zp = (t[...].astype(f32) for t in (m2.at[12], sp.at[16], z1.at[12], z2.at[12]))
 
@@ -157,17 +204,19 @@
         out += placed(par, slot, 32 * other, 0, 4, 2 - 2 * ta)
         return out + placed(zp, slot, 32 * other, 2 - 2 * ta, 2, 4 * ta)
 
-    def edge_products(w, low, high):
+    time_first = [(t, a) for t in range(3) for a in range(3)]
+    row_first = [(t, a) for a in range(3) for t in range(3)]
+
+    def edge_products(w, low, high, order):
         pieces = []
-        for t in range(3):
-            for a in range(3):
-                s = 32 * t + 4 * a
-                if s == 0:
-                    pieces.append(low.astype(bf16))
-                    continue
-                moved = pltpu.roll(low, 128 - s, 1)
-                beyond = 0.0 if high is None else pltpu.roll(high, 128 - s, 1)
-                pieces.append(jnp.where(lane < 128 - s, moved, beyond).astype(bf16))
+        for t, a in order:
+            s = 32 * t + 4 * a
+            if s == 0:
+                pieces.append(low.astype(bf16))
+                continue
+            moved = pltpu.roll(low, 128 - s, 1)
+            beyond = 0.0 if high is None else pltpu.roll(high, 128 - s, 1)
+            pieces.append(jnp.where(lane < 128 - s, moved, beyond).astype(bf16))
         p = jnp.dot(w[...], jnp.concatenate(pieces, axis=0), preferred_element_type=f32)
         p0, p1, p2 = (p[b * channels : (b + 1) * channels] for b in range(3))
         across = jnp.where(column == 2, p0, p2)
@@ -177,31 +226,29 @@
     act_edges = pltpu.roll(act(group(0, True), gin), 64, 1)
     cin_edges = caches(4)
     across, own_part = edge_products(
-        w1, jnp.where(lane < 64, cin_edges, act_edges), jnp.where(lane < 64, act_edges, 0.0)
+        w1, jnp.where(lane < 64, cin_edges, act_edges), jnp.where(lane < 64, act_edges, 0.0),
+        row_first,
     )
     PA[...] = across
     EA[...] = own_part
-    across, own_part = edge_products(w2f, group(2, True), None)
+    across, own_part = edge_products(w2f, group(2, True), None, time_first)
     PC[...] = across
     EC[...] = own_part
     cmid_edges = pltpu.roll(caches(5), 124, 1)
 
-    def products(w, ref, f, row):
-        cols = []
-        for i in range(2):
-            cols.append(
-                jnp.concatenate(
-                    [ref[f + t, row + i + a] for t in range(3) for a in range(3)], axis=0
-                )
-            )
-        p = jnp.dot(w[...], jnp.concatenate(cols, axis=1), preferred_element_type=f32)
+    def products(w, ref, f, row, order):
+        cols = [
+            jnp.concatenate([ref[f + t, row + i + a] for t, a in order], axis=0) for i in range(2)
+        ]
+        weights = w[:, : len(order) * channels]
+        p = jnp.dot(weights, jnp.concatenate(cols, axis=1), preferred_element_type=f32)
         return [
             [p[b * channels : (b + 1) * channels, 128 * i : 128 * (i + 1)] for b in range(3)]
             for i in range(2)
         ]
 
     def shifted_sum(p, edge_ref, q):
-        back = pltpu.roll(edge_ref[...], lax.rem(256 - (q + 2), 128), 1)
+        back = pltpu.roll(edge_ref[...], lax.rem(256 - (q + 2), 128) if not isinstance(q, int) else (126 - q) % 128, 1)
         out = p[1] + jnp.where(lane == 0, back, pltpu.roll(p[0], 1, 1))
         return out + jnp.where(lane == 127, back, pltpu.roll(p[2], 127, 1))
 
@@ -210,10 +257,10 @@
         here = (lane == q + 1) | (lane == q + 2)
         edge_ref[...] = edge_ref[...] + jnp.where(here, moved, 0.0)
 
-    def first_layer(f, carry):
+    def first_layer(f):
         for pair in range(2):
-            pf = products(w1, A, f, 2 * pair)
-            pb = products(w2f, C, f, 2 * pair)
+            pf = products(w1, A, f, 2 * pair, row_first)
+            pb = products(w2f, C, f, 2 * pair, time_first[: 3 * (4 - f)])
             for i in range(2):
                 e = 2 * pair + i
                 q = f * 32 + e * 4
@@ -230,9 +277,9 @@
                     d = jnp.where(last_row, d, 0.0)
                 M[2 + f, e] = a.astype(bf16)
                 D[f, e] = d.astype(bf16)
-        return carry
-
-    lax.fori_loop(0, 4, first_layer, 0)
+
+    for f in range(4):
+        first_layer(f)
 
     hidden = (EA[...] + bin_).astype(bf16).astype(f32)
     a, d = act_and_back(hidden, gmid, EC[...])
@@ -243,36 +290,31 @@
     d = jnp.where(inside, d, 0.0).astype(bf16).astype(f32)
     a = pltpu.roll(a, 64, 1)
     low = jnp.where(lane < 64, cmid_edges, a)
-    across, _ = edge_products(w2, low, jnp.where(lane < 64, a, 0.0))
+    across, _ = edge_products(w2, low, jnp.where(lane < 64, a, 0.0), row_first)
     PA[...] = across
-    across, _ = edge_products(w1f, d, None)
+    across, _ = edge_products(w1f, d, None, time_first)
     PC[...] = across
 
-    def second_layer(f, mine, slot):
-        pf = products(w2, M, f, 0)
-        pb = products(w1f, D, f, 0)
+    def second_layer(f, mine, slot, out):
+        pf = products(w2, M, f, 0, row_first)
+        pb = products(w1f, D, f, 0, time_first)
         for i in range(2):
             q = f * 32 + i * 4
             frame = mine[2 * slot + i].astype(f32)
             cot = mine[4 + 2 * slot + i].astype(f32)
             decoded = frame + (shifted_sum(pf[i], PA, q) + bmid)
+            out[0, slot, i] = decoded.astype(bf16).astype(f32)
             _, back = act_and_back(frame, gin, shifted_sum(pb[i], PC, q))
-            yield i, decoded.astype(bf16).astype(f32), cot + back
-
-    def second(slot, carry):
-        for i, decoded, grad in second_layer(2 * ta + slot, m2, slot):
-            keep[0, slot, i] = decoded
-            keep[1, slot, i] = grad
-        for i, decoded, grad in second_layer(2 * other + slot, sp, slot):
-            send[0, slot, i] = decoded
-            send[1, slot, i] = grad
-        return carry
-
-    lax.fori_loop(0, 2, second, 0)
+            out[1, slot, i] = cot + back
+
+    for slot in range(2):
+        second_layer(2 * other + slot, sp, slot, send)
+    for slot in range(2):
+        second_layer(2 * ta + slot, m2, slot, keep)
 
 
 def assemble_body(keep, got, dec, grad, scr):
-    channels = keep.shape[3]
+    channels = got.shape[3]
     flat = 4 * channels
     ta = lax.axis_index("ta")
 
@@ -292,18 +334,6 @@
         write(2, 0)
 
     dec[...] = scr[...].astype(bf16)
-
-
-def forward_weights(weight):
-    c = weight.shape[2]
-    five = weight.reshape(3, 3, c, 3, c)
-    return jnp.transpose(five, (1, 2, 3, 0, 4)).reshape(3 * c, 9 * c)
-
-
-def flipped_weights(weight):
-    c = weight.shape[2]
-    five = weight.reshape(3, 3, c, 3, c)[::-1, ::-1, :, ::-1, :]
-    return jnp.transpose(five, (1, 4, 3, 0, 2)).reshape(3 * c, 9 * c)
 
 
 def per_device(
@@ -313,27 +343,47 @@
     n, c, height, width = frames.shape
     flat = lambda v: v.reshape(n * c * height, width)
     tile = (c, width)
+    limit = lambda mib: pltpu.CompilerParams(vmem_limit_bytes=mib << 20)
     m1, m2, oc, sw, ed = pl.pallas_call(
         pack_body,
+        in_specs=[HB] * 4,
+        out_specs=(VM,) * 5,
         out_shape=(
-            jax.ShapeDtypeStruct((13,) + tile, bf16),
-            jax.ShapeDtypeStruct((13,) + tile, bf16),
-            jax.ShapeDtypeStruct((2, 4) + tile, bf16),
-            jax.ShapeDtypeStruct((17,) + tile, bf16),
-            jax.ShapeDtypeStruct(tile, bf16),
+            pltpu.VMEM((13,) + tile, bf16),
+            pltpu.VMEM((13,) + tile, bf16),
+            pltpu.VMEM((2, 4) + tile, bf16),
+            pltpu.VMEM((17,) + tile, bf16),
+            pltpu.VMEM(tile, bf16),
         ),
-        scratch_shapes=[pltpu.VMEM((8, c * height, width), f32)],
+        scratch_shapes=[
+            pltpu.VMEM((8, c * height, width), f32),
+            pltpu.VMEM((4, n * c * height, width), bf16),
+            pltpu.SemaphoreType.DMA((4,)),
+        ],
+        compiler_params=limit(8),
         name="pack",
-    )(flat(frames), flat(cotangent), flat(cache_in), flat(cache_mid))
+    )(*far(flat(frames), flat(cotangent), flat(cache_in), flat(cache_mid)))
 
     wide = lax.axis_size("wa")
     high = lax.axis_size("ha")
-    from_left = lax.ppermute(ed, "wa", [(i, i + 1) for i in range(wide - 1)])
-    from_right = lax.ppermute(ed, "wa", [(i + 1, i) for i in range(wide - 1)])
-    edge = jnp.where(lanes_of(tile) % 4 >= 2, from_left, from_right)
-    m1 = m1.at[12].set(edge)
-    m2 = m2.at[12].set(edge)
-    sw = sw.at[16].set(edge)
+    pairs = lambda start: [
+        p for i in range(start, wide - 1, 2) for p in ((i, i + 1), (i + 1, i))
+    ]
+    first = lax.ppermute(ed, "wa", pairs(0))
+    second = lax.ppermute(ed, "wa", pairs(1))
+    m1, m2, sw = pl.pallas_call(
+        merge_body,
+        in_specs=[VM] * 5,
+        out_specs=(VM,) * 3,
+        out_shape=(
+            pltpu.VMEM((13,) + tile, bf16),
+            pltpu.VMEM((13,) + tile, bf16),
+            pltpu.VMEM((17,) + tile, bf16),
+        ),
+        input_output_aliases={2: 0, 3: 1, 4: 2},
+        compiler_params=limit(2),
+        name="merge",
+    )(*near(first, second, m1, m2, sw))
     one = [(2 * i, 2 * i + 2) for i in range(high - 1)]
     one += [(2 * i + 3, 2 * i + 1) for i in range(high - 1)]
     two = [(2 * i + 2, 2 * i + 1) for i in range(high - 1)]
@@ -342,37 +392,56 @@
     z2 = lax.ppermute(m2, ("ha", "ta"), two)
     sp = lax.ppermute(sw, "ta", [(0, 1), (1, 0)])
 
-    w1, w2 = forward_weights(weight_in), forward_weights(weight_mid)
-    w1f, w2f = flipped_weights(weight_in), flipped_weights(weight_mid)
-    vec = jnp.stack([gain_in, gain_mid, bias_in, bias_mid], axis=1)
-    half = jax.ShapeDtypeStruct((2, 2, 2) + tile, f32)
+    row = lambda v: v.reshape(1, c)
+    taps = lambda w: w.reshape(3, 3 * c, 3 * c)
+    matrix = pltpu.VMEM((3 * c, 9 * c), bf16)
+    w1, w2, w1f, w2f, vec = pl.pallas_call(
+        weights_body,
+        in_specs=[HB] * 2 + [VM] * 4 + [pl.BlockSpec(memory_space=pl.ANY)],
+        out_specs=(VM,) * 5,
+        out_shape=(matrix,) * 4 + (pltpu.VMEM((4,) + tile, f32),),
+        scratch_shapes=[
+            pltpu.VMEM((3, 3 * c, 3 * c), bf16),
+            pltpu.VMEM((3, 3 * c, 3 * c), bf16),
+            pltpu.SemaphoreType.DMA((2,)),
+        ],
+        compiler_params=limit(8),
+        name="weights",
+    )(
+        *far(taps(weight_in), taps(weight_mid)),
+        row(gain_in), row(gain_mid), row(bias_in), row(bias_mid), m2,
+    )
     keep, send = pl.pallas_call(
         main_body,
-        out_shape=(half, half),
+        in_specs=[VM] * 11,
+        out_specs=(VM,) * 2,
+        out_shape=(pltpu.VMEM((2, 2, 2) + tile, f32),) * 2,
         scratch_shapes=[
             pltpu.VMEM((6, 6) + tile, bf16),
-            pltpu.VMEM((6, 6) + tile, bf16),
+            pltpu.VMEM((4, 6) + tile, bf16),
             pltpu.VMEM((6, 4) + tile, bf16),
             pltpu.VMEM((6, 4) + tile, bf16),
-            pltpu.VMEM((4, 4) + tile, bf16),
             pltpu.VMEM(tile, f32),
             pltpu.VMEM(tile, f32),
             pltpu.VMEM(tile, f32),
             pltpu.VMEM(tile, f32),
         ],
+        compiler_params=limit(16),
         name="block",
-    )(m1, m2, oc, sp, z1, z2, w1, w2, w1f, w2f, vec)
+    )(*near(m1, m2, oc, sp, z1, z2, w1, w2, w1f, w2f, vec))
 
     got = lax.ppermute(send, "ta", [(0, 1), (1, 0)])
     decoded, grad = pl.pallas_call(
         assemble_body,
+        in_specs=[VM] * 2,
         out_shape=(
             jax.ShapeDtypeStruct((n * c * height, width), bf16),
             jax.ShapeDtypeStruct((n * c * height, width), f32),
         ),
         scratch_shapes=[pltpu.VMEM((n * c * height, width), f32)],
+        compiler_params=limit(8),
         name="assemble",
-    )(keep, got)
+    )(*near(keep, got))
     return decoded.reshape(frames.shape), grad.reshape(frames.shape)
 
 

time: 91.2 us -> 75 us (0.82)
  local copies, waits for them, and re-layouts: 12.7 us -> 0.66 us
  waiting for transfers between devices: 2.65 us -> 7.87 us
  Pallas kernels: 16.3 us -> 11.7 us
  starting transfers between devices: 57.7 us -> 53.7 us
    reshape x4 -> x0, local copies, waits for them, and re-layouts: 5.19 us -> none  [the longest x2 2.6 us: flipped_weights(): return jnp.transpose(five, (1, 4, 3, 0, 2)).reshape(3 * c, 9 * c)]
    pallas_call x3 -> x5, Pallas kernels: 16.3 us -> 11.7 us  [the longest x1 5.93 us: per_device(): pl.pallas_call(main_body, in_specs=[VM] * 11, out_specs=(VM,) * 2, out_sh...]
    unnamed x22 -> x8, local copies, waits for them, and re-layouts: 3.81 us -> 0.66 us
    ppermute x1, waiting for transfers between devices: 0.01 us -> 3.09 us  [per_device(): z1 = lax.ppermute(m1, ('ha', 'ta'), one)]
    ppermute x1, starting transfers between devices: 4.7 us -> 1.95 us  [per_device(): got = lax.ppermute(send, 'ta', [(0, 1), (1, 0)])]
    ppermute x1, starting transfers between devices: 43.7 us -> 41.1 us  [per_device(): sp = lax.ppermute(sw, 'ta', [(0, 1), (1, 0)])]
    transpose x6 -> x0, local copies, waits for them, and re-layouts: 2.31 us -> none  [the longest x2 1.3 us: forward_weights(): return jnp.transpose(five, (1, 2, 3, 0, 4)).reshape(3 * c, 9 * c)]
    ppermute x1, waiting for transfers between devices: 0.01 us -> 1.89 us  [per_device(): z2 = lax.ppermute(m2, ('ha', 'ta'), two)]
  transfers between devices with their start and end apart: 6 -> 6, of which waited for: 2 -> 4; matrix products, arithmetic and copies ran while one was open for 11% -> 0% of each run, Pallas kernels for 0% -> 3%
where the time goes in v2:
time: 75 us; the launch traced here: 74.7 us
  starting transfers between devices  53.7 us (72%)
  Pallas kernels  11.7 us (16%)
  waiting for transfers between devices  7.87 us (10%)
  between operations  0.75 us (1%)
    ppermute x1, starting transfers between devices, per_device(): sp = lax.ppermute(sw, 'ta', [(0, 1), (1, 0)])  41.1 us
    ppermute x1, starting transfers between devices, per_device(): first = lax.ppermute(ed, 'wa', pairs(0))  6.73 us
    pallas_call x1, Pallas kernels, per_device(): pl.pallas_call(main_body, in_specs=[VM] * 11, out_specs=(VM,) * 2, out_sh...  5.93 us
    ppermute x1, waiting for transfers between devices, per_device(): z1 = lax.ppermute(m1, ('ha', 'ta'), one)  3.09 us
    pallas_call x1, Pallas kernels, per_device(): pl.pallas_call(pack_body, in_specs=[HB] * 4, out_specs=(VM,) * 5, out_sha...  2.58 us
    pallas_call x1, Pallas kernels, per_device(): pl.pallas_call(weights_body, in_specs=[HB] * 2 + [VM] * 4 + [pl.BlockSpec...  2.22 us
    ppermute x1, starting transfers between devices, per_device(): z2 = lax.ppermute(m2, ('ha', 'ta'), two)  1.95 us
    ppermute x1, starting transfers between devices, per_device(): got = lax.ppermute(send, 'ta', [(0, 1), (1, 0)])  1.95 us
  transfers between devices with their start and end apart: 6, of which 4 were waited for; matrix products, arithmetic and copies ran while one was open for 0% of the time, Pallas kernels for 3%

profile of v2, /device:TPU:65, one launch (start us, length us, event | category | flops | bytes accessed | tf_op | source)
XLA Modules:
  0.0 74.7 jit_solution(6957977093323885462)
XLA Ops:
  0.6 2.6 %pack.1 = (bf16[13,96,128]{2,1,0:T(8,128)(2,1)S(1)}, bf16[13,96,128]{2,1,0:T(8,128)(2,1)S(1)}, bf16[2,4,96,128]{3,2,1,0:T(8,128)(2,1)S(1)}, bf16[17,96,128]{2,1,0:T(8,128)(2,1)S(1)}, bf16[96,128]{1,0:T(8,128)(2,1)S(1)}) custom-call(bf16[768,128]{1,0:T(8,128)(2,1)} %bitcast.18, bf16[768,128]{1,0:T(8,128)(2,1)} %bitcast.19, bf16[768,128]{1,0:T(8,128)(2,1)} %bitcast.20, ...), custom_call_target="tpu_custom_call" | custom-call | tf_op jit(solution)/shard_map/pack/pallas_call | solution.py:347
  3.2 0.7 collective-permute-start.1
  3.9 6.7 %collective-permute-start = (bf16[96,128]{1,0:T(8,128)(2,1)S(1)}, bf16[96,128]{1,0:T(8,128)(2,1)S(1)}, u32[]{:S(2)}, u32[]{:S(2)}) collective-permute-start(bf16[96,128]{1,0:T(8,128)(2,1)S(1)} %get-tuple-element.19), channel_id=1, source_target_pairs={{0,2},{2,0},{4,6},{6,4},{8,10},{10,8},{12,14},{14,12},{1,3},{3,1},... | collective-permute-start | bytes 73736 | tf_op jit(solution)/shard_map/ppermute | solution.py:372
  10.6 0.0 collective-permute-done.1.second
  10.6 1.2 %collective-permute-done.first = bf16[96,128]{1,0:T(8,128)(2,1)S(1)} collective-permute-done((bf16[96,128]{1,0:T(8,128)(2,1)S(1)}, bf16[96,128]{1,0:T(8,128)(2,1)S(1)}, u32[]{:S(2)}, u32[]{:S(2)}) %collective-permute-start) | collective-permute-done | bytes 24608 | tf_op jit(solution)/shard_map/ppermute | solution.py:372
  11.8 0.0 copy-start.3
  11.8 41.1 %collective-permute-start.2 = (bf16[17,96,128]{2,1,0:T(8,128)(2,1)S(1)}, bf16[17,96,128]{2,1,0:T(8,128)(2,1)S(1)}, u32[]{:S(2)}, u32[]{:S(2)}) collective-permute-start(bf16[17,96,128]{2,1,0:T(8,128)(2,1)S(1)} %get-tuple-element.26), channel_id=1, source_target_pairs={{0,1},{1,0},{2,3},{3,2},{4,5},{5,4},{6,7},{7,6},{8,9},{9,8},{10,11... | collective-permute-start | bytes 1253384 | tf_op jit(solution)/shard_map/ppermute | solution.py:393
  53.0 1.3 %collective-permute-start.3 = (bf16[13,96,128]{2,1,0:T(8,128)(2,1)S(1)}, bf16[13,96,128]{2,1,0:T(8,128)(2,1)S(1)}, u32[]{:S(2)}, u32[]{:S(2)}) collective-permute-start(bf16[13,96,128]{2,1,0:T(8,128)(2,1)S(1)} %get-tuple-element.23.m1), channel_id=1, source_target_pairs={{0,16},{16,32},{32,48},{48,64},{64,80},{80,96},{96,112},{112,128},... | collective-permute-start | bytes 958472 | tf_op jit(solution)/shard_map/ppermute | solution.py:391
  54.3 2.0 %collective-permute-start.4 = (bf16[13,96,128]{2,1,0:T(8,128)(2,1)S(1)}, bf16[13,96,128]{2,1,0:T(8,128)(2,1)S(1)}, u32[]{:S(2)}, u32[]{:S(2)}) collective-permute-start(bf16[13,96,128]{2,1,0:T(8,128)(2,1)S(1)} %get-tuple-element.24.after.m2), channel_id=1, source_target_pairs={{16,1},{32,17},{48,33},{64,49},{80,65},{96,81},{112,97},{128,113},... | collective-permute-start | bytes 958472 | tf_op jit(solution)/shard_map/ppermute | solution.py:392
  56.3 0.0 copy-start
  56.3 0.0 copy-start.1
  56.3 0.0 copy-start.2
  56.3 0.0 copy-done.3
  56.3 0.6 copy-done
  56.9 0.0 copy-done.1
  56.9 0.0 copy-done.2
  57.0 2.2 %weights.1 = (bf16[288,864]{1,0:T(8,128)(2,1)S(1)}, bf16[288,864]{1,0:T(8,128)(2,1)S(1)}, bf16[288,864]{1,0:T(8,128)(2,1)S(1)}, bf16[288,864]{1,0:T(8,128)(2,1)S(1)}, f32[4,96,128]{2,1,0:T(8,128)S(1)}) custom-call(bf16[3,288,288]{2,1,0:T(8,128)(2,1)} %bitcast.16, bf16[3,288,288]{2,1,0:T(8,128)(2,1)} %bitcast.17, f32[1,96]{1,0:T(1,128)S(1)} %bitcast.12, ...), custom_call_target="tpu_custom_call" | custom-call | tf_op jit(solution)/shard_map/weights/pallas_call | solution.py:398
  59.2 3.1 %collective-permute-done.3.z1 = bf16[13,96,128]{2,1,0:T(8,128)(2,1)S(1)} collective-permute-done((bf16[13,96,128]{2,1,0:T(8,128)(2,1)S(1)}, bf16[13,96,128]{2,1,0:T(8,128)(2,1)S(1)}, u32[]{:S(2)}, u32[]{:S(2)}) %collective-permute-start.3) | collective-permute-done | bytes 319520 | tf_op jit(solution)/shard_map/ppermute | solution.py:391
  62.3 1.9 %collective-permute-done.4.z2 = bf16[13,96,128]{2,1,0:T(8,128)(2,1)S(1)} collective-permute-done((bf16[13,96,128]{2,1,0:T(8,128)(2,1)S(1)}, bf16[13,96,128]{2,1,0:T(8,128)(2,1)S(1)}, u32[]{:S(2)}, u32[]{:S(2)}) %collective-permute-start.4) | collective-permute-done | bytes 319520 | tf_op jit(solution)/shard_map/ppermute | solution.py:392
  64.2 0.0 collective-permute-done.2.sp
  64.2 5.9 %block.1 = (f32[2,2,2,96,128]{4,3,2,1,0:T(8,128)S(1)}, f32[2,2,2,96,128]{4,3,2,1,0:T(8,128)S(1)}) custom-call(bf16[13,96,128]{2,1,0:T(8,128)(2,1)S(1)} %get-tuple-element.23.m1, bf16[13,96,128]{2,1,0:T(8,128)(2,1)S(1)} %get-tuple-element.24.after.m2, bf16[2,4,96,128]{3,2,1,0:T(8,128)(2,1)S(1)} %get-tuple-element.25.oc, ...), custom_call_target="tpu_custom_call" | custom-call | tf_op jit(solution)/shard_map/block/pallas_call | solution.py:414
  70.1 2.0 %collective-permute-start.5 = (f32[2,2,2,96,128]{4,3,2,1,0:T(8,128)S(1)}, f32[2,2,2,96,128]{4,3,2,1,0:T(8,128)S(1)}, u32[]{:S(2)}, u32[]{:S(2)}) collective-permute-start(f32[2,2,2,96,128]{4,3,2,1,0:T(8,128)S(1)} %get-tuple-element.33), channel_id=1, source_target_pairs={{0,1},{1,0},{2,3},{3,2},{4,5},{5,4},{6,7},{7,6},{8,9},{9,8},{10,11... | collective-permute-start | bytes 1179656 | tf_op jit(solution)/shard_map/ppermute | solution.py:433
  72.1 1.7 %collective-permute-done.5.got = f32[2,2,2,96,128]{4,3,2,1,0:T(8,128)S(1)} collective-permute-done((f32[2,2,2,96,128]{4,3,2,1,0:T(8,128)S(1)}, f32[2,2,2,96,128]{4,3,2,1,0:T(8,128)S(1)}, u32[]{:S(2)}, u32[]{:S(2)}) %collective-permute-start.5) | collective-permute-done | bytes 393248 | tf_op jit(solution)/shard_map/ppermute | solution.py:433
  73.8 0.9 %assemble.1 = (bf16[768,128]{1,0:T(8,128)(2,1)}, f32[768,128]{1,0:T(8,128)}) custom-call(f32[2,2,2,96,128]{4,3,2,1,0:T(8,128)S(1)} %get-tuple-element.32.keep, f32[2,2,2,96,128]{4,3,2,1,0:T(8,128)S(1)} %collective-permute-done.5.got), custom_call_target="tpu_custom_call" | custom-call | tf_op jit(solution)/shard_map/assemble/pallas_call | solution.py:434
  (1 shorter events, 0.0 us)
Async XLA Ops:
  3.2 7.4 %collective-permute-start.1 = (bf16[96,128]{1,0:T(8,128)(2,1)S(1)}, bf16[96,128]{1,0:T(8,128)(2,1)S(1)}, u32[]{:S(2)}, u32[]{:S(2)}) collective-permute-start(bf16[96,128]{1,0:T(8,128)(2,1)S(1)} %get-tuple-element.19), channel_id=1, source_target_pairs={{2,4},{4,2},{6,8},{8,6},{10,12},{12,10},{3,5},{5,3},{7,9},{9,7},{1... | collective-permute-start | bytes 73736 | tf_op jit(solution)/shard_map/ppermute | solution.py:373
  3.9 7.9 %collective-permute-start = (bf16[96,128]{1,0:T(8,128)(2,1)S(1)}, bf16[96,128]{1,0:T(8,128)(2,1)S(1)}, u32[]{:S(2)}, u32[]{:S(2)}) collective-permute-start(bf16[96,128]{1,0:T(8,128)(2,1)S(1)} %get-tuple-element.19), channel_id=1, source_target_pairs={{0,2},{2,0},{4,6},{6,4},{8,10},{10,8},{12,14},{14,12},{1,3},{3,1},... | collective-permute-start | bytes 73736 | tf_op jit(solution)/shard_map/ppermute | solution.py:372
  11.8 44.5 %copy-start.3 = (f32[96]{0:T(128)S(1)}, f32[96]{0:T(128)}, u32[]{:S(2)}) copy-start(f32[96]{0:T(128)} %param.18) | copy-start | bytes 1156
  11.8 52.3 %collective-permute-start.2 = (bf16[17,96,128]{2,1,0:T(8,128)(2,1)S(1)}, bf16[17,96,128]{2,1,0:T(8,128)(2,1)S(1)}, u32[]{:S(2)}, u32[]{:S(2)}) collective-permute-start(bf16[17,96,128]{2,1,0:T(8,128)(2,1)S(1)} %get-tuple-element.26), channel_id=1, source_target_pairs={{0,1},{1,0},{2,3},{3,2},{4,5},{5,4},{6,7},{7,6},{8,9},{9,8},{10,11... | collective-permute-start | bytes 1253384 | tf_op jit(solution)/shard_map/ppermute | solution.py:393
  53.0 9.3 %collective-permute-start.3 = (bf16[13,96,128]{2,1,0:T(8,128)(2,1)S(1)}, bf16[13,96,128]{2,1,0:T(8,128)(2,1)S(1)}, u32[]{:S(2)}, u32[]{:S(2)}) collective-permute-start(bf16[13,96,128]{2,1,0:T(8,128)(2,1)S(1)} %get-tuple-element.23.m1), channel_id=1, source_target_pairs={{0,16},{16,32},{32,48},{48,64},{64,80},{80,96},{96,112},{112,128},... | collective-permute-start | bytes 958472 | tf_op jit(solution)/shard_map/ppermute | solution.py:391
  54.3 9.9 %collective-permute-start.4 = (bf16[13,96,128]{2,1,0:T(8,128)(2,1)S(1)}, bf16[13,96,128]{2,1,0:T(8,128)(2,1)S(1)}, u32[]{:S(2)}, u32[]{:S(2)}) collective-permute-start(bf16[13,96,128]{2,1,0:T(8,128)(2,1)S(1)} %get-tuple-element.24.after.m2), channel_id=1, source_target_pairs={{16,1},{32,17},{48,33},{64,49},{80,65},{96,81},{112,97},{128,113},... | collective-permute-start | bytes 958472 | tf_op jit(solution)/shard_map/ppermute | solution.py:392
  56.3 0.7 copy-start
  56.3 0.7 copy-start.1
  56.3 0.7 copy-start.2
  70.1 3.6 %collective-permute-start.5 = (f32[2,2,2,96,128]{4,3,2,1,0:T(8,128)S(1)}, f32[2,2,2,96,128]{4,3,2,1,0:T(8,128)S(1)}, u32[]{:S(2)}, u32[]{:S(2)}) collective-permute-start(f32[2,2,2,96,128]{4,3,2,1,0:T(8,128)S(1)} %get-tuple-element.33), channel_id=1, source_target_pairs={{0,1},{1,0},{2,3},{3,2},{4,5},{5,4},{6,7},{7,6},{8,9},{9,8},{10,11... | collective-permute-start | bytes 1179656 | tf_op jit(solution)/shard_map/ppermute | solution.py:433

commit v3 on v2

--- a/solution.py
+++ b/solution.py
@@ -4,6 +4,7 @@
 from jax.experimental import pallas as pl
 from jax.experimental.pallas import tpu as pltpu
 from jax.sharding import PartitionSpec as P
+
 
 epsilon = 1e-06
 f32 = jnp.float32
@@ -40,11 +41,18 @@
     return z * s, back
 
 
-def pack_body(fr_far, ct_far, ci_far, cm_far, m1, m2, oc, sw, ed, scr, inp, sems):
+def pack_body(
+    fr_far, ct_far, ci_far, cm_far, wi_far, wm_far, gi, gm, bi, bm,
+    m1, m2, oc, sw, ed, wi, wm, rows_of, scr, inp, sems,
+):
     copies = [
         pltpu.make_async_copy(source, inp.at[i], sems.at[i])
         for i, source in enumerate((fr_far, ct_far, ci_far, cm_far))
     ]
+    copies.append(pltpu.make_async_copy(wi_far, wi, sems.at[4]))
+    copies.append(pltpu.make_async_copy(wm_far, wm, sems.at[5]))
+    for k, source in enumerate((gi, gm, bi, bm)):
+        copies.append(pltpu.make_async_copy(source, rows_of.at[k], sems.at[6 + k]))
     for copy in copies:
         copy.start()
     channels = m1.shape[1]
@@ -90,32 +98,22 @@
         for r in range(rows):
             oc[s, r] = scr[6 + s, pl.ds(r, channels, stride=rows), :].astype(bf16)
     ed[...] = edges.astype(bf16)
-
-
-def merge_body(first, second, m1_in, m2_in, sw_in, m1, m2, sw):
+    for copy in copies[4:]:
+        copy.wait()
+
+
+def merge_body(first, second, sw_in, sw, edge_out):
     even = lax.rem(lax.axis_index("wa"), 2) == 0
     a, b = first[...].astype(f32), second[...].astype(f32)
     inner = lanes_of(a.shape) % 4 >= 2
     edge = jnp.where(inner == even, b, a).astype(bf16)
-    m1[12] = edge
-    m2[12] = edge
+    edge_out[...] = edge
     sw[16] = edge
 
 
-def weights_body(
-    far_in, far_mid, gi, gm, bi, bm, after, w1, w2, w1f, w2f, vec, win, wmid, sems
-):
-    copies = [
-        pltpu.make_async_copy(far_in, win, sems.at[0]),
-        pltpu.make_async_copy(far_mid, wmid, sems.at[1]),
-    ]
-    for copy in copies:
-        copy.start()
+def weights_body(win, wmid, rows, after, w1, w2, w1f, w2f, vec):
     channels = w1.shape[0] // 3
-    for k, row in enumerate((gi, gm, bi, bm)):
-        vec[k] = jnp.transpose(jnp.broadcast_to(row[...], (128, channels)))
-    for copy, src, plain, turned in zip(copies, (win, wmid), (w1, w2), (w1f, w2f)):
-        copy.wait()
+    for src, plain, turned in zip((win, wmid), (w1, w2), (w1f, w2f)):
         plain[...] = jnp.concatenate([src[a].astype(f32) for a in range(3)], axis=1).astype(bf16)
         for b in range(3):
             flat = [
@@ -128,10 +126,12 @@
             turned[b * channels : (b + 1) * channels, :] = jnp.concatenate(blocks, axis=1).astype(
                 bf16
             )
+    for k in range(4):
+        vec[k] = jnp.transpose(jnp.broadcast_to(rows[k], (128, channels)))
 
 
 def main_body(
-    m1, m2, oc, sp, z1, z2, w1, w2, w1f, w2f, vec, keep, send,
+    m1, m2, oc, sp, z1, z2, edge, e1, e2, w1, w2, w1f, w2f, vec, keep, send,
     A, C, M, D, PA, PC, EA, EC,
 ):
     channels = m1.shape[1]
@@ -180,14 +180,14 @@
         D[4, e] = jnp.zeros(tile, bf16)
         D[5, e] = jnp.zeros(tile, bf16)
 
-    own, par, zo, zp = (t[...].astype(f32) for t in (m2.at[12], sp.at[16], z1.at[12], z2.at[12]))
+    own, par, zo, zp = (t[...].astype(f32) for t in (edge, sp.at[16], e1, e2))
 
     def placed(t, slot, start, rows_from, rows, to):
         moved = pltpu.roll(t, (start + 4 * to - 16 * slot - 4 * rows_from) % 128, 1)
         low = start + 4 * to
         return jnp.where((lane >= low) & (lane < low + 4 * rows), moved, 0.0)
 
-    def group(first, swapped):
+    def group(first):
         mine = yours = 0.0
         for i in range(2):
             mine += placed(own, first + i, 32 * i, 0, 4, 2 - 2 * ta)
@@ -223,7 +223,7 @@
         own_part = jnp.where(column == 2, pltpu.roll(p0, 127, 1), pltpu.roll(p2, 1, 1)) + p1
         return across, own_part
 
-    act_edges = pltpu.roll(act(group(0, True), gin), 64, 1)
+    act_edges = pltpu.roll(act(group(0), gin), 64, 1)
     cin_edges = caches(4)
     across, own_part = edge_products(
         w1, jnp.where(lane < 64, cin_edges, act_edges), jnp.where(lane < 64, act_edges, 0.0),
@@ -231,7 +231,7 @@
     )
     PA[...] = across
     EA[...] = own_part
-    across, own_part = edge_products(w2f, group(2, True), None, time_first)
+    across, own_part = edge_products(w2f, group(2), None, time_first)
     PC[...] = across
     EC[...] = own_part
     cmid_edges = pltpu.roll(caches(5), 124, 1)
@@ -344,76 +344,75 @@
     flat = lambda v: v.reshape(n * c * height, width)
     tile = (c, width)
     limit = lambda mib: pltpu.CompilerParams(vmem_limit_bytes=mib << 20)
-    m1, m2, oc, sw, ed = pl.pallas_call(
+    row = lambda v: v.reshape(1, c)
+    taps = lambda w: w.reshape(3, 3 * c, 3 * c)
+    m1, m2, oc, sw, ed, wi, wm, rows = pl.pallas_call(
         pack_body,
-        in_specs=[HB] * 4,
-        out_specs=(VM,) * 5,
+        in_specs=[HB] * 10,
+        out_specs=(VM,) * 8,
         out_shape=(
-            pltpu.VMEM((13,) + tile, bf16),
-            pltpu.VMEM((13,) + tile, bf16),
+            pltpu.VMEM((12,) + tile, bf16),
+            pltpu.VMEM((12,) + tile, bf16),
             pltpu.VMEM((2, 4) + tile, bf16),
             pltpu.VMEM((17,) + tile, bf16),
             pltpu.VMEM(tile, bf16),
+            pltpu.VMEM((3, 3 * c, 3 * c), bf16),
+            pltpu.VMEM((3, 3 * c, 3 * c), bf16),
+            pltpu.VMEM((4, 1, c), f32),
         ),
         scratch_shapes=[
             pltpu.VMEM((8, c * height, width), f32),
             pltpu.VMEM((4, n * c * height, width), bf16),
-            pltpu.SemaphoreType.DMA((4,)),
+            pltpu.SemaphoreType.DMA((10,)),
         ],
         compiler_params=limit(8),
         name="pack",
-    )(*far(flat(frames), flat(cotangent), flat(cache_in), flat(cache_mid)))
+    )(
+        *far(
+            flat(frames), flat(cotangent), flat(cache_in), flat(cache_mid),
+            taps(weight_in), taps(weight_mid),
+            row(gain_in), row(gain_mid), row(bias_in), row(bias_mid),
+        )
+    )
 
     wide = lax.axis_size("wa")
     high = lax.axis_size("ha")
     pairs = lambda start: [
         p for i in range(start, wide - 1, 2) for p in ((i, i + 1), (i + 1, i))
     ]
-    first = lax.ppermute(ed, "wa", pairs(0))
-    second = lax.ppermute(ed, "wa", pairs(1))
-    m1, m2, sw = pl.pallas_call(
-        merge_body,
-        in_specs=[VM] * 5,
-        out_specs=(VM,) * 3,
-        out_shape=(
-            pltpu.VMEM((13,) + tile, bf16),
-            pltpu.VMEM((13,) + tile, bf16),
-            pltpu.VMEM((17,) + tile, bf16),
-        ),
-        input_output_aliases={2: 0, 3: 1, 4: 2},
-        compiler_params=limit(2),
-        name="merge",
-    )(*near(first, second, m1, m2, sw))
     one = [(2 * i, 2 * i + 2) for i in range(high - 1)]
     one += [(2 * i + 3, 2 * i + 1) for i in range(high - 1)]
     two = [(2 * i + 2, 2 * i + 1) for i in range(high - 1)]
     two += [(2 * i + 1, 2 * i + 2) for i in range(high - 1)]
+    second = lax.ppermute(ed, "wa", pairs(1))
+    first = lax.ppermute(ed, "wa", pairs(0))
     z1 = lax.ppermute(m1, ("ha", "ta"), one)
     z2 = lax.ppermute(m2, ("ha", "ta"), two)
+    sw, edge = pl.pallas_call(
+        merge_body,
+        in_specs=[VM] * 3,
+        out_specs=(VM,) * 2,
+        out_shape=(pltpu.VMEM((17,) + tile, bf16), pltpu.VMEM(tile, bf16)),
+        input_output_aliases={2: 0},
+        compiler_params=limit(2),
+        name="merge",
+    )(*near(first, second, sw))
     sp = lax.ppermute(sw, "ta", [(0, 1), (1, 0)])
-
-    row = lambda v: v.reshape(1, c)
-    taps = lambda w: w.reshape(3, 3 * c, 3 * c)
+    e1 = lax.ppermute(edge, ("ha", "ta"), one)
+    e2 = lax.ppermute(edge, ("ha", "ta"), two)
+
     matrix = pltpu.VMEM((3 * c, 9 * c), bf16)
     w1, w2, w1f, w2f, vec = pl.pallas_call(
         weights_body,
-        in_specs=[HB] * 2 + [VM] * 4 + [pl.BlockSpec(memory_space=pl.ANY)],
+        in_specs=[VM] * 3 + [pl.BlockSpec(memory_space=pl.ANY)],
         out_specs=(VM,) * 5,
         out_shape=(matrix,) * 4 + (pltpu.VMEM((4,) + tile, f32),),
-        scratch_shapes=[
-            pltpu.VMEM((3, 3 * c, 3 * c), bf16),
-            pltpu.VMEM((3, 3 * c, 3 * c), bf16),
-            pltpu.SemaphoreType.DMA((2,)),
-        ],
         compiler_params=limit(8),
         name="weights",
-    )(
-        *far(taps(weight_in), taps(weight_mid)),
-        row(gain_in), row(gain_mid), row(bias_in), row(bias_mid), m2,
-    )
+    )(*near(wi, wm, rows), edge)
     keep, send = pl.pallas_call(
         main_body,
-        in_specs=[VM] * 11,
+        in_specs=[VM] * 14,
         out_specs=(VM,) * 2,
         out_shape=(pltpu.VMEM((2, 2, 2) + tile, f32),) * 2,
         scratch_shapes=[
@@ -428,7 +427,7 @@
         ],
         compiler_params=limit(16),
         name="block",
-    )(*near(m1, m2, oc, sp, z1, z2, w1, w2, w1f, w2f, vec))
+    )(*near(m1, m2, oc, sp, z1, z2, edge, e1, e2, w1, w2, w1f, w2f, vec))
 
     got = lax.ppermute(send, "ta", [(0, 1), (1, 0)])
     decoded, grad = pl.pallas_call(

time: 75 us -> 77.6 us (1.035)
  the two profiles are of different devices: /device:TPU:65 before, /device:TPU:67 now
where the time goes in v3:
time: 77.6 us; the launch traced here: 77.3 us
  starting transfers between devices  62.6 us (81%)
  Pallas kernels  10.7 us (14%)
  waiting for transfers between devices  3.29 us (4%)
    ppermute x1, starting transfers between devices, per_device(): sp = lax.ppermute(sw, 'ta', [(0, 1), (1, 0)])  42.8 us
    ppermute x1, starting transfers between devices, per_device(): e2 = lax.ppermute(edge, ('ha', 'ta'), two)  6.68 us
    pallas_call x1, Pallas kernels, per_device(): pl.pallas_call(main_body, in_specs=[VM] * 14, out_specs=(VM,) * 2, out_sh...  6.03 us
    ppermute x1, starting transfers between devices, per_device(): second = lax.ppermute(ed, 'wa', pairs(1))  4.61 us
    pallas_call x1, Pallas kernels, per_device(): pl.pallas_call(pack_body, in_specs=[HB] * 10, out_specs=(VM,) * 8, out_sh...  2.65 us
    ppermute x1, starting transfers between devices, per_device(): first = lax.ppermute(ed, 'wa', pairs(0))  1.95 us
    ppermute x1, starting transfers between devices, per_device(): z2 = lax.ppermute(m2, ('ha', 'ta'), two)  1.95 us
    ppermute x1, starting transfers between devices, per_device(): got = lax.ppermute(send, 'ta', [(0, 1), (1, 0)])  1.95 us
  transfers between devices with their start and end apart: 8, of which 3 were waited for; matrix products, arithmetic and copies ran while one was open for 0% of the time, Pallas kernels for 1%

profile of v3, /device:TPU:67, one launch (start us, length us, event | category | flops | bytes accessed | tf_op | source)
XLA Modules:
  0.0 77.3 jit_solution(5120644048483015124)
XLA Ops:
  0.6 2.7 %pack.1 = (bf16[12,96,128]{2,1,0:T(8,128)(2,1)S(1)}, bf16[12,96,128]{2,1,0:T(8,128)(2,1)S(1)}, bf16[2,4,96,128]{3,2,1,0:T(8,128)(2,1)S(1)}, bf16[17,96,128]{2,1,...) custom-call(bf16[768,128]{1,0:T(8,128)(2,1)} %bitcast.14, ...), custom_call_target="tpu_custom_call" | custom-call | tf_op jit(solution)/shard_map/pack/pallas_call | solution.py:349
  3.3 2.0 %collective-permute-start = (bf16[96,128]{1,0:T(8,128)(2,1)S(1)}, bf16[96,128]{1,0:T(8,128)(2,1)S(1)}, u32[]{:S(2)}, u32[]{:S(2)}) collective-permute-start(bf16[96,128]{1,0:T(8,128)(2,1)S(1)} %get-tuple-element.24), channel_id=1, source_target_pairs={{0,2},{2,0},{4,6},{6,4},{8,10},{10,8},{12,14},{14,12},{1,3},{3,1},... | collective-permute-start | bytes 73736 | tf_op jit(solution)/shard_map/ppermute | solution.py:388
  5.3 4.6 %collective-permute-start.1 = (bf16[96,128]{1,0:T(8,128)(2,1)S(1)}, bf16[96,128]{1,0:T(8,128)(2,1)S(1)}, u32[]{:S(2)}, u32[]{:S(2)}) collective-permute-start(bf16[96,128]{1,0:T(8,128)(2,1)S(1)} %get-tuple-element.24), channel_id=1, source_target_pairs={{2,4},{4,2},{6,8},{8,6},{10,12},{12,10},{3,5},{5,3},{7,9},{9,7},{1... | collective-permute-start | bytes 73736 | tf_op jit(solution)/shard_map/ppermute | solution.py:387
  9.9 0.0 collective-permute-done.first
  9.9 1.2 %collective-permute-done.1.second = bf16[96,128]{1,0:T(8,128)(2,1)S(1)} collective-permute-done((bf16[96,128]{1,0:T(8,128)(2,1)S(1)}, bf16[96,128]{1,0:T(8,128)(2,1)S(1)}, u32[]{:S(2)}, u32[]{:S(2)}) %collective-permute-start.1) | collective-permute-done | bytes 24608 | tf_op jit(solution)/shard_map/ppermute | solution.py:387
  11.1 42.8 %collective-permute-start.2 = (bf16[17,96,128]{2,1,0:T(8,128)(2,1)S(1)}, bf16[17,96,128]{2,1,0:T(8,128)(2,1)S(1)}, u32[]{:S(2)}, u32[]{:S(2)}) collective-permute-start(bf16[17,96,128]{2,1,0:T(8,128)(2,1)S(1)} %get-tuple-element.26), channel_id=1, source_target_pairs={{0,1},{1,0},{2,3},{3,2},{4,5},{5,4},{6,7},{7,6},{8,9},{9,8},{10,11... | collective-permute-start | bytes 1253384 | tf_op jit(solution)/shard_map/ppermute | solution.py:400
  53.9 1.3 %collective-permute-start.3 = (bf16[12,96,128]{2,1,0:T(8,128)(2,1)S(1)}, bf16[12,96,128]{2,1,0:T(8,128)(2,1)S(1)}, u32[]{:S(2)}, u32[]{:S(2)}) collective-permute-start(bf16[12,96,128]{2,1,0:T(8,128)(2,1)S(1)} %get-tuple-element.21.m1), channel_id=1, source_target_pairs={{0,16},{16,32},{32,48},{48,64},{64,80},{80,96},{96,112},{112,128},... | collective-permute-start | bytes 884744 | tf_op jit(solution)/shard_map/ppermute | solution.py:389
  55.2 2.0 %collective-permute-start.4 = (bf16[12,96,128]{2,1,0:T(8,128)(2,1)S(1)}, bf16[12,96,128]{2,1,0:T(8,128)(2,1)S(1)}, u32[]{:S(2)}, u32[]{:S(2)}) collective-permute-start(bf16[12,96,128]{2,1,0:T(8,128)(2,1)S(1)} %get-tuple-element.22.m2), channel_id=1, source_target_pairs={{16,1},{32,17},{48,33},{64,49},{80,65},{96,81},{112,97},{128,113},... | collective-permute-start | bytes 884744 | tf_op jit(solution)/shard_map/ppermute | solution.py:390
  57.2 1.3 %collective-permute-start.5 = (bf16[96,128]{1,0:T(8,128)(2,1)S(1)}, bf16[96,128]{1,0:T(8,128)(2,1)S(1)}, u32[]{:S(2)}, u32[]{:S(2)}) collective-permute-start(bf16[96,128]{1,0:T(8,128)(2,1)S(1)} %get-tuple-element.27.after.edge), channel_id=1, source_target_pairs={{0,16},{16,32},{32,48},{48,64},{64,80},{80,96},{96,112},{112,128},... | collective-permute-start | bytes 73736 | tf_op jit(solution)/shard_map/ppermute | solution.py:401
  58.5 6.7 %collective-permute-start.6 = (bf16[96,128]{1,0:T(8,128)(2,1)S(1)}, bf16[96,128]{1,0:T(8,128)(2,1)S(1)}, u32[]{:S(2)}, u32[]{:S(2)}) collective-permute-start(bf16[96,128]{1,0:T(8,128)(2,1)S(1)} %get-tuple-element.27.after.edge), channel_id=1, source_target_pairs={{16,1},{32,17},{48,33},{64,49},{80,65},{96,81},{112,97},{128,113},... | collective-permute-start | bytes 73736 | tf_op jit(solution)/shard_map/ppermute | solution.py:402
  65.2 1.1 %weights.1 = (bf16[288,864]{1,0:T(8,128)(2,1)S(1)}, bf16[288,864]{1,0:T(8,128)(2,1)S(1)}, bf16[288,864]{1,0:T(8,128)(2,1)S(1)}, bf16[288,864]{1,0:T(8,128)(2,1)S(1)}, f32[4,96,128]{2,1,0:T(8,128)S(1)}) custom-call(bf16[3,288,288]{2,1,0:T(8,128)(2,1)S(1)} %get-tuple-element.28.win, bf16[3,288,288]{2,1,0:T(8,128)(2,1)S(1)} %get-tuple-element.29.wmid, ...), custom_call_target="tpu_custom_call" | custom-call | tf_op jit(solution)/shard_map/weights/pallas_call | solution.py:405
  66.3 0.0 collective-permute-done.5.e1
  66.3 0.4 collective-permute-done.6.e2
  66.7 0.0 collective-permute-done.3.z1
  66.7 0.0 collective-permute-done.4.z2
  66.7 0.0 collective-permute-done.2.sp
  66.7 6.0 %block.1 = (f32[2,2,2,96,128]{4,3,2,1,0:T(8,128)S(1)}, f32[2,2,2,96,128]{4,3,2,1,0:T(8,128)S(1)}) custom-call(bf16[12,96,128]{2,1,0:T(8,128)(2,1)S(1)} %get-tuple-element.21.m1, bf16[12,96,128]{2,1,0:T(8,128)(2,1)S(1)} %get-tuple-element.22.m2, bf16[2,4,96,128]{3,2,1,0:T(8,128)(2,1)S(1)} %get-tuple-element.23.oc, ...), custom_call_target="tpu_custom_call" | custom-call | tf_op jit(solution)/shard_map/block/pallas_call | solution.py:413
  72.7 2.0 %collective-permute-start.7 = (f32[2,2,2,96,128]{4,3,2,1,0:T(8,128)S(1)}, f32[2,2,2,96,128]{4,3,2,1,0:T(8,128)S(1)}, u32[]{:S(2)}, u32[]{:S(2)}) collective-permute-start(f32[2,2,2,96,128]{4,3,2,1,0:T(8,128)S(1)} %get-tuple-element.37), channel_id=1, source_target_pairs={{0,1},{1,0},{2,3},{3,2},{4,5},{5,4},{6,7},{7,6},{8,9},{9,8},{10,11... | collective-permute-start | bytes 1179656 | tf_op jit(solution)/shard_map/ppermute | solution.py:432
  74.7 1.7 %collective-permute-done.7.got = f32[2,2,2,96,128]{4,3,2,1,0:T(8,128)S(1)} collective-permute-done((f32[2,2,2,96,128]{4,3,2,1,0:T(8,128)S(1)}, f32[2,2,2,96,128]{4,3,2,1,0:T(8,128)S(1)}, u32[]{:S(2)}, u32[]{:S(2)}) %collective-permute-start.7) | collective-permute-done | bytes 393248 | tf_op jit(solution)/shard_map/ppermute | solution.py:432
  76.4 0.9 %assemble.1 = (bf16[768,128]{1,0:T(8,128)(2,1)}, f32[768,128]{1,0:T(8,128)}) custom-call(f32[2,2,2,96,128]{4,3,2,1,0:T(8,128)S(1)} %get-tuple-element.36.keep, f32[2,2,2,96,128]{4,3,2,1,0:T(8,128)S(1)} %collective-permute-done.7.got), custom_call_target="tpu_custom_call" | custom-call | tf_op jit(solution)/shard_map/assemble/pallas_call | solution.py:433
  (1 shorter events, 0.0 us)
Async XLA Ops:
  3.3 6.6 %collective-permute-start = (bf16[96,128]{1,0:T(8,128)(2,1)S(1)}, bf16[96,128]{1,0:T(8,128)(2,1)S(1)}, u32[]{:S(2)}, u32[]{:S(2)}) collective-permute-start(bf16[96,128]{1,0:T(8,128)(2,1)S(1)} %get-tuple-element.24), channel_id=1, source_target_pairs={{0,2},{2,0},{4,6},{6,4},{8,10},{10,8},{12,14},{14,12},{1,3},{3,1},... | collective-permute-start | bytes 73736 | tf_op jit(solution)/shard_map/ppermute | solution.py:388
  5.3 5.8 %collective-permute-start.1 = (bf16[96,128]{1,0:T(8,128)(2,1)S(1)}, bf16[96,128]{1,0:T(8,128)(2,1)S(1)}, u32[]{:S(2)}, u32[]{:S(2)}) collective-permute-start(bf16[96,128]{1,0:T(8,128)(2,1)S(1)} %get-tuple-element.24), channel_id=1, source_target_pairs={{2,4},{4,2},{6,8},{8,6},{10,12},{12,10},{3,5},{5,3},{7,9},{9,7},{1... | collective-permute-start | bytes 73736 | tf_op jit(solution)/shard_map/ppermute | solution.py:387
  11.1 55.6 %collective-permute-start.2 = (bf16[17,96,128]{2,1,0:T(8,128)(2,1)S(1)}, bf16[17,96,128]{2,1,0:T(8,128)(2,1)S(1)}, u32[]{:S(2)}, u32[]{:S(2)}) collective-permute-start(bf16[17,96,128]{2,1,0:T(8,128)(2,1)S(1)} %get-tuple-element.26), channel_id=1, source_target_pairs={{0,1},{1,0},{2,3},{3,2},{4,5},{5,4},{6,7},{7,6},{8,9},{9,8},{10,11... | collective-permute-start | bytes 1253384 | tf_op jit(solution)/shard_map/ppermute | solution.py:400
  53.9 12.8 %collective-permute-start.3 = (bf16[12,96,128]{2,1,0:T(8,128)(2,1)S(1)}, bf16[12,96,128]{2,1,0:T(8,128)(2,1)S(1)}, u32[]{:S(2)}, u32[]{:S(2)}) collective-permute-start(bf16[12,96,128]{2,1,0:T(8,128)(2,1)S(1)} %get-tuple-element.21.m1), channel_id=1, source_target_pairs={{0,16},{16,32},{32,48},{48,64},{64,80},{80,96},{96,112},{112,128},... | collective-permute-start | bytes 884744 | tf_op jit(solution)/shard_map/ppermute | solution.py:389
  55.2 11.5 %collective-permute-start.4 = (bf16[12,96,128]{2,1,0:T(8,128)(2,1)S(1)}, bf16[12,96,128]{2,1,0:T(8,128)(2,1)S(1)}, u32[]{:S(2)}, u32[]{:S(2)}) collective-permute-start(bf16[12,96,128]{2,1,0:T(8,128)(2,1)S(1)} %get-tuple-element.22.m2), channel_id=1, source_target_pairs={{16,1},{32,17},{48,33},{64,49},{80,65},{96,81},{112,97},{128,113},... | collective-permute-start | bytes 884744 | tf_op jit(solution)/shard_map/ppermute | solution.py:390
  57.2 9.1 %collective-permute-start.5 = (bf16[96,128]{1,0:T(8,128)(2,1)S(1)}, bf16[96,128]{1,0:T(8,128)(2,1)S(1)}, u32[]{:S(2)}, u32[]{:S(2)}) collective-permute-start(bf16[96,128]{1,0:T(8,128)(2,1)S(1)} %get-tuple-element.27.after.edge), channel_id=1, source_target_pairs={{0,16},{16,32},{32,48},{48,64},{64,80},{80,96},{96,112},{112,128},... | collective-permute-start | bytes 73736 | tf_op jit(solution)/shard_map/ppermute | solution.py:401
  58.5 8.2 %collective-permute-start.6 = (bf16[96,128]{1,0:T(8,128)(2,1)S(1)}, bf16[96,128]{1,0:T(8,128)(2,1)S(1)}, u32[]{:S(2)}, u32[]{:S(2)}) collective-permute-start(bf16[96,128]{1,0:T(8,128)(2,1)S(1)} %get-tuple-element.27.after.edge), channel_id=1, source_target_pairs={{16,1},{32,17},{48,33},{64,49},{80,65},{96,81},{112,97},{128,113},... | collective-permute-start | bytes 73736 | tf_op jit(solution)/shard_map/ppermute | solution.py:402
  72.7 3.6 %collective-permute-start.7 = (f32[2,2,2,96,128]{4,3,2,1,0:T(8,128)S(1)}, f32[2,2,2,96,128]{4,3,2,1,0:T(8,128)S(1)}, u32[]{:S(2)}, u32[]{:S(2)}) collective-permute-start(f32[2,2,2,96,128]{4,3,2,1,0:T(8,128)S(1)} %get-tuple-element.37), channel_id=1, source_target_pairs={{0,1},{1,0},{2,3},{3,2},{4,5},{5,4},{6,7},{7,6},{8,9},{9,8},{10,11... | collective-permute-start | bytes 1179656 | tf_op jit(solution)/shard_map/ppermute | solution.py:432

commit v4 on v3

--- a/solution.py
+++ b/solution.py
@@ -130,31 +130,93 @@
         vec[k] = jnp.transpose(jnp.broadcast_to(rows[k], (128, channels)))
 
 
+def offsets():
+    ta = lax.axis_index("ta")
+    return ta, 1 - ta, 4 * ta, 4 - 4 * ta
+
+
+time_first = [(t, a) for t in range(3) for a in range(3)]
+row_first = [(t, a) for a in range(3) for t in range(3)]
+
+
+def lead_body(m1, m2, oc, vec, after, A, C, M):
+    ta, other, _, mb = offsets()
+    gin = vec[0]
+    for i in range(2):
+        for r in range(2):
+            for src, row in ((m2, 2 + r), (m1, mb + r)):
+                at = 2 * i + r
+                A[2 + 2 * ta + i, row] = act(src[at].astype(f32), gin).astype(bf16)
+                C[2 * ta + i, row] = src[at + 4]
+    for r in range(2):
+        A[ta, 2 + r] = m2[8 + r]
+        A[ta, mb + r] = m1[8 + r]
+        M[ta, 1 + r] = m2[10 + r]
+    M[ta, 3 - 3 * ta] = m1[10 + ta]
+    for r in range(4):
+        A[other, r + 2 - 2 * ta] = oc[0, r]
+    for k in range(3):
+        M[other, k + 1 - ta] = oc[1, k + ta]
+
+
+def products(w, ref, f, row, order):
+    channels = ref.shape[2]
+    cols = [jnp.concatenate([ref[f + t, row + i + a] for t, a in order], axis=0) for i in range(2)]
+    weights = w[:, : len(order) * channels]
+    p = jnp.dot(weights, jnp.concatenate(cols, axis=1), preferred_element_type=f32)
+    return [
+        [p[b * channels : (b + 1) * channels, 128 * i : 128 * (i + 1)] for b in range(3)]
+        for i in range(2)
+    ]
+
+
+def shifted_sum(p, edge_ref, q):
+    lane = lanes_of(p[1].shape)
+    amount = (126 - q) % 128 if isinstance(q, int) else lax.rem(254 - q, 128)
+    back = pltpu.roll(edge_ref[...], amount, 1)
+    out = p[1] + jnp.where(lane == 0, back, pltpu.roll(p[0], 1, 1))
+    return out + jnp.where(lane == 127, back, pltpu.roll(p[2], 127, 1))
+
+
+def second_layer(f, mine, slot, out, M, D, PA, PC, w2, w1f, vec):
+    pf = products(w2, M, f, 0, row_first)
+    pb = products(w1f, D, f, 0, time_first)
+    for i in range(2):
+        q = f * 32 + i * 4
+        frame = mine[2 * slot + i].astype(f32)
+        cot = mine[4 + 2 * slot + i].astype(f32)
+        decoded = frame + (shifted_sum(pf[i], PA, q) + vec[3])
+        out[0, slot, i] = decoded.astype(bf16).astype(f32)
+        _, back = act_and_back(frame, vec[0], shifted_sum(pb[i], PC, q))
+        out[1, slot, i] = cot + back
+
+
+def own_body(m2, M, D, PA, PC, w2, w1f, vec, keep):
+    ta = lax.axis_index("ta")
+    for slot in range(2):
+        second_layer(2 * ta + slot, m2, slot, keep, M, D, PA, PC, w2, w1f, vec)
+
+
 def main_body(
-    m1, m2, oc, sp, z1, z2, edge, e1, e2, w1, w2, w1f, w2f, vec, keep, send,
-    A, C, M, D, PA, PC, EA, EC,
+    A_in, C_in, M_in, sp, z1, z2, edge, e1, e2, w1, w2, w1f, w2f, vec,
+    A, C, M, D, PA, PC, send, EA, EC,
 ):
-    channels = m1.shape[1]
+    channels = sp.shape[1]
     tile = (channels, 128)
-    ta = lax.axis_index("ta")
+    ta, other, zb, mb = offsets()
     ha = lax.axis_index("ha")
     wa = lax.axis_index("wa")
     first_row = (ta == 1) | (ha > 0)
     last_row = (ta == 0) | (ha < lax.axis_size("ha") - 1)
     left_col = wa > 0
     right_col = wa < lax.axis_size("wa") - 1
-    other = 1 - ta
-    zb = 4 * ta
-    mb = 4 - 4 * ta
     lane = lanes_of(tile)
     column = lane % 4
-    gin, gmid, bin_, bmid = (vec[k] for k in range(4))
+    gin, gmid, bin_, _ = (vec[k] for k in range(4))
 
     for i in range(2):
         for r in range(2):
             for src, at, frame, row in (
-                (m2, 2 * i + r, 2 * ta + i, 2 + r),
-                (m1, 2 * i + r, 2 * ta + i, mb + r),
                 (z1, 2 * i + r, 2 * ta + i, zb + r),
                 (sp, 2 * i + r, 2 * other + i, 2 + r),
                 (sp, 8 + 2 * i + r, 2 * other + i, mb + r),
@@ -163,19 +225,10 @@
                 A[2 + frame, row] = act(src[at].astype(f32), gin).astype(bf16)
                 C[frame, row] = src[at + 4]
     for r in range(2):
-        A[ta, 2 + r] = m2[8 + r]
-        A[ta, mb + r] = m1[8 + r]
         A[ta, zb + r] = z1[8 + r]
         A[other, zb + r] = z2[8 + r]
-        M[ta, 1 + r] = m2[10 + r]
-    M[ta, 3 - 3 * ta] = m1[10 + ta]
     M[ta, 3 * ta] = z1[11 - ta]
     M[other, 3 * ta] = z2[11 - ta]
-    for r in range(4):
-        A[other, r + 2 - 2 * ta] = oc[0, r]
-    for k in range(3):
-        M[other, k + 1 - ta] = oc[1, k + ta]
-
     for e in range(4):
         D[4, e] = jnp.zeros(tile, bf16)
         D[5, e] = jnp.zeros(tile, bf16)
@@ -203,9 +256,6 @@
         out += placed(zo, slot, 32 * ta, 2 - 2 * ta, 2, 4 * ta)
         out += placed(par, slot, 32 * other, 0, 4, 2 - 2 * ta)
         return out + placed(zp, slot, 32 * other, 2 - 2 * ta, 2, 4 * ta)
-
-    time_first = [(t, a) for t in range(3) for a in range(3)]
-    row_first = [(t, a) for a in range(3) for t in range(3)]
 
     def edge_products(w, low, high, order):
         pieces = []
@@ -235,22 +285,6 @@
     PC[...] = across
     EC[...] = own_part
     cmid_edges = pltpu.roll(caches(5), 124, 1)
-
-    def products(w, ref, f, row, order):
-        cols = [
-            jnp.concatenate([ref[f + t, row + i + a] for t, a in order], axis=0) for i in range(2)
-        ]
-        weights = w[:, : len(order) * channels]
-        p = jnp.dot(weights, jnp.concatenate(cols, axis=1), preferred_element_type=f32)
-        return [
-            [p[b * channels : (b + 1) * channels, 128 * i : 128 * (i + 1)] for b in range(3)]
-            for i in range(2)
-        ]
-
-    def shifted_sum(p, edge_ref, q):
-        back = pltpu.roll(edge_ref[...], lax.rem(256 - (q + 2), 128) if not isinstance(q, int) else (126 - q) % 128, 1)
-        out = p[1] + jnp.where(lane == 0, back, pltpu.roll(p[0], 1, 1))
-        return out + jnp.where(lane == 127, back, pltpu.roll(p[2], 127, 1))
 
     def to_edges(p, edge_ref, q):
         moved = pltpu.roll(jnp.where(lane == 0, p[2], p[0]), q + 2, 1)
@@ -295,22 +329,8 @@
     across, _ = edge_products(w1f, d, None, time_first)
     PC[...] = across
 
-    def second_layer(f, mine, slot, out):
-        pf = products(w2, M, f, 0, row_first)
-        pb = products(w1f, D, f, 0, time_first)
-        for i in range(2):
-            q = f * 32 + i * 4
-            frame = mine[2 * slot + i].astype(f32)
-            cot = mine[4 + 2 * slot + i].astype(f32)
-            decoded = frame + (shifted_sum(pf[i], PA, q) + bmid)
-            out[0, slot, i] = decoded.astype(bf16).astype(f32)
-            _, back = act_and_back(frame, gin, shifted_sum(pb[i], PC, q))
-            out[1, slot, i] = cot + back
-
     for slot in range(2):
-        second_layer(2 * other + slot, sp, slot, send)
-    for slot in range(2):
-        second_layer(2 * ta + slot, m2, slot, keep)
+        second_layer(2 * other + slot, sp, slot, send, M, D, PA, PC, w2, w1f, vec)
 
 
 def assemble_body(keep, got, dec, grad, scr):
@@ -409,27 +429,46 @@
         out_shape=(matrix,) * 4 + (pltpu.VMEM((4,) + tile, f32),),
         compiler_params=limit(8),
         name="weights",
-    )(*near(wi, wm, rows), edge)
-    keep, send = pl.pallas_call(
+    )(*near(wi, wm, rows), m2)
+    staged = (
+        pltpu.VMEM((6, 6) + tile, bf16),
+        pltpu.VMEM((4, 6) + tile, bf16),
+        pltpu.VMEM((6, 4) + tile, bf16),
+    )
+    A, C, M = pl.pallas_call(
+        lead_body,
+        in_specs=[VM] * 4 + [pl.BlockSpec(memory_space=pl.ANY)],
+        out_specs=(VM,) * 3,
+        out_shape=staged,
+        compiler_params=limit(8),
+        name="lead",
+    )(*near(m1, m2, oc, vec), edge)
+    half = pltpu.VMEM((2, 2, 2) + tile, f32)
+    A, C, M, D, PA, PC, send = pl.pallas_call(
         main_body,
         in_specs=[VM] * 14,
-        out_specs=(VM,) * 2,
-        out_shape=(pltpu.VMEM((2, 2, 2) + tile, f32),) * 2,
-        scratch_shapes=[
-            pltpu.VMEM((6, 6) + tile, bf16),
-            pltpu.VMEM((4, 6) + tile, bf16),
-            pltpu.VMEM((6, 4) + tile, bf16),
+        out_specs=(VM,) * 7,
+        out_shape=staged
+        + (
             pltpu.VMEM((6, 4) + tile, bf16),
             pltpu.VMEM(tile, f32),
             pltpu.VMEM(tile, f32),
-            pltpu.VMEM(tile, f32),
-            pltpu.VMEM(tile, f32),
-        ],
-        compiler_params=limit(16),
+            half,
+        ),
+        scratch_shapes=[pltpu.VMEM(tile, f32), pltpu.VMEM(tile, f32)],
+        input_output_aliases={0: 0, 1: 1, 2: 2},
+        compiler_params=limit(12),
         name="block",
-    )(*near(m1, m2, oc, sp, z1, z2, edge, e1, e2, w1, w2, w1f, w2f, vec))
-
+    )(*near(A, C, M, sp, z1, z2, edge, e1, e2, w1, w2, w1f, w2f, vec))
     got = lax.ppermute(send, "ta", [(0, 1), (1, 0)])
+    keep = pl.pallas_call(
+        own_body,
+        in_specs=[VM] * 8,
+        out_specs=VM,
+        out_shape=half,
+        compiler_params=limit(8),
+        name="own",
+    )(*near(m2, M, D, PA, PC, w2, w1f, vec))
     decoded, grad = pl.pallas_call(
         assemble_body,
         in_specs=[VM] * 2,

time: 77.6 us -> 75.3 us (0.970)
  the two profiles are of different devices: /device:TPU:67 before, /device:TPU:65 now
where the time goes in v4:
time: 75.3 us; the launch traced here: 75 us
  starting transfers between devices  58.7 us (78%)
  Pallas kernels  11 us (15%)
  waiting for transfers between devices  4.59 us (6%)
    ppermute x1, starting transfers between devices, per_device(): sp = lax.ppermute(sw, 'ta', [(0, 1), (1, 0)])  41.1 us
    ppermute x1, starting transfers between devices, per_device(): first = lax.ppermute(ed, 'wa', pairs(0))  6.73 us
    pallas_call x1, Pallas kernels, per_device(): pl.pallas_call(main_body, in_specs=[VM] * 14, out_specs=(VM,) * 7, out_sh...  5.21 us
    ppermute x1, starting transfers between devices, per_device(): e2 = lax.ppermute(edge, ('ha', 'ta'), two)  3.67 us
    pallas_call x1, Pallas kernels, per_device(): pl.pallas_call(pack_body, in_specs=[HB] * 10, out_specs=(VM,) * 8, out_sh...  2.65 us
    ppermute x1, starting transfers between devices, per_device(): z2 = lax.ppermute(m2, ('ha', 'ta'), two)  1.95 us
    ppermute x1, starting transfers between devices, per_device(): got = lax.ppermute(send, 'ta', [(0, 1), (1, 0)])  1.95 us
  transfers between devices with their start and end apart: 8, of which 4 were waited for; matrix products, arithmetic and copies ran while one was open for 0% of the time, Pallas kernels for 3%

profile of v4, /device:TPU:65, one launch (start us, length us, event | category | flops | bytes accessed | tf_op | source)
XLA Modules:
  0.0 75.0 jit_solution(13922847660426549895)
XLA Ops:
  0.6 2.6 %pack.1 = (bf16[12,96,128]{2,1,0:T(8,128)(2,1)S(1)}, bf16[12,96,128]{2,1,0:T(8,128)(2,1)S(1)}, bf16[2,4,96,128]{3,2,1,0:T(8,128)(2,1)S(1)}, bf16[17,96,128]{2,1,...) custom-call(bf16[768,128]{1,0:T(8,128)(2,1)} %bitcast.14, ...), custom_call_target="tpu_custom_call" | custom-call | tf_op jit(solution)/shard_map/pack/pallas_call | solution.py:369
  3.3 0.7 collective-permute-start.1
  4.0 6.7 %collective-permute-start = (bf16[96,128]{1,0:T(8,128)(2,1)S(1)}, bf16[96,128]{1,0:T(8,128)(2,1)S(1)}, u32[]{:S(2)}, u32[]{:S(2)}) collective-permute-start(bf16[96,128]{1,0:T(8,128)(2,1)S(1)} %get-tuple-element.34), channel_id=1, source_target_pairs={{0,2},{2,0},{4,6},{6,4},{8,10},{10,8},{12,14},{14,12},{1,3},{3,1},... | collective-permute-start | bytes 73736 | tf_op jit(solution)/shard_map/ppermute | solution.py:408
  10.7 0.0 collective-permute-done.1.second
  10.7 1.2 %collective-permute-done.first = bf16[96,128]{1,0:T(8,128)(2,1)S(1)} collective-permute-done((bf16[96,128]{1,0:T(8,128)(2,1)S(1)}, bf16[96,128]{1,0:T(8,128)(2,1)S(1)}, u32[]{:S(2)}, u32[]{:S(2)}) %collective-permute-start) | collective-permute-done | bytes 24608 | tf_op jit(solution)/shard_map/ppermute | solution.py:408
  11.9 41.1 %collective-permute-start.2 = (bf16[17,96,128]{2,1,0:T(8,128)(2,1)S(1)}, bf16[17,96,128]{2,1,0:T(8,128)(2,1)S(1)}, u32[]{:S(2)}, u32[]{:S(2)}) collective-permute-start(bf16[17,96,128]{2,1,0:T(8,128)(2,1)S(1)} %get-tuple-element.40), channel_id=1, source_target_pairs={{0,1},{1,0},{2,3},{3,2},{4,5},{5,4},{6,7},{7,6},{8,9},{9,8},{10,11... | collective-permute-start | bytes 1253384 | tf_op jit(solution)/shard_map/ppermute | solution.py:420
  53.1 1.3 %collective-permute-start.3 = (bf16[12,96,128]{2,1,0:T(8,128)(2,1)S(1)}, bf16[12,96,128]{2,1,0:T(8,128)(2,1)S(1)}, u32[]{:S(2)}, u32[]{:S(2)}) collective-permute-start(bf16[12,96,128]{2,1,0:T(8,128)(2,1)S(1)} %get-tuple-element.28.m1), channel_id=1, source_target_pairs={{0,16},{16,32},{32,48},{48,64},{64,80},{80,96},{96,112},{112,128},... | collective-permute-start | bytes 884744 | tf_op jit(solution)/shard_map/ppermute | solution.py:409
  54.4 2.0 %collective-permute-start.4 = (bf16[12,96,128]{2,1,0:T(8,128)(2,1)S(1)}, bf16[12,96,128]{2,1,0:T(8,128)(2,1)S(1)}, u32[]{:S(2)}, u32[]{:S(2)}) collective-permute-start(bf16[12,96,128]{2,1,0:T(8,128)(2,1)S(1)} %get-tuple-element.27.after.m2), channel_id=1, source_target_pairs={{16,1},{32,17},{48,33},{64,49},{80,65},{96,81},{112,97},{128,113},... | collective-permute-start | bytes 884744 | tf_op jit(solution)/shard_map/ppermute | solution.py:410
  56.3 3.7 %collective-permute-start.6 = (bf16[96,128]{1,0:T(8,128)(2,1)S(1)}, bf16[96,128]{1,0:T(8,128)(2,1)S(1)}, u32[]{:S(2)}, u32[]{:S(2)}) collective-permute-start(bf16[96,128]{1,0:T(8,128)(2,1)S(1)} %get-tuple-element.36.after.edge), channel_id=1, source_target_pairs={{16,1},{32,17},{48,33},{64,49},{80,65},{96,81},{112,97},{128,113},... | collective-permute-start | bytes 73736 | tf_op jit(solution)/shard_map/ppermute | solution.py:422
  60.0 1.3 %collective-permute-start.5 = (bf16[96,128]{1,0:T(8,128)(2,1)S(1)}, bf16[96,128]{1,0:T(8,128)(2,1)S(1)}, u32[]{:S(2)}, u32[]{:S(2)}) collective-permute-start(bf16[96,128]{1,0:T(8,128)(2,1)S(1)} %get-tuple-element.36.after.edge), channel_id=1, source_target_pairs={{0,16},{16,32},{32,48},{48,64},{64,80},{80,96},{96,112},{112,128},... | collective-permute-start | bytes 73736 | tf_op jit(solution)/shard_map/ppermute | solution.py:421
  61.3 1.1 %weights.1 = (bf16[288,864]{1,0:T(8,128)(2,1)S(1)}, bf16[288,864]{1,0:T(8,128)(2,1)S(1)}, bf16[288,864]{1,0:T(8,128)(2,1)S(1)}, bf16[288,864]{1,0:T(8,128)(2,1)S(1)}, f32[4,96,128]{2,1,0:T(8,128)S(1)}) custom-call(bf16[3,288,288]{2,1,0:T(8,128)(2,1)S(1)} %get-tuple-element.30.win, bf16[3,288,288]{2,1,0:T(8,128)(2,1)S(1)} %get-tuple-element.31.wmid, ...), custom_call_target="tpu_custom_call" | custom-call | tf_op jit(solution)/shard_map/weights/pallas_call | solution.py:425
  62.4 0.2 lead.1
  62.6 1.4 %collective-permute-done.6.e2 = bf16[96,128]{1,0:T(8,128)(2,1)S(1)} collective-permute-done((bf16[96,128]{1,0:T(8,128)(2,1)S(1)}, bf16[96,128]{1,0:T(8,128)(2,1)S(1)}, u32[]{:S(2)}, u32[]{:S(2)}) %collective-permute-start.6) | collective-permute-done | bytes 24608 | tf_op jit(solution)/shard_map/ppermute | solution.py:422
  64.0 1.3 %collective-permute-done.5.e1 = bf16[96,128]{1,0:T(8,128)(2,1)S(1)} collective-permute-done((bf16[96,128]{1,0:T(8,128)(2,1)S(1)}, bf16[96,128]{1,0:T(8,128)(2,1)S(1)}, u32[]{:S(2)}, u32[]{:S(2)}) %collective-permute-start.5) | collective-permute-done | bytes 24608 | tf_op jit(solution)/shard_map/ppermute | solution.py:421
  65.3 0.0 collective-permute-done.3.z1
  65.3 0.0 collective-permute-done.4.z2
  65.3 0.0 collective-permute-done.2.sp
  65.3 5.2 %block.1 = (bf16[6,6,96,128]{3,2,1,0:T(8,128)(2,1)S(1)}, bf16[4,6,96,128]{3,2,1,0:T(8,128)(2,1)S(1)}, bf16[6,4,96,128]{3,2,1,0:T(8,128)(2,1)S(1)}, bf16[6,4,96,1...) custom-call(bf16[6,6,96,128]{3,2,1,0:T(8,128)(2,1)S(1)} %get-tuple-e, ...), custom_call_target="tpu_custom_call", output_to_operand_aliasing={{0}: (0, {}), {1}: (1, {}), {2}: (2, {})} | custom-call | tf_op jit(solution)/shard_map/block/pallas_call | solution.py:447
  70.5 2.0 %collective-permute-start.7 = (f32[2,2,2,96,128]{4,3,2,1,0:T(8,128)S(1)}, f32[2,2,2,96,128]{4,3,2,1,0:T(8,128)S(1)}, u32[]{:S(2)}, u32[]{:S(2)}) collective-permute-start(f32[2,2,2,96,128]{4,3,2,1,0:T(8,128)S(1)} %get-tuple-element.49), channel_id=1, source_target_pairs={{0,1},{1,0},{2,3},{3,2},{4,5},{5,4},{6,7},{7,6},{8,9},{9,8},{10,11... | collective-permute-start | bytes 1179656 | tf_op jit(solution)/shard_map/ppermute | solution.py:463
  72.4 1.0 %own.1.keep = f32[2,2,2,96,128]{4,3,2,1,0:T(8,128)S(1)} custom-call(bf16[12,96,128]{2,1,0:T(8,128)(2,1)S(1)} %get-tuple-element.27.after.m2, bf16[6,4,96,128]{3,2,1,0:T(8,128)(2,1)S(1)} %get-tuple-element.45.M, bf16[6,4,96,128]{3,2,1,0:T(8,128)(2,1)S(1)} %get-tuple-element.46.D, f32[96,128]{1,0:T(8,128)S(1)} %get-tuple-element.47.PA, ...), custom_call_target="tpu_custom_call" | custom-call | tf_op jit(solution)/shard_map/own/pallas_call | solution.py:464
  73.4 0.7 collective-permute-done.7.got
  74.1 0.9 %assemble.1 = (bf16[768,128]{1,0:T(8,128)(2,1)}, f32[768,128]{1,0:T(8,128)}) custom-call(f32[2,2,2,96,128]{4,3,2,1,0:T(8,128)S(1)} %own.1.keep, f32[2,2,2,96,128]{4,3,2,1,0:T(8,128)S(1)} %collective-permute-done.7.got), custom_call_target="tpu_custom_call" | custom-call | tf_op jit(solution)/shard_map/assemble/pallas_call | solution.py:472
  (1 shorter events, 0.0 us)
Async XLA Ops:
  3.3 7.4 %collective-permute-start.1 = (bf16[96,128]{1,0:T(8,128)(2,1)S(1)}, bf16[96,128]{1,0:T(8,128)(2,1)S(1)}, u32[]{:S(2)}, u32[]{:S(2)}) collective-permute-start(bf16[96,128]{1,0:T(8,128)(2,1)S(1)} %get-tuple-element.34), channel_id=1, source_target_pairs={{2,4},{4,2},{6,8},{8,6},{10,12},{12,10},{3,5},{5,3},{7,9},{9,7},{1... | collective-permute-start | bytes 73736 | tf_op jit(solution)/shard_map/ppermute | solution.py:407
  4.0 7.9 %collective-permute-start = (bf16[96,128]{1,0:T(8,128)(2,1)S(1)}, bf16[96,128]{1,0:T(8,128)(2,1)S(1)}, u32[]{:S(2)}, u32[]{:S(2)}) collective-permute-start(bf16[96,128]{1,0:T(8,128)(2,1)S(1)} %get-tuple-element.34), channel_id=1, source_target_pairs={{0,2},{2,0},{4,6},{6,4},{8,10},{10,8},{12,14},{14,12},{1,3},{3,1},... | collective-permute-start | bytes 73736 | tf_op jit(solution)/shard_map/ppermute | solution.py:408
  11.9 53.4 %collective-permute-start.2 = (bf16[17,96,128]{2,1,0:T(8,128)(2,1)S(1)}, bf16[17,96,128]{2,1,0:T(8,128)(2,1)S(1)}, u32[]{:S(2)}, u32[]{:S(2)}) collective-permute-start(bf16[17,96,128]{2,1,0:T(8,128)(2,1)S(1)} %get-tuple-element.40), channel_id=1, source_target_pairs={{0,1},{1,0},{2,3},{3,2},{4,5},{5,4},{6,7},{7,6},{8,9},{9,8},{10,11... | collective-permute-start | bytes 1253384 | tf_op jit(solution)/shard_map/ppermute | solution.py:420
  53.1 12.2 %collective-permute-start.3 = (bf16[12,96,128]{2,1,0:T(8,128)(2,1)S(1)}, bf16[12,96,128]{2,1,0:T(8,128)(2,1)S(1)}, u32[]{:S(2)}, u32[]{:S(2)}) collective-permute-start(bf16[12,96,128]{2,1,0:T(8,128)(2,1)S(1)} %get-tuple-element.28.m1), channel_id=1, source_target_pairs={{0,16},{16,32},{32,48},{48,64},{64,80},{80,96},{96,112},{112,128},... | collective-permute-start | bytes 884744 | tf_op jit(solution)/shard_map/ppermute | solution.py:409
  54.4 10.9 %collective-permute-start.4 = (bf16[12,96,128]{2,1,0:T(8,128)(2,1)S(1)}, bf16[12,96,128]{2,1,0:T(8,128)(2,1)S(1)}, u32[]{:S(2)}, u32[]{:S(2)}) collective-permute-start(bf16[12,96,128]{2,1,0:T(8,128)(2,1)S(1)} %get-tuple-element.27.after.m2), channel_id=1, source_target_pairs={{16,1},{32,17},{48,33},{64,49},{80,65},{96,81},{112,97},{128,113},... | collective-permute-start | bytes 884744 | tf_op jit(solution)/shard_map/ppermute | solution.py:410
  56.3 7.6 %collective-permute-start.6 = (bf16[96,128]{1,0:T(8,128)(2,1)S(1)}, bf16[96,128]{1,0:T(8,128)(2,1)S(1)}, u32[]{:S(2)}, u32[]{:S(2)}) collective-permute-start(bf16[96,128]{1,0:T(8,128)(2,1)S(1)} %get-tuple-element.36.after.edge), channel_id=1, source_target_pairs={{16,1},{32,17},{48,33},{64,49},{80,65},{96,81},{112,97},{128,113},... | collective-permute-start | bytes 73736 | tf_op jit(solution)/shard_map/ppermute | solution.py:422
  60.0 5.2 %collective-permute-start.5 = (bf16[96,128]{1,0:T(8,128)(2,1)S(1)}, bf16[96,128]{1,0:T(8,128)(2,1)S(1)}, u32[]{:S(2)}, u32[]{:S(2)}) collective-permute-start(bf16[96,128]{1,0:T(8,128)(2,1)S(1)} %get-tuple-element.36.after.edge), channel_id=1, source_target_pairs={{0,16},{16,32},{32,48},{48,64},{64,80},{80,96},{96,112},{112,128},... | collective-permute-start | bytes 73736 | tf_op jit(solution)/shard_map/ppermute | solution.py:421
  70.5 3.6 %collective-permute-start.7 = (f32[2,2,2,96,128]{4,3,2,1,0:T(8,128)S(1)}, f32[2,2,2,96,128]{4,3,2,1,0:T(8,128)S(1)}, u32[]{:S(2)}, u32[]{:S(2)}) collective-permute-start(f32[2,2,2,96,128]{4,3,2,1,0:T(8,128)S(1)} %get-tuple-element.49), channel_id=1, source_target_pairs={{0,1},{1,0},{2,3},{3,2},{4,5},{5,4},{6,7},{7,6},{8,9},{9,8},{10,11... | collective-permute-start | bytes 1179656 | tf_op jit(solution)/shard_map/ppermute | solution.py:463

commit v5 on v4

--- a/solution.py
+++ b/solution.py
@@ -139,20 +139,29 @@
 row_first = [(t, a) for a in range(3) for t in range(3)]
 
 
-def lead_body(m1, m2, oc, vec, after, A, C, M):
-    ta, other, _, mb = offsets()
+def lead_body(m1, m2, oc, z1, z2, vec, A, C, M):
+    ta, other, zb, mb = offsets()
     gin = vec[0]
     for i in range(2):
         for r in range(2):
-            for src, row in ((m2, 2 + r), (m1, mb + r)):
-                at = 2 * i + r
-                A[2 + 2 * ta + i, row] = act(src[at].astype(f32), gin).astype(bf16)
-                C[2 * ta + i, row] = src[at + 4]
+            at = 2 * i + r
+            for src, frame, row in (
+                (m2, 2 * ta + i, 2 + r),
+                (m1, 2 * ta + i, mb + r),
+                (z1, 2 * ta + i, zb + r),
+                (z2, 2 * other + i, zb + r),
+            ):
+                A[2 + frame, row] = act(src[at].astype(f32), gin).astype(bf16)
+                C[frame, row] = src[at + 4]
     for r in range(2):
         A[ta, 2 + r] = m2[8 + r]
         A[ta, mb + r] = m1[8 + r]
+        A[ta, zb + r] = z1[8 + r]
+        A[other, zb + r] = z2[8 + r]
         M[ta, 1 + r] = m2[10 + r]
     M[ta, 3 - 3 * ta] = m1[10 + ta]
+    M[ta, 3 * ta] = z1[11 - ta]
+    M[other, 3 * ta] = z2[11 - ta]
     for r in range(4):
         A[other, r + 2 - 2 * ta] = oc[0, r]
     for k in range(3):
@@ -178,9 +187,12 @@
     return out + jnp.where(lane == 127, back, pltpu.roll(p[2], 127, 1))
 
 
-def second_layer(f, mine, slot, out, M, D, PA, PC, w2, w1f, vec):
-    pf = products(w2, M, f, 0, row_first)
-    pb = products(w1f, D, f, 0, time_first)
+def second_products(f, M, D, w2, w1f):
+    return products(w2, M, f, 0, row_first), products(w1f, D, f, 0, time_first)
+
+
+def second_layer(f, mine, slot, out, both, PA, PC, vec):
+    pf, pb = both
     for i in range(2):
         q = f * 32 + i * 4
         frame = mine[2 * slot + i].astype(f32)
@@ -194,16 +206,17 @@
 def own_body(m2, M, D, PA, PC, w2, w1f, vec, keep):
     ta = lax.axis_index("ta")
     for slot in range(2):
-        second_layer(2 * ta + slot, m2, slot, keep, M, D, PA, PC, w2, w1f, vec)
+        f = 2 * ta + slot
+        second_layer(f, m2, slot, keep, second_products(f, M, D, w2, w1f), PA, PC, vec)
 
 
 def main_body(
-    A_in, C_in, M_in, sp, z1, z2, edge, e1, e2, w1, w2, w1f, w2f, vec,
+    A_in, C_in, M_in, sp, edge, e1, e2, w1, w2, w1f, w2f, vec,
     A, C, M, D, PA, PC, send, EA, EC,
 ):
     channels = sp.shape[1]
     tile = (channels, 128)
-    ta, other, zb, mb = offsets()
+    ta, other, _, mb = offsets()
     ha = lax.axis_index("ha")
     wa = lax.axis_index("wa")
     first_row = (ta == 1) | (ha > 0)
@@ -217,18 +230,11 @@
     for i in range(2):
         for r in range(2):
             for src, at, frame, row in (
-                (z1, 2 * i + r, 2 * ta + i, zb + r),
                 (sp, 2 * i + r, 2 * other + i, 2 + r),
                 (sp, 8 + 2 * i + r, 2 * other + i, mb + r),
-                (z2, 2 * i + r, 2 * other + i, zb + r),
             ):
                 A[2 + frame, row] = act(src[at].astype(f32), gin).astype(bf16)
                 C[frame, row] = src[at + 4]
-    for r in range(2):
-        A[ta, zb + r] = z1[8 + r]
-        A[other, zb + r] = z2[8 + r]
-    M[ta, 3 * ta] = z1[11 - ta]
-    M[other, 3 * ta] = z2[11 - ta]
     for e in range(4):
         D[4, e] = jnp.zeros(tile, bf16)
         D[5, e] = jnp.zeros(tile, bf16)
@@ -257,7 +263,7 @@
         out += placed(par, slot, 32 * other, 0, 4, 2 - 2 * ta)
         return out + placed(zp, slot, 32 * other, 2 - 2 * ta, 2, 4 * ta)
 
-    def edge_products(w, low, high, order):
+    def edge_products(w, low, high, order, last=False):
         pieces = []
         for t, a in order:
             s = 32 * t + 4 * a
@@ -267,12 +273,27 @@
             moved = pltpu.roll(low, 128 - s, 1)
             beyond = 0.0 if high is None else pltpu.roll(high, 128 - s, 1)
             pieces.append(jnp.where(lane < 128 - s, moved, beyond).astype(bf16))
-        p = jnp.dot(w[...], jnp.concatenate(pieces, axis=0), preferred_element_type=f32)
+        stacked = jnp.concatenate(pieces, axis=0)
+        if last:
+            outer = jnp.concatenate([w[:channels, :], w[2 * channels :, :]], axis=0)
+            p = jnp.dot(outer, stacked, preferred_element_type=f32)
+            return jnp.where(column == 2, p[:channels], p[channels:])
+        p = jnp.dot(w[...], stacked, preferred_element_type=f32)
         p0, p1, p2 = (p[b * channels : (b + 1) * channels] for b in range(3))
         across = jnp.where(column == 2, p0, p2)
         own_part = jnp.where(column == 2, pltpu.roll(p0, 127, 1), pltpu.roll(p2, 1, 1)) + p1
         return across, own_part
 
+    def to_edges(p, edge_ref, q):
+        moved = pltpu.roll(jnp.where(lane == 0, p[2], p[0]), q + 2, 1)
+        here = (lane == q + 1) | (lane == q + 2)
+        edge_ref[...] = edge_ref[...] + jnp.where(here, moved, 0.0)
+
+    def first_products(f, pair):
+        pf = products(w1, A, f, 2 * pair, row_first)
+        return pf, products(w2f, C, f, 2 * pair, time_first[: 3 * (4 - f)])
+
+    early = [first_products(0, pair) for pair in range(2)]
     act_edges = pltpu.roll(act(group(0), gin), 64, 1)
     cin_edges = caches(4)
     across, own_part = edge_products(
@@ -286,15 +307,9 @@
     EC[...] = own_part
     cmid_edges = pltpu.roll(caches(5), 124, 1)
 
-    def to_edges(p, edge_ref, q):
-        moved = pltpu.roll(jnp.where(lane == 0, p[2], p[0]), q + 2, 1)
-        here = (lane == q + 1) | (lane == q + 2)
-        edge_ref[...] = edge_ref[...] + jnp.where(here, moved, 0.0)
-
     def first_layer(f):
         for pair in range(2):
-            pf = products(w1, A, f, 2 * pair, row_first)
-            pb = products(w2f, C, f, 2 * pair, time_first[: 3 * (4 - f)])
+            pf, pb = early[pair] if f == 0 else first_products(f, pair)
             for i in range(2):
                 e = 2 * pair + i
                 q = f * 32 + e * 4
@@ -315,6 +330,7 @@
     for f in range(4):
         first_layer(f)
 
+    late = [second_products(2 * other + slot, M, D, w2, w1f) for slot in range(2)]
     hidden = (EA[...] + bin_).astype(bf16).astype(f32)
     a, d = act_and_back(hidden, gmid, EC[...])
     row = (lane % 32) // 4
@@ -324,13 +340,11 @@
     d = jnp.where(inside, d, 0.0).astype(bf16).astype(f32)
     a = pltpu.roll(a, 64, 1)
     low = jnp.where(lane < 64, cmid_edges, a)
-    across, _ = edge_products(w2, low, jnp.where(lane < 64, a, 0.0), row_first)
-    PA[...] = across
-    across, _ = edge_products(w1f, d, None, time_first)
-    PC[...] = across
+    PA[...] = edge_products(w2, low, jnp.where(lane < 64, a, 0.0), row_first, last=True)
+    PC[...] = edge_products(w1f, d, None, time_first, last=True)
 
     for slot in range(2):
-        second_layer(2 * other + slot, sp, slot, send, M, D, PA, PC, w2, w1f, vec)
+        second_layer(2 * other + slot, sp, slot, send, late[slot], PA, PC, vec)
 
 
 def assemble_body(keep, got, dec, grad, scr):
@@ -437,16 +451,16 @@
     )
     A, C, M = pl.pallas_call(
         lead_body,
-        in_specs=[VM] * 4 + [pl.BlockSpec(memory_space=pl.ANY)],
+        in_specs=[VM] * 6,
         out_specs=(VM,) * 3,
         out_shape=staged,
         compiler_params=limit(8),
         name="lead",
-    )(*near(m1, m2, oc, vec), edge)
+    )(*near(m1, m2, oc, z1, z2, vec))
     half = pltpu.VMEM((2, 2, 2) + tile, f32)
     A, C, M, D, PA, PC, send = pl.pallas_call(
         main_body,
-        in_specs=[VM] * 14,
+        in_specs=[VM] * 12,
         out_specs=(VM,) * 7,
         out_shape=staged
         + (
@@ -459,7 +473,7 @@
         input_output_aliases={0: 0, 1: 1, 2: 2},
         compiler_params=limit(12),
         name="block",
-    )(*near(A, C, M, sp, z1, z2, edge, e1, e2, w1, w2, w1f, w2f, vec))
+    )(*near(A, C, M, sp, edge, e1, e2, w1, w2, w1f, w2f, vec))
     got = lax.ppermute(send, "ta", [(0, 1), (1, 0)])
     keep = pl.pallas_call(
         own_body,

time: 75.3 us -> 74.5 us (0.989)
    ppermute x1, waiting for transfers between devices: 1.39 us -> 0.01 us  [per_device(): e2 = lax.ppermute(edge, ('ha', 'ta'), two)]
    ppermute x1, waiting for transfers between devices: 0.01 us -> 1.28 us  [per_device(): z2 = lax.ppermute(m2, ('ha', 'ta'), two)]
where the time goes in v5:
time: 74.5 us; the launch traced here: 74.2 us
  starting transfers between devices  58.7 us (79%)
  Pallas kernels  10.3 us (14%)
  waiting for transfers between devices  4.44 us (6%)
  between operations  0.76 us (1%)
    ppermute x1, starting transfers between devices, per_device(): sp = lax.ppermute(sw, 'ta', [(0, 1), (1, 0)])  41.1 us
    ppermute x1, starting transfers between devices, per_device(): first = lax.ppermute(ed, 'wa', pairs(0))  6.73 us
    pallas_call x1, Pallas kernels, per_device(): pl.pallas_call(main_body, in_specs=[VM] * 12, out_specs=(VM,) * 7, out_sh...  4.4 us
    ppermute x1, starting transfers between devices, per_device(): e2 = lax.ppermute(edge, ('ha', 'ta'), two)  3.67 us
    pallas_call x1, Pallas kernels, per_device(): pl.pallas_call(pack_body, in_specs=[HB] * 10, out_specs=(VM,) * 8, out_sh...  2.65 us
    ppermute x1, starting transfers between devices, per_device(): z2 = lax.ppermute(m2, ('ha', 'ta'), two)  1.95 us
    ppermute x1, starting transfers between devices, per_device(): got = lax.ppermute(send, 'ta', [(0, 1), (1, 0)])  1.95 us
  transfers between devices with their start and end apart: 8, of which 4 were waited for; matrix products, arithmetic and copies ran while one was open for 0% of the time, Pallas kernels for 3%

profile of v5, /device:TPU:65, one launch (start us, length us, event | category | flops | bytes accessed | tf_op | source)
XLA Modules:
  0.0 74.2 jit_solution(1467626803803083240)
XLA Ops:
  0.6 2.6 %pack.1 = (bf16[12,96,128]{2,1,0:T(8,128)(2,1)S(1)}, bf16[12,96,128]{2,1,0:T(8,128)(2,1)S(1)}, bf16[2,4,96,128]{3,2,1,0:T(8,128)(2,1)S(1)}, bf16[17,96,128]{2,1,...) custom-call(bf16[768,128]{1,0:T(8,128)(2,1)} %bitcast.14, ...), custom_call_target="tpu_custom_call" | custom-call | tf_op jit(solution)/shard_map/pack/pallas_call | solution.py:383
  3.3 0.7 collective-permute-start.3
  4.0 6.7 %collective-permute-start.2 = (bf16[96,128]{1,0:T(8,128)(2,1)S(1)}, bf16[96,128]{1,0:T(8,128)(2,1)S(1)}, u32[]{:S(2)}, u32[]{:S(2)}) collective-permute-start(bf16[96,128]{1,0:T(8,128)(2,1)S(1)} %get-tuple-element.37), channel_id=1, source_target_pairs={{0,2},{2,0},{4,6},{6,4},{8,10},{10,8},{12,14},{14,12},{1,3},{3,1},... | collective-permute-start | bytes 73736 | tf_op jit(solution)/shard_map/ppermute | solution.py:422
  10.7 0.0 collective-permute-done.3.second
  10.7 1.2 %collective-permute-done.2.first = bf16[96,128]{1,0:T(8,128)(2,1)S(1)} collective-permute-done((bf16[96,128]{1,0:T(8,128)(2,1)S(1)}, bf16[96,128]{1,0:T(8,128)(2,1)S(1)}, u32[]{:S(2)}, u32[]{:S(2)}) %collective-permute-start.2) | collective-permute-done | bytes 24608 | tf_op jit(solution)/shard_map/ppermute | solution.py:422
  11.9 41.1 %collective-permute-start.4 = (bf16[17,96,128]{2,1,0:T(8,128)(2,1)S(1)}, bf16[17,96,128]{2,1,0:T(8,128)(2,1)S(1)}, u32[]{:S(2)}, u32[]{:S(2)}) collective-permute-start(bf16[17,96,128]{2,1,0:T(8,128)(2,1)S(1)} %get-tuple-element.39), channel_id=1, source_target_pairs={{0,1},{1,0},{2,3},{3,2},{4,5},{5,4},{6,7},{7,6},{8,9},{9,8},{10,11... | collective-permute-start | bytes 1253384 | tf_op jit(solution)/shard_map/ppermute | solution.py:434
  53.1 1.3 %collective-permute-start = (bf16[12,96,128]{2,1,0:T(8,128)(2,1)S(1)}, bf16[12,96,128]{2,1,0:T(8,128)(2,1)S(1)}, u32[]{:S(2)}, u32[]{:S(2)}) collective-permute-start(bf16[12,96,128]{2,1,0:T(8,128)(2,1)S(1)} %get-tuple-element.28.m1), channel_id=1, source_target_pairs={{0,16},{16,32},{32,48},{48,64},{64,80},{80,96},{96,112},{112,128},... | collective-permute-start | bytes 884744 | tf_op jit(solution)/shard_map/ppermute | solution.py:423
  54.4 2.0 %collective-permute-start.1 = (bf16[12,96,128]{2,1,0:T(8,128)(2,1)S(1)}, bf16[12,96,128]{2,1,0:T(8,128)(2,1)S(1)}, u32[]{:S(2)}, u32[]{:S(2)}) collective-permute-start(bf16[12,96,128]{2,1,0:T(8,128)(2,1)S(1)} %get-tuple-element.27.after.m2), channel_id=1, source_target_pairs={{16,1},{32,17},{48,33},{64,49},{80,65},{96,81},{112,97},{128,113},... | collective-permute-start | bytes 884744 | tf_op jit(solution)/shard_map/ppermute | solution.py:424
  56.3 3.7 %collective-permute-start.6 = (bf16[96,128]{1,0:T(8,128)(2,1)S(1)}, bf16[96,128]{1,0:T(8,128)(2,1)S(1)}, u32[]{:S(2)}, u32[]{:S(2)}) collective-permute-start(bf16[96,128]{1,0:T(8,128)(2,1)S(1)} %get-tuple-element.40.edge), channel_id=1, source_target_pairs={{16,1},{32,17},{48,33},{64,49},{80,65},{96,81},{112,97},{128,113},... | collective-permute-start | bytes 73736 | tf_op jit(solution)/shard_map/ppermute | solution.py:436
  60.0 1.3 %collective-permute-start.5 = (bf16[96,128]{1,0:T(8,128)(2,1)S(1)}, bf16[96,128]{1,0:T(8,128)(2,1)S(1)}, u32[]{:S(2)}, u32[]{:S(2)}) collective-permute-start(bf16[96,128]{1,0:T(8,128)(2,1)S(1)} %get-tuple-element.40.edge), channel_id=1, source_target_pairs={{0,16},{16,32},{32,48},{48,64},{64,80},{80,96},{96,112},{112,128},... | collective-permute-start | bytes 73736 | tf_op jit(solution)/shard_map/ppermute | solution.py:435
  61.3 1.1 %weights.1 = (bf16[288,864]{1,0:T(8,128)(2,1)S(1)}, bf16[288,864]{1,0:T(8,128)(2,1)S(1)}, bf16[288,864]{1,0:T(8,128)(2,1)S(1)}, bf16[288,864]{1,0:T(8,128)(2,1)S(1)}, f32[4,96,128]{2,1,0:T(8,128)S(1)}) custom-call(bf16[3,288,288]{2,1,0:T(8,128)(2,1)S(1)} %get-tuple-element.30.win, bf16[3,288,288]{2,1,0:T(8,128)(2,1)S(1)} %get-tuple-element.31.wmid, ...), custom_call_target="tpu_custom_call" | custom-call | tf_op jit(solution)/shard_map/weights/pallas_call | solution.py:439
  62.4 0.0 collective-permute-done.z1
  62.4 1.3 %collective-permute-done.1.z2 = bf16[12,96,128]{2,1,0:T(8,128)(2,1)S(1)} collective-permute-done((bf16[12,96,128]{2,1,0:T(8,128)(2,1)S(1)}, bf16[12,96,128]{2,1,0:T(8,128)(2,1)S(1)}, u32[]{:S(2)}, u32[]{:S(2)}) %collective-permute-start.1) | collective-permute-done | bytes 294944 | tf_op jit(solution)/shard_map/ppermute | solution.py:424
  63.7 0.3 lead.1
  64.0 0.0 collective-permute-done.6.e2
  64.0 1.2 %collective-permute-done.5.e1 = bf16[96,128]{1,0:T(8,128)(2,1)S(1)} collective-permute-done((bf16[96,128]{1,0:T(8,128)(2,1)S(1)}, bf16[96,128]{1,0:T(8,128)(2,1)S(1)}, u32[]{:S(2)}, u32[]{:S(2)}) %collective-permute-start.5) | collective-permute-done | bytes 24608 | tf_op jit(solution)/shard_map/ppermute | solution.py:435
  65.3 0.0 collective-permute-done.4.sp
  65.3 4.4 %block.1 = (bf16[6,6,96,128]{3,2,1,0:T(8,128)(2,1)S(1)}, bf16[4,6,96,128]{3,2,1,0:T(8,128)(2,1)S(1)}, bf16[6,4,96,128]{3,2,1,0:T(8,128)(2,1)S(1)}, bf16[6,4,96,1...) custom-call(bf16[6,6,96,128]{3,2,1,0:T(8,128)(2,1)S(1)} %get-tuple-e, ...), custom_call_target="tpu_custom_call", output_to_operand_aliasing={{0}: (0, {}), {1}: (1, {}), {2}: (2, {})} | custom-call | tf_op jit(solution)/shard_map/block/pallas_call | solution.py:461
  69.7 2.0 %collective-permute-start.7 = (f32[2,2,2,96,128]{4,3,2,1,0:T(8,128)S(1)}, f32[2,2,2,96,128]{4,3,2,1,0:T(8,128)S(1)}, u32[]{:S(2)}, u32[]{:S(2)}) collective-permute-start(f32[2,2,2,96,128]{4,3,2,1,0:T(8,128)S(1)} %get-tuple-element.49), channel_id=1, source_target_pairs={{0,1},{1,0},{2,3},{3,2},{4,5},{5,4},{6,7},{7,6},{8,9},{9,8},{10,11... | collective-permute-start | bytes 1179656 | tf_op jit(solution)/shard_map/ppermute | solution.py:477
  71.6 0.9 %own.1.keep = f32[2,2,2,96,128]{4,3,2,1,0:T(8,128)S(1)} custom-call(bf16[12,96,128]{2,1,0:T(8,128)(2,1)S(1)} %get-tuple-element.27.after.m2, bf16[6,4,96,128]{3,2,1,0:T(8,128)(2,1)S(1)} %get-tuple-element.45.M, bf16[6,4,96,128]{3,2,1,0:T(8,128)(2,1)S(1)} %get-tuple-element.46.D, f32[96,128]{1,0:T(8,128)S(1)} %get-tuple-element.47.PA, ...), custom_call_target="tpu_custom_call" | custom-call | tf_op jit(solution)/shard_map/own/pallas_call | solution.py:478
  72.6 0.7 collective-permute-done.7.got
  73.3 0.9 %assemble.1 = (bf16[768,128]{1,0:T(8,128)(2,1)}, f32[768,128]{1,0:T(8,128)}) custom-call(f32[2,2,2,96,128]{4,3,2,1,0:T(8,128)S(1)} %own.1.keep, f32[2,2,2,96,128]{4,3,2,1,0:T(8,128)S(1)} %collective-permute-done.7.got), custom_call_target="tpu_custom_call" | custom-call | tf_op jit(solution)/shard_map/assemble/pallas_call | solution.py:486
  (1 shorter events, 0.0 us)
Async XLA Ops:
  3.3 7.4 %collective-permute-start.3 = (bf16[96,128]{1,0:T(8,128)(2,1)S(1)}, bf16[96,128]{1,0:T(8,128)(2,1)S(1)}, u32[]{:S(2)}, u32[]{:S(2)}) collective-permute-start(bf16[96,128]{1,0:T(8,128)(2,1)S(1)} %get-tuple-element.37), channel_id=1, source_target_pairs={{2,4},{4,2},{6,8},{8,6},{10,12},{12,10},{3,5},{5,3},{7,9},{9,7},{1... | collective-permute-start | bytes 73736 | tf_op jit(solution)/shard_map/ppermute | solution.py:421
  4.0 7.9 %collective-permute-start.2 = (bf16[96,128]{1,0:T(8,128)(2,1)S(1)}, bf16[96,128]{1,0:T(8,128)(2,1)S(1)}, u32[]{:S(2)}, u32[]{:S(2)}) collective-permute-start(bf16[96,128]{1,0:T(8,128)(2,1)S(1)} %get-tuple-element.37), channel_id=1, source_target_pairs={{0,2},{2,0},{4,6},{6,4},{8,10},{10,8},{12,14},{14,12},{1,3},{3,1},... | collective-permute-start | bytes 73736 | tf_op jit(solution)/shard_map/ppermute | solution.py:422
  11.9 53.3 %collective-permute-start.4 = (bf16[17,96,128]{2,1,0:T(8,128)(2,1)S(1)}, bf16[17,96,128]{2,1,0:T(8,128)(2,1)S(1)}, u32[]{:S(2)}, u32[]{:S(2)}) collective-permute-start(bf16[17,96,128]{2,1,0:T(8,128)(2,1)S(1)} %get-tuple-element.39), channel_id=1, source_target_pairs={{0,1},{1,0},{2,3},{3,2},{4,5},{5,4},{6,7},{7,6},{8,9},{9,8},{10,11... | collective-permute-start | bytes 1253384 | tf_op jit(solution)/shard_map/ppermute | solution.py:434
  53.1 9.4 %collective-permute-start = (bf16[12,96,128]{2,1,0:T(8,128)(2,1)S(1)}, bf16[12,96,128]{2,1,0:T(8,128)(2,1)S(1)}, u32[]{:S(2)}, u32[]{:S(2)}) collective-permute-start(bf16[12,96,128]{2,1,0:T(8,128)(2,1)S(1)} %get-tuple-element.28.m1), channel_id=1, source_target_pairs={{0,16},{16,32},{32,48},{48,64},{64,80},{80,96},{96,112},{112,128},... | collective-permute-start | bytes 884744 | tf_op jit(solution)/shard_map/ppermute | solution.py:423
  54.4 9.3 %collective-permute-start.1 = (bf16[12,96,128]{2,1,0:T(8,128)(2,1)S(1)}, bf16[12,96,128]{2,1,0:T(8,128)(2,1)S(1)}, u32[]{:S(2)}, u32[]{:S(2)}) collective-permute-start(bf16[12,96,128]{2,1,0:T(8,128)(2,1)S(1)} %get-tuple-element.27.after.m2), channel_id=1, source_target_pairs={{16,1},{32,17},{48,33},{64,49},{80,65},{96,81},{112,97},{128,113},... | collective-permute-start | bytes 884744 | tf_op jit(solution)/shard_map/ppermute | solution.py:424
  56.3 7.7 %collective-permute-start.6 = (bf16[96,128]{1,0:T(8,128)(2,1)S(1)}, bf16[96,128]{1,0:T(8,128)(2,1)S(1)}, u32[]{:S(2)}, u32[]{:S(2)}) collective-permute-start(bf16[96,128]{1,0:T(8,128)(2,1)S(1)} %get-tuple-element.40.edge), channel_id=1, source_target_pairs={{16,1},{32,17},{48,33},{64,49},{80,65},{96,81},{112,97},{128,113},... | collective-permute-start | bytes 73736 | tf_op jit(solution)/shard_map/ppermute | solution.py:436
  60.0 5.2 %collective-permute-start.5 = (bf16[96,128]{1,0:T(8,128)(2,1)S(1)}, bf16[96,128]{1,0:T(8,128)(2,1)S(1)}, u32[]{:S(2)}, u32[]{:S(2)}) collective-permute-start(bf16[96,128]{1,0:T(8,128)(2,1)S(1)} %get-tuple-element.40.edge), channel_id=1, source_target_pairs={{0,16},{16,32},{32,48},{48,64},{64,80},{80,96},{96,112},{112,128},... | collective-permute-start | bytes 73736 | tf_op jit(solution)/shard_map/ppermute | solution.py:435
  69.7 3.6 %collective-permute-start.7 = (f32[2,2,2,96,128]{4,3,2,1,0:T(8,128)S(1)}, f32[2,2,2,96,128]{4,3,2,1,0:T(8,128)S(1)}, u32[]{:S(2)}, u32[]{:S(2)}) collective-permute-start(f32[2,2,2,96,128]{4,3,2,1,0:T(8,128)S(1)} %get-tuple-element.49), channel_id=1, source_target_pairs={{0,1},{1,0},{2,3},{3,2},{4,5},{5,4},{6,7},{7,6},{8,9},{9,8},{10,11... | collective-permute-start | bytes 1179656 | tf_op jit(solution)/shard_map/ppermute | solution.py:477

commit v6 on v5

--- a/solution.py
+++ b/solution.py
@@ -41,23 +41,32 @@
     return z * s, back
 
 
-def pack_body(
+def fetch_body(
     fr_far, ct_far, ci_far, cm_far, wi_far, wm_far, gi, gm, bi, bm,
-    m1, m2, oc, sw, ed, wi, wm, rows_of, scr, inp, sems,
+    ed, scr, wi, wm, rows_of, inp, sems, others,
 ):
+    channels = ed.shape[0]
+    rows = 4
+    flat = channels * rows
+    quarter = inp.shape[1] // 4
     copies = [
-        pltpu.make_async_copy(source, inp.at[i], sems.at[i])
+        [
+            pltpu.make_async_copy(
+                source.at[pl.ds(k * quarter, quarter)],
+                inp.at[i, pl.ds(k * quarter, quarter)],
+                sems.at[4 * i + k],
+            )
+            for k in range(4)
+        ]
         for i, source in enumerate((fr_far, ct_far, ci_far, cm_far))
     ]
-    copies.append(pltpu.make_async_copy(wi_far, wi, sems.at[4]))
-    copies.append(pltpu.make_async_copy(wm_far, wm, sems.at[5]))
+    rest = [pltpu.make_async_copy(wi_far, wi, others.at[0])]
+    rest.append(pltpu.make_async_copy(wm_far, wm, others.at[1]))
     for k, source in enumerate((gi, gm, bi, bm)):
-        copies.append(pltpu.make_async_copy(source, rows_of.at[k], sems.at[6 + k]))
-    for copy in copies:
-        copy.start()
-    channels = m1.shape[1]
-    rows = 4
-    flat = channels * rows
+        rest.append(pltpu.make_async_copy(source, rows_of.at[k], others.at[2 + k]))
+    for group in copies + [rest]:
+        for copy in group:
+            copy.start()
     ta = lax.axis_index("ta")
     starts = [(0, 0), (0, flat), (1, 0), (1, flat), (2, ta * flat), (3, ta * flat)]
     starts += [(2, (1 - ta) * flat), (3, (1 - ta) * flat)]
@@ -69,37 +78,34 @@
     edges = jnp.zeros((channels, 128), f32)
     for s, (array, start) in enumerate(starts):
         if s in (0, 2, 4, 5):
-            copies[array].wait()
+            for copy in copies[array]:
+                copy.wait()
         scr[s] = inp[array, pl.ds(start, flat), :].astype(f32)
     for s in range(6):
         tiles = [scr[s, pl.ds(r, channels, stride=rows), :].astype(bf16) for r in range(rows)]
         part = jnp.dot(jnp.concatenate(tiles, axis=1), chosen, preferred_element_type=f32)
         edges = edges + (pltpu.roll(part, 4 * rows * s, 1) if s else part)
-
-        @pl.when(ta == 0)
-        def _():
-            for i in range(2):
-                m1[2 * s + i] = tiles[2 + i]
-                m2[2 * s + i] = tiles[i]
-                if s < 4:
-                    sw[2 * s + i] = tiles[2 + i]
-                    sw[8 + 2 * s + i] = tiles[i]
-
-        @pl.when(ta == 1)
-        def _():
-            for i in range(2):
-                m1[2 * s + i] = tiles[i]
-                m2[2 * s + i] = tiles[2 + i]
-                if s < 4:
-                    sw[2 * s + i] = tiles[i]
-                    sw[8 + 2 * s + i] = tiles[2 + i]
-
+    ed[...] = edges.astype(bf16)
+    for copy in rest:
+        copy.wait()
+
+
+def pack_body(scr, m1, m2, oc, sw):
+    channels = m1.shape[1]
+    ta = lax.axis_index("ta")
+    tile_of = lambda s, r: scr[s, pl.ds(r, channels, stride=4), :].astype(bf16)
+    for s in range(6):
+        for i in range(2):
+            far_half = tile_of(s, 2 - 2 * ta + i)
+            own_half = tile_of(s, 2 * ta + i)
+            m1[2 * s + i] = far_half
+            m2[2 * s + i] = own_half
+            if s < 4:
+                sw[2 * s + i] = far_half
+                sw[8 + 2 * s + i] = own_half
     for s in range(2):
-        for r in range(rows):
-            oc[s, r] = scr[6 + s, pl.ds(r, channels, stride=rows), :].astype(bf16)
-    ed[...] = edges.astype(bf16)
-    for copy in copies[4:]:
-        copy.wait()
+        for r in range(4):
+            oc[s, r] = tile_of(6 + s, r)
 
 
 def merge_body(first, second, sw_in, sw, edge_out):
@@ -380,27 +386,24 @@
     limit = lambda mib: pltpu.CompilerParams(vmem_limit_bytes=mib << 20)
     row = lambda v: v.reshape(1, c)
     taps = lambda w: w.reshape(3, 3 * c, 3 * c)
-    m1, m2, oc, sw, ed, wi, wm, rows = pl.pallas_call(
-        pack_body,
+    ed, scr, wi, wm, rows = pl.pallas_call(
+        fetch_body,
         in_specs=[HB] * 10,
-        out_specs=(VM,) * 8,
+        out_specs=(VM,) * 5,
         out_shape=(
-            pltpu.VMEM((12,) + tile, bf16),
-            pltpu.VMEM((12,) + tile, bf16),
-            pltpu.VMEM((2, 4) + tile, bf16),
-            pltpu.VMEM((17,) + tile, bf16),
             pltpu.VMEM(tile, bf16),
+            pltpu.VMEM((8, c * height, width), f32),
             pltpu.VMEM((3, 3 * c, 3 * c), bf16),
             pltpu.VMEM((3, 3 * c, 3 * c), bf16),
             pltpu.VMEM((4, 1, c), f32),
         ),
         scratch_shapes=[
-            pltpu.VMEM((8, c * height, width), f32),
             pltpu.VMEM((4, n * c * height, width), bf16),
-            pltpu.SemaphoreType.DMA((10,)),
+            pltpu.SemaphoreType.DMA((16,)),
+            pltpu.SemaphoreType.DMA((6,)),
         ],
-        compiler_params=limit(8),
-        name="pack",
+        compiler_params=limit(6),
+        name="fetch",
     )(
         *far(
             flat(frames), flat(cotangent), flat(cache_in), flat(cache_mid),
@@ -408,6 +411,19 @@
             row(gain_in), row(gain_mid), row(bias_in), row(bias_mid),
         )
     )
+    m1, m2, oc, sw = pl.pallas_call(
+        pack_body,
+        in_specs=[VM],
+        out_specs=(VM,) * 4,
+        out_shape=(
+            pltpu.VMEM((12,) + tile, bf16),
+            pltpu.VMEM((12,) + tile, bf16),
+            pltpu.VMEM((2, 4) + tile, bf16),
+            pltpu.VMEM((17,) + tile, bf16),
+        ),
+        compiler_params=limit(4),
+        name="pack",
+    )(*near(scr))
 
     wide = lax.axis_size("wa")
     high = lax.axis_size("ha")

time: 74.5 us -> 74.1 us (level)
    pallas_call x1 -> x2, Pallas kernels: 2.65 us -> 2.28 us  [the longest x1 2.14 us: per_device(): pl.pallas_call(fetch_body, in_specs=[HB] * 10, out_specs=(VM,) * 5, out_s...]
where the time goes in v6:
time: 74.1 us; the launch traced here: 73.8 us
  starting transfers between devices  58.8 us (79%)
  Pallas kernels  9.92 us (13%)
  waiting for transfers between devices  4.3 us (6%)
  between operations  0.77 us (1%)
    ppermute x1, starting transfers between devices, per_device(): sp = lax.ppermute(sw, 'ta', [(0, 1), (1, 0)])  41.2 us
    ppermute x1, starting transfers between devices, per_device(): first = lax.ppermute(ed, 'wa', pairs(0))  6.73 us
    pallas_call x1, Pallas kernels, per_device(): pl.pallas_call(main_body, in_specs=[VM] * 12, out_specs=(VM,) * 7, out_sh...  4.4 us
    ppermute x1, starting transfers between devices, per_device(): e2 = lax.ppermute(edge, ('ha', 'ta'), two)  3.67 us
    pallas_call x1, Pallas kernels, per_device(): pl.pallas_call(fetch_body, in_specs=[HB] * 10, out_specs=(VM,) * 5, out_s...  2.14 us
    ppermute x1, starting transfers between devices, per_device(): z2 = lax.ppermute(m2, ('ha', 'ta'), two)  1.95 us
    ppermute x1, starting transfers between devices, per_device(): got = lax.ppermute(send, 'ta', [(0, 1), (1, 0)])  1.95 us
  transfers between devices with their start and end apart: 8, of which 4 were waited for; matrix products, arithmetic and copies ran while one was open for 0% of the time, Pallas kernels for 3%

profile of v6, /device:TPU:65, one launch (start us, length us, event | category | flops | bytes accessed | tf_op | source)
XLA Modules:
  0.0 73.8 jit_solution(11999468547363895938)
XLA Ops:
  0.6 2.1 %fetch.1 = (bf16[96,128]{1,0:T(8,128)(2,1)S(1)}, f32[8,384,128]{2,1,0:T(8,128)S(1)}, bf16[3,288,288]{2,1,0:T(8,128)(2,1)S(1)}, bf16[3,288,288]{2,1,0:T(8,128)(2,1)S(1)}, f32[4,1,96]{2,1,0:T(1,128)S(1)}) custom-call(bf16[768,128]{1,0:T(8,128)(2,1)} %bitcast.14, bf16[768,128]{1,0:T(8,128)(2,1)} %bitcast.15, bf16[768,128]{1,0:T(8,128)(2,1)} %bitcast.16, ...), custom_call_target="tpu_custom_call" | custom-call | tf_op jit(solution)/shard_map/fetch/pallas_call | solution.py:389
  2.8 0.7 collective-permute-start.3
  3.4 6.7 %collective-permute-start.2 = (bf16[96,128]{1,0:T(8,128)(2,1)S(1)}, bf16[96,128]{1,0:T(8,128)(2,1)S(1)}, u32[]{:S(2)}, u32[]{:S(2)}) collective-permute-start(bf16[96,128]{1,0:T(8,128)(2,1)S(1)} %get-tuple-element.39), channel_id=1, source_target_pairs={{0,2},{2,0},{4,6},{6,4},{8,10},{10,8},{12,14},{14,12},{1,3},{3,1},... | collective-permute-start | bytes 73736 | tf_op jit(solution)/shard_map/ppermute | solution.py:438
  10.2 0.1 pack.1
  10.3 0.0 collective-permute-done.3.second
  10.3 1.0 %collective-permute-done.2.first = bf16[96,128]{1,0:T(8,128)(2,1)S(1)} collective-permute-done((bf16[96,128]{1,0:T(8,128)(2,1)S(1)}, bf16[96,128]{1,0:T(8,128)(2,1)S(1)}, u32[]{:S(2)}, u32[]{:S(2)}) %collective-permute-start.2) | collective-permute-done | bytes 24608 | tf_op jit(solution)/shard_map/ppermute | solution.py:438
  11.4 41.2 %collective-permute-start.4 = (bf16[17,96,128]{2,1,0:T(8,128)(2,1)S(1)}, bf16[17,96,128]{2,1,0:T(8,128)(2,1)S(1)}, u32[]{:S(2)}, u32[]{:S(2)}) collective-permute-start(bf16[17,96,128]{2,1,0:T(8,128)(2,1)S(1)} %get-tuple-element.41), channel_id=1, source_target_pairs={{0,1},{1,0},{2,3},{3,2},{4,5},{5,4},{6,7},{7,6},{8,9},{9,8},{10,11... | collective-permute-start | bytes 1253384 | tf_op jit(solution)/shard_map/ppermute | solution.py:450
  52.6 1.3 %collective-permute-start = (bf16[12,96,128]{2,1,0:T(8,128)(2,1)S(1)}, bf16[12,96,128]{2,1,0:T(8,128)(2,1)S(1)}, u32[]{:S(2)}, u32[]{:S(2)}) collective-permute-start(bf16[12,96,128]{2,1,0:T(8,128)(2,1)S(1)} %get-tuple-element.30.m1), channel_id=1, source_target_pairs={{0,16},{16,32},{32,48},{48,64},{64,80},{80,96},{96,112},{112,128},... | collective-permute-start | bytes 884744 | tf_op jit(solution)/shard_map/ppermute | solution.py:439
  53.9 2.0 %collective-permute-start.1 = (bf16[12,96,128]{2,1,0:T(8,128)(2,1)S(1)}, bf16[12,96,128]{2,1,0:T(8,128)(2,1)S(1)}, u32[]{:S(2)}, u32[]{:S(2)}) collective-permute-start(bf16[12,96,128]{2,1,0:T(8,128)(2,1)S(1)} %get-tuple-element.29.after.m2), channel_id=1, source_target_pairs={{16,1},{32,17},{48,33},{64,49},{80,65},{96,81},{112,97},{128,113},... | collective-permute-start | bytes 884744 | tf_op jit(solution)/shard_map/ppermute | solution.py:440
  55.9 3.7 %collective-permute-start.6 = (bf16[96,128]{1,0:T(8,128)(2,1)S(1)}, bf16[96,128]{1,0:T(8,128)(2,1)S(1)}, u32[]{:S(2)}, u32[]{:S(2)}) collective-permute-start(bf16[96,128]{1,0:T(8,128)(2,1)S(1)} %get-tuple-element.42.edge), channel_id=1, source_target_pairs={{16,1},{32,17},{48,33},{64,49},{80,65},{96,81},{112,97},{128,113},... | collective-permute-start | bytes 73736 | tf_op jit(solution)/shard_map/ppermute | solution.py:452
  59.5 1.3 %collective-permute-start.5 = (bf16[96,128]{1,0:T(8,128)(2,1)S(1)}, bf16[96,128]{1,0:T(8,128)(2,1)S(1)}, u32[]{:S(2)}, u32[]{:S(2)}) collective-permute-start(bf16[96,128]{1,0:T(8,128)(2,1)S(1)} %get-tuple-element.42.edge), channel_id=1, source_target_pairs={{0,16},{16,32},{32,48},{48,64},{64,80},{80,96},{96,112},{112,128},... | collective-permute-start | bytes 73736 | tf_op jit(solution)/shard_map/ppermute | solution.py:451
  60.9 1.1 %weights.1 = (bf16[288,864]{1,0:T(8,128)(2,1)S(1)}, bf16[288,864]{1,0:T(8,128)(2,1)S(1)}, bf16[288,864]{1,0:T(8,128)(2,1)S(1)}, bf16[288,864]{1,0:T(8,128)(2,1)S(1)}, f32[4,96,128]{2,1,0:T(8,128)S(1)}) custom-call(bf16[3,288,288]{2,1,0:T(8,128)(2,1)S(1)} %get-tuple-element.32.win, bf16[3,288,288]{2,1,0:T(8,128)(2,1)S(1)} %get-tuple-element.33.wmid, ...), custom_call_target="tpu_custom_call" | custom-call | tf_op jit(solution)/shard_map/weights/pallas_call | solution.py:455
  61.9 0.0 collective-permute-done.z1
  62.0 1.3 %collective-permute-done.1.z2 = bf16[12,96,128]{2,1,0:T(8,128)(2,1)S(1)} collective-permute-done((bf16[12,96,128]{2,1,0:T(8,128)(2,1)S(1)}, bf16[12,96,128]{2,1,0:T(8,128)(2,1)S(1)}, u32[]{:S(2)}, u32[]{:S(2)}) %collective-permute-start.1) | collective-permute-done | bytes 294944 | tf_op jit(solution)/shard_map/ppermute | solution.py:440
  63.3 0.3 lead.1
  63.6 0.0 collective-permute-done.6.e2
  63.6 1.2 %collective-permute-done.5.e1 = bf16[96,128]{1,0:T(8,128)(2,1)S(1)} collective-permute-done((bf16[96,128]{1,0:T(8,128)(2,1)S(1)}, bf16[96,128]{1,0:T(8,128)(2,1)S(1)}, u32[]{:S(2)}, u32[]{:S(2)}) %collective-permute-start.5) | collective-permute-done | bytes 24608 | tf_op jit(solution)/shard_map/ppermute | solution.py:451
  64.8 0.0 collective-permute-done.4.sp
  64.8 4.4 %block.1 = (bf16[6,6,96,128]{3,2,1,0:T(8,128)(2,1)S(1)}, bf16[4,6,96,128]{3,2,1,0:T(8,128)(2,1)S(1)}, bf16[6,4,96,128]{3,2,1,0:T(8,128)(2,1)S(1)}, bf16[6,4,96,1...) custom-call(bf16[6,6,96,128]{3,2,1,0:T(8,128)(2,1)S(1)} %get-tuple-e, ...), custom_call_target="tpu_custom_call", output_to_operand_aliasing={{0}: (0, {}), {1}: (1, {}), {2}: (2, {})} | custom-call | tf_op jit(solution)/shard_map/block/pallas_call | solution.py:477
  69.2 2.0 %collective-permute-start.7 = (f32[2,2,2,96,128]{4,3,2,1,0:T(8,128)S(1)}, f32[2,2,2,96,128]{4,3,2,1,0:T(8,128)S(1)}, u32[]{:S(2)}, u32[]{:S(2)}) collective-permute-start(f32[2,2,2,96,128]{4,3,2,1,0:T(8,128)S(1)} %get-tuple-element.51), channel_id=1, source_target_pairs={{0,1},{1,0},{2,3},{3,2},{4,5},{5,4},{6,7},{7,6},{8,9},{9,8},{10,11... | collective-permute-start | bytes 1179656 | tf_op jit(solution)/shard_map/ppermute | solution.py:493
  71.2 0.9 %own.1.keep = f32[2,2,2,96,128]{4,3,2,1,0:T(8,128)S(1)} custom-call(bf16[12,96,128]{2,1,0:T(8,128)(2,1)S(1)} %get-tuple-element.29.after.m2, bf16[6,4,96,128]{3,2,1,0:T(8,128)(2,1)S(1)} %get-tuple-element.47.M, bf16[6,4,96,128]{3,2,1,0:T(8,128)(2,1)S(1)} %get-tuple-element.48.D, f32[96,128]{1,0:T(8,128)S(1)} %get-tuple-element.49.PA, ...), custom_call_target="tpu_custom_call" | custom-call | tf_op jit(solution)/shard_map/own/pallas_call | solution.py:494
  72.1 0.7 %collective-permute-done.7.got = f32[2,2,2,96,128]{4,3,2,1,0:T(8,128)S(1)} collective-permute-done((f32[2,2,2,96,128]{4,3,2,1,0:T(8,128)S(1)}, f32[2,2,2,96,128]{4,3,2,1,0:T(8,128)S(1)}, u32[]{:S(2)}, u32[]{:S(2)}) %collective-permute-start.7) | collective-permute-done | bytes 393248 | tf_op jit(solution)/shard_map/ppermute | solution.py:493
  72.9 0.9 %assemble.1 = (bf16[768,128]{1,0:T(8,128)(2,1)}, f32[768,128]{1,0:T(8,128)}) custom-call(f32[2,2,2,96,128]{4,3,2,1,0:T(8,128)S(1)} %own.1.keep, f32[2,2,2,96,128]{4,3,2,1,0:T(8,128)S(1)} %collective-permute-done.7.got), custom_call_target="tpu_custom_call" | custom-call | tf_op jit(solution)/shard_map/assemble/pallas_call | solution.py:502
  (1 shorter events, 0.0 us)
Async XLA Ops:
  2.8 7.5 %collective-permute-start.3 = (bf16[96,128]{1,0:T(8,128)(2,1)S(1)}, bf16[96,128]{1,0:T(8,128)(2,1)S(1)}, u32[]{:S(2)}, u32[]{:S(2)}) collective-permute-start(bf16[96,128]{1,0:T(8,128)(2,1)S(1)} %get-tuple-element.39), channel_id=1, source_target_pairs={{2,4},{4,2},{6,8},{8,6},{10,12},{12,10},{3,5},{5,3},{7,9},{9,7},{1... | collective-permute-start | bytes 73736 | tf_op jit(solution)/shard_map/ppermute | solution.py:437
  3.4 7.9 %collective-permute-start.2 = (bf16[96,128]{1,0:T(8,128)(2,1)S(1)}, bf16[96,128]{1,0:T(8,128)(2,1)S(1)}, u32[]{:S(2)}, u32[]{:S(2)}) collective-permute-start(bf16[96,128]{1,0:T(8,128)(2,1)S(1)} %get-tuple-element.39), channel_id=1, source_target_pairs={{0,2},{2,0},{4,6},{6,4},{8,10},{10,8},{12,14},{14,12},{1,3},{3,1},... | collective-permute-start | bytes 73736 | tf_op jit(solution)/shard_map/ppermute | solution.py:438
  11.4 53.4 %collective-permute-start.4 = (bf16[17,96,128]{2,1,0:T(8,128)(2,1)S(1)}, bf16[17,96,128]{2,1,0:T(8,128)(2,1)S(1)}, u32[]{:S(2)}, u32[]{:S(2)}) collective-permute-start(bf16[17,96,128]{2,1,0:T(8,128)(2,1)S(1)} %get-tuple-element.41), channel_id=1, source_target_pairs={{0,1},{1,0},{2,3},{3,2},{4,5},{5,4},{6,7},{7,6},{8,9},{9,8},{10,11... | collective-permute-start | bytes 1253384 | tf_op jit(solution)/shard_map/ppermute | solution.py:450
  52.6 9.4 %collective-permute-start = (bf16[12,96,128]{2,1,0:T(8,128)(2,1)S(1)}, bf16[12,96,128]{2,1,0:T(8,128)(2,1)S(1)}, u32[]{:S(2)}, u32[]{:S(2)}) collective-permute-start(bf16[12,96,128]{2,1,0:T(8,128)(2,1)S(1)} %get-tuple-element.30.m1), channel_id=1, source_target_pairs={{0,16},{16,32},{32,48},{48,64},{64,80},{80,96},{96,112},{112,128},... | collective-permute-start | bytes 884744 | tf_op jit(solution)/shard_map/ppermute | solution.py:439
  53.9 9.3 %collective-permute-start.1 = (bf16[12,96,128]{2,1,0:T(8,128)(2,1)S(1)}, bf16[12,96,128]{2,1,0:T(8,128)(2,1)S(1)}, u32[]{:S(2)}, u32[]{:S(2)}) collective-permute-start(bf16[12,96,128]{2,1,0:T(8,128)(2,1)S(1)} %get-tuple-element.29.after.m2), channel_id=1, source_target_pairs={{16,1},{32,17},{48,33},{64,49},{80,65},{96,81},{112,97},{128,113},... | collective-permute-start | bytes 884744 | tf_op jit(solution)/shard_map/ppermute | solution.py:440
  55.9 7.7 %collective-permute-start.6 = (bf16[96,128]{1,0:T(8,128)(2,1)S(1)}, bf16[96,128]{1,0:T(8,128)(2,1)S(1)}, u32[]{:S(2)}, u32[]{:S(2)}) collective-permute-start(bf16[96,128]{1,0:T(8,128)(2,1)S(1)} %get-tuple-element.42.edge), channel_id=1, source_target_pairs={{16,1},{32,17},{48,33},{64,49},{80,65},{96,81},{112,97},{128,113},... | collective-permute-start | bytes 73736 | tf_op jit(solution)/shard_map/ppermute | solution.py:452
  59.5 5.2 %collective-permute-start.5 = (bf16[96,128]{1,0:T(8,128)(2,1)S(1)}, bf16[96,128]{1,0:T(8,128)(2,1)S(1)}, u32[]{:S(2)}, u32[]{:S(2)}) collective-permute-start(bf16[96,128]{1,0:T(8,128)(2,1)S(1)} %get-tuple-element.42.edge), channel_id=1, source_target_pairs={{0,16},{16,32},{32,48},{48,64},{64,80},{80,96},{96,112},{112,128},... | collective-permute-start | bytes 73736 | tf_op jit(solution)/shard_map/ppermute | solution.py:451
  69.2 3.6 %collective-permute-start.7 = (f32[2,2,2,96,128]{4,3,2,1,0:T(8,128)S(1)}, f32[2,2,2,96,128]{4,3,2,1,0:T(8,128)S(1)}, u32[]{:S(2)}, u32[]{:S(2)}) collective-permute-start(f32[2,2,2,96,128]{4,3,2,1,0:T(8,128)S(1)} %get-tuple-element.51), channel_id=1, source_target_pairs={{0,1},{1,0},{2,3},{3,2},{4,5},{5,4},{6,7},{7,6},{8,9},{9,8},{10,11... | collective-permute-start | bytes 1179656 | tf_op jit(solution)/shard_map/ppermute | solution.py:493

commit v7 on v6

--- a/solution.py
+++ b/solution.py
@@ -42,8 +42,8 @@
 
 
 def fetch_body(
-    fr_far, ct_far, ci_far, cm_far, wi_far, wm_far, gi, gm, bi, bm,
-    ed, scr, wi, wm, rows_of, inp, sems, others,
+    fr_far, ct_far, ci_far, cm_far, gi, gm, bi, bm,
+    ed, scr, rows_of, inp, sems, others,
 ):
     channels = ed.shape[0]
     rows = 4
@@ -60,10 +60,10 @@
         ]
         for i, source in enumerate((fr_far, ct_far, ci_far, cm_far))
     ]
-    rest = [pltpu.make_async_copy(wi_far, wi, others.at[0])]
-    rest.append(pltpu.make_async_copy(wm_far, wm, others.at[1]))
-    for k, source in enumerate((gi, gm, bi, bm)):
-        rest.append(pltpu.make_async_copy(source, rows_of.at[k], others.at[2 + k]))
+    rest = [
+        pltpu.make_async_copy(source, rows_of.at[k], others.at[k])
+        for k, source in enumerate((gi, gm, bi, bm))
+    ]
     for group in copies + [rest]:
         for copy in group:
             copy.start()
@@ -90,7 +90,7 @@
         copy.wait()
 
 
-def pack_body(scr, m1, m2, oc, sw):
+def pack_body(scr, early_weight, m1, m2, oc, sw):
     channels = m1.shape[1]
     ta = lax.axis_index("ta")
     tile_of = lambda s, r: scr[s, pl.ds(r, channels, stride=4), :].astype(bf16)
@@ -117,8 +117,9 @@
     sw[16] = edge
 
 
-def weights_body(win, wmid, rows, after, w1, w2, w1f, w2f, vec):
-    channels = w1.shape[0] // 3
+def weights_body(win, wmid, rows, after, ws, w2, w1f, vec):
+    channels = w2.shape[0] // 3
+    w1, w2f = ws.at[0], ws.at[1]
     for src, plain, turned in zip((win, wmid), (w1, w2), (w1f, w2f)):
         plain[...] = jnp.concatenate([src[a].astype(f32) for a in range(3)], axis=1).astype(bf16)
         for b in range(3):
@@ -127,7 +128,7 @@
                 for a in range(3)
             ]
             blocks = [
-                flat[a][(2 - t) * channels : (3 - t) * channels] for t in range(3) for a in range(3)
+                flat[a][(2 - t) * channels : (3 - t) * channels] for a in range(3) for t in range(3)
             ]
             turned[b * channels : (b + 1) * channels, :] = jnp.concatenate(blocks, axis=1).astype(
                 bf16
@@ -141,11 +142,30 @@
     return ta, 1 - ta, 4 * ta, 4 - 4 * ta
 
 
-time_first = [(t, a) for t in range(3) for a in range(3)]
-row_first = [(t, a) for a in range(3) for t in range(3)]
-
-
-def lead_body(m1, m2, oc, z1, z2, vec, A, C, M):
+taps_order = [(t, a) for a in range(3) for t in range(3)]
+
+
+def product(weights, ref, lead, f, row):
+    cols = [
+        jnp.concatenate([ref[lead + (f + t, row + i + a)] for t, a in taps_order], axis=0)
+        for i in range(2)
+    ]
+    return jnp.dot(weights, jnp.concatenate(cols, axis=1), preferred_element_type=f32)
+
+
+def parts(p):
+    n = p.shape[0] // 3
+    return [[p[b * n : (b + 1) * n, 128 * i : 128 * (i + 1)] for b in range(3)] for i in range(2)]
+
+
+def partial_products(ws, AC, PV, which):
+    for k in range(2):
+        for pair in range(2):
+            PV[which, k, pair] = product(ws[which], AC, (which,), 2 * which + k, 2 * pair)
+
+
+def lead_body(m1, m2, oc, z1, z2, vec, ws, AC, M, PV):
+    A, C = AC.at[0], AC.at[1]
     ta, other, zb, mb = offsets()
     gin = vec[0]
     for i in range(2):
@@ -172,17 +192,10 @@
         A[other, r + 2 - 2 * ta] = oc[0, r]
     for k in range(3):
         M[other, k + 1 - ta] = oc[1, k + ta]
-
-
-def products(w, ref, f, row, order):
-    channels = ref.shape[2]
-    cols = [jnp.concatenate([ref[f + t, row + i + a] for t, a in order], axis=0) for i in range(2)]
-    weights = w[:, : len(order) * channels]
-    p = jnp.dot(weights, jnp.concatenate(cols, axis=1), preferred_element_type=f32)
-    return [
-        [p[b * channels : (b + 1) * channels, 128 * i : 128 * (i + 1)] for b in range(3)]
-        for i in range(2)
-    ]
+    for e in range(6):
+        C[4, e] = jnp.zeros(m1.shape[1:], bf16)
+        C[5, e] = jnp.zeros(m1.shape[1:], bf16)
+    partial_products(ws, AC, PV, ta)
 
 
 def shifted_sum(p, edge_ref, q):
@@ -194,7 +207,7 @@
 
 
 def second_products(f, M, D, w2, w1f):
-    return products(w2, M, f, 0, row_first), products(w1f, D, f, 0, time_first)
+    return parts(product(w2[...], M, (), f, 0)), parts(product(w1f[...], D, (), f, 0))
 
 
 def second_layer(f, mine, slot, out, both, PA, PC, vec):
@@ -217,9 +230,10 @@
 
 
 def main_body(
-    A_in, C_in, M_in, sp, edge, e1, e2, w1, w2, w1f, w2f, vec,
-    A, C, M, D, PA, PC, send, EA, EC,
+    AC_in, M_in, PV_in, sp, edge, e1, e2, ws, w2, w1f, vec,
+    AC, M, PV, D, PA, PC, send, EA, EC,
 ):
+    A, C, w1, w2f = AC.at[0], AC.at[1], ws.at[0], ws.at[1]
     channels = sp.shape[1]
     tile = (channels, 128)
     ta, other, _, mb = offsets()
@@ -269,9 +283,9 @@
         out += placed(par, slot, 32 * other, 0, 4, 2 - 2 * ta)
         return out + placed(zp, slot, 32 * other, 2 - 2 * ta, 2, 4 * ta)
 
-    def edge_products(w, low, high, order, last=False):
+    def edge_products(w, low, high, last=False):
         pieces = []
-        for t, a in order:
+        for t, a in taps_order:
             s = 32 * t + 4 * a
             if s == 0:
                 pieces.append(low.astype(bf16))
@@ -296,26 +310,26 @@
         edge_ref[...] = edge_ref[...] + jnp.where(here, moved, 0.0)
 
     def first_products(f, pair):
-        pf = products(w1, A, f, 2 * pair, row_first)
-        return pf, products(w2f, C, f, 2 * pair, time_first[: 3 * (4 - f)])
-
-    early = [first_products(0, pair) for pair in range(2)]
+        forward = PV[0, f, pair] if f < 2 else product(w1[...], A, (), f, 2 * pair)
+        gradient = PV[1, f - 2, pair] if f > 1 else product(w2f[...], C, (), f, 2 * pair)
+        return parts(forward), parts(gradient)
+
+    partial_products(ws, AC, PV, other)
     act_edges = pltpu.roll(act(group(0), gin), 64, 1)
     cin_edges = caches(4)
     across, own_part = edge_products(
-        w1, jnp.where(lane < 64, cin_edges, act_edges), jnp.where(lane < 64, act_edges, 0.0),
-        row_first,
+        w1, jnp.where(lane < 64, cin_edges, act_edges), jnp.where(lane < 64, act_edges, 0.0)
     )
     PA[...] = across
     EA[...] = own_part
-    across, own_part = edge_products(w2f, group(2), None, time_first)
+    across, own_part = edge_products(w2f, group(2), None)
     PC[...] = across
     EC[...] = own_part
     cmid_edges = pltpu.roll(caches(5), 124, 1)
 
     def first_layer(f):
         for pair in range(2):
-            pf, pb = early[pair] if f == 0 else first_products(f, pair)
+            pf, pb = first_products(f, pair)
             for i in range(2):
                 e = 2 * pair + i
                 q = f * 32 + e * 4
@@ -346,8 +360,8 @@
     d = jnp.where(inside, d, 0.0).astype(bf16).astype(f32)
     a = pltpu.roll(a, 64, 1)
     low = jnp.where(lane < 64, cmid_edges, a)
-    PA[...] = edge_products(w2, low, jnp.where(lane < 64, a, 0.0), row_first, last=True)
-    PC[...] = edge_products(w1f, d, None, time_first, last=True)
+    PA[...] = edge_products(w2, low, jnp.where(lane < 64, a, 0.0), last=True)
+    PC[...] = edge_products(w1f, d, None, last=True)
 
     for slot in range(2):
         second_layer(2 * other + slot, sp, slot, send, late[slot], PA, PC, vec)
@@ -386,34 +400,32 @@
     limit = lambda mib: pltpu.CompilerParams(vmem_limit_bytes=mib << 20)
     row = lambda v: v.reshape(1, c)
     taps = lambda w: w.reshape(3, 3 * c, 3 * c)
-    ed, scr, wi, wm, rows = pl.pallas_call(
+    ed, scr, rows = pl.pallas_call(
         fetch_body,
-        in_specs=[HB] * 10,
-        out_specs=(VM,) * 5,
+        in_specs=[HB] * 8,
+        out_specs=(VM,) * 3,
         out_shape=(
             pltpu.VMEM(tile, bf16),
             pltpu.VMEM((8, c * height, width), f32),
-            pltpu.VMEM((3, 3 * c, 3 * c), bf16),
-            pltpu.VMEM((3, 3 * c, 3 * c), bf16),
             pltpu.VMEM((4, 1, c), f32),
         ),
         scratch_shapes=[
             pltpu.VMEM((4, n * c * height, width), bf16),
             pltpu.SemaphoreType.DMA((16,)),
-            pltpu.SemaphoreType.DMA((6,)),
+            pltpu.SemaphoreType.DMA((4,)),
         ],
         compiler_params=limit(6),
         name="fetch",
     )(
         *far(
             flat(frames), flat(cotangent), flat(cache_in), flat(cache_mid),
-            taps(weight_in), taps(weight_mid),
             row(gain_in), row(gain_mid), row(bias_in), row(bias_mid),
         )
     )
+    wi, wm = near(taps(weight_in), taps(weight_mid))
     m1, m2, oc, sw = pl.pallas_call(
         pack_body,
-        in_specs=[VM],
+        in_specs=[VM] * 2,
         out_specs=(VM,) * 4,
         out_shape=(
             pltpu.VMEM((12,) + tile, bf16),
@@ -423,7 +435,7 @@
         ),
         compiler_params=limit(4),
         name="pack",
-    )(*near(scr))
+    )(*near(scr, wi))
 
     wide = lax.axis_size("wa")
     high = lax.axis_size("ha")
@@ -452,31 +464,36 @@
     e2 = lax.ppermute(edge, ("ha", "ta"), two)
 
     matrix = pltpu.VMEM((3 * c, 9 * c), bf16)
-    w1, w2, w1f, w2f, vec = pl.pallas_call(
+    ws, w2, w1f, vec = pl.pallas_call(
         weights_body,
         in_specs=[VM] * 3 + [pl.BlockSpec(memory_space=pl.ANY)],
-        out_specs=(VM,) * 5,
-        out_shape=(matrix,) * 4 + (pltpu.VMEM((4,) + tile, f32),),
+        out_specs=(VM,) * 4,
+        out_shape=(
+            pltpu.VMEM((2, 3 * c, 9 * c), bf16),
+            matrix,
+            matrix,
+            pltpu.VMEM((4,) + tile, f32),
+        ),
         compiler_params=limit(8),
         name="weights",
     )(*near(wi, wm, rows), m2)
     staged = (
-        pltpu.VMEM((6, 6) + tile, bf16),
-        pltpu.VMEM((4, 6) + tile, bf16),
+        pltpu.VMEM((2, 6, 6) + tile, bf16),
         pltpu.VMEM((6, 4) + tile, bf16),
+        pltpu.VMEM((2, 2, 2, 3 * c, 2 * width), f32),
     )
-    A, C, M = pl.pallas_call(
+    AC, M, PV = pl.pallas_call(
         lead_body,
-        in_specs=[VM] * 6,
+        in_specs=[VM] * 7,
         out_specs=(VM,) * 3,
         out_shape=staged,
         compiler_params=limit(8),
         name="lead",
-    )(*near(m1, m2, oc, z1, z2, vec))
+    )(*near(m1, m2, oc, z1, z2, vec, ws))
     half = pltpu.VMEM((2, 2, 2) + tile, f32)
-    A, C, M, D, PA, PC, send = pl.pallas_call(
+    AC, M, PV, D, PA, PC, send = pl.pallas_call(
         main_body,
-        in_specs=[VM] * 12,
+        in_specs=[VM] * 11,
         out_specs=(VM,) * 7,
         out_shape=staged
         + (
@@ -489,7 +506,7 @@
         input_output_aliases={0: 0, 1: 1, 2: 2},
         compiler_params=limit(12),
         name="block",
-    )(*near(A, C, M, sp, edge, e1, e2, w1, w2, w1f, w2f, vec))
+    )(*near(AC, M, PV, sp, edge, e1, e2, ws, w2, w1f, vec))
     got = lax.ppermute(send, "ta", [(0, 1), (1, 0)])
     keep = pl.pallas_call(
         own_body,

time: 74.1 us -> 73.5 us (level)
  waiting for transfers between devices: 4.3 us -> 2.45 us
  local copies, waits for them, and re-layouts: 0 us -> 1.1 us
    unnamed x0 -> x6, local copies, waits for them, and re-layouts: none -> 1.1 us
    ppermute x1, waiting for transfers between devices: 1.05 us -> 0.01 us  [per_device(): first = lax.ppermute(ed, 'wa', pairs(0))]
    ppermute x1, waiting for transfers between devices: 1.21 us -> 0.43 us  [per_device(): e1 = lax.ppermute(edge, ('ha', 'ta'), one)]
  transfers between devices with their start and end apart: 8 -> 8, of which waited for: 4 -> 3; matrix products, arithmetic and copies ran while one was open for 0% -> 0% of each run, Pallas kernels for 3% -> 4%
where the time goes in v7:
time: 73.5 us; the launch traced here: 73.2 us
  starting transfers between devices  58.7 us (80%)
  Pallas kernels  10.1 us (14%)
  waiting for transfers between devices  2.45 us (3%)
  local copies, waits for them, and re-layouts  1.1 us (1%)
  between operations  0.81 us (1%)
    ppermute x1, starting transfers between devices, per_device(): sp = lax.ppermute(sw, 'ta', [(0, 1), (1, 0)])  41.1 us
    ppermute x1, starting transfers between devices, per_device(): first = lax.ppermute(ed, 'wa', pairs(0))  6.73 us
    pallas_call x1, Pallas kernels, per_device(): pl.pallas_call(main_body, in_specs=[VM] * 11, out_specs=(VM,) * 7, out_sh...  4.15 us
    ppermute x1, starting transfers between devices, per_device(): e2 = lax.ppermute(edge, ('ha', 'ta'), two)  3.67 us
    ppermute x1, starting transfers between devices, per_device(): got = lax.ppermute(send, 'ta', [(0, 1), (1, 0)])  1.95 us
    ppermute x1, starting transfers between devices, per_device(): z2 = lax.ppermute(m2, ('ha', 'ta'), two)  1.95 us
    pallas_call x1, Pallas kernels, per_device(): pl.pallas_call(fetch_body, in_specs=[HB] * 8, out_specs=(VM,) * 3, out_sh...  1.77 us
  transfers between devices with their start and end apart: 8, of which 3 were waited for; matrix products, arithmetic and copies ran while one was open for 0% of the time, Pallas kernels for 4%

profile of v7, /device:TPU:65, one launch (start us, length us, event | category | flops | bytes accessed | tf_op | source)
XLA Modules:
  0.0 73.2 jit_solution(3697127801068390926)
XLA Ops:
  0.6 0.0 copy-start.1
  0.6 1.8 %fetch.1 = (bf16[96,128]{1,0:T(8,128)(2,1)S(1)}, f32[8,384,128]{2,1,0:T(8,128)S(1)}, f32[4,1,96]{2,1,0:T(1,128)S(1)}) custom-call(bf16[768,128]{1,0:T(8,128)(2,1)} %bitcast.15, bf16[768,128]{1,0:T(8,128)(2,1)} %bitcast.16, bf16[768,128]{1,0:T(8,128)(2,1)} %bitcast.17, bf16[768,128]{1,0:T(8,128)(2,1)} %bitcast.18, f32[1,96]{1,0:T(1,128)} %bitcast.19, ...), custom_call_target="tpu_custom_call" | custom-call | tf_op jit(solution)/shard_map/fetch/pallas_call | solution.py:403
  2.4 0.7 collective-permute-start.3
  3.1 6.7 %collective-permute-start.2 = (bf16[96,128]{1,0:T(8,128)(2,1)S(1)}, bf16[96,128]{1,0:T(8,128)(2,1)S(1)}, u32[]{:S(2)}, u32[]{:S(2)}) collective-permute-start(bf16[96,128]{1,0:T(8,128)(2,1)S(1)} %get-tuple-element.35), channel_id=1, source_target_pairs={{0,2},{2,0},{4,6},{6,4},{8,10},{10,8},{12,14},{14,12},{1,3},{3,1},... | collective-permute-start | bytes 73736 | tf_op jit(solution)/shard_map/ppermute | solution.py:450
  9.8 0.0 copy-start
  9.8 1.1 %copy-done = bf16[3,3,96,288]{3,2,1,0:T(8,128)(2,1)S(1)} copy-done((bf16[3,3,96,288]{3,2,1,0:T(8,128)(2,1)S(1)}, bf16[3,3,96,288]{3,2,1,0:T(8,128)(2,1)}, u32[]{:S(2)}) %copy-start) | copy-done | bytes 497688
  10.9 0.0 copy-start.2
  10.9 0.1 pack.1
  11.1 0.0 collective-permute-done.3.second
  11.1 0.0 collective-permute-done.2.first
  11.1 41.1 %collective-permute-start.4 = (bf16[17,96,128]{2,1,0:T(8,128)(2,1)S(1)}, bf16[17,96,128]{2,1,0:T(8,128)(2,1)S(1)}, u32[]{:S(2)}, u32[]{:S(2)}) collective-permute-start(bf16[17,96,128]{2,1,0:T(8,128)(2,1)S(1)} %get-tuple-element.37), channel_id=1, source_target_pairs={{0,1},{1,0},{2,3},{3,2},{4,5},{5,4},{6,7},{7,6},{8,9},{9,8},{10,11... | collective-permute-start | bytes 1253384 | tf_op jit(solution)/shard_map/ppermute | solution.py:462
  52.2 1.3 %collective-permute-start = (bf16[12,96,128]{2,1,0:T(8,128)(2,1)S(1)}, bf16[12,96,128]{2,1,0:T(8,128)(2,1)S(1)}, u32[]{:S(2)}, u32[]{:S(2)}) collective-permute-start(bf16[12,96,128]{2,1,0:T(8,128)(2,1)S(1)} %get-tuple-element.27.m1), channel_id=1, source_target_pairs={{0,16},{16,32},{32,48},{48,64},{64,80},{80,96},{96,112},{112,128},... | collective-permute-start | bytes 884744 | tf_op jit(solution)/shard_map/ppermute | solution.py:451
  53.6 2.0 %collective-permute-start.1 = (bf16[12,96,128]{2,1,0:T(8,128)(2,1)S(1)}, bf16[12,96,128]{2,1,0:T(8,128)(2,1)S(1)}, u32[]{:S(2)}, u32[]{:S(2)}) collective-permute-start(bf16[12,96,128]{2,1,0:T(8,128)(2,1)S(1)} %get-tuple-element.26.after.m2), channel_id=1, source_target_pairs={{16,1},{32,17},{48,33},{64,49},{80,65},{96,81},{112,97},{128,113},... | collective-permute-start | bytes 884744 | tf_op jit(solution)/shard_map/ppermute | solution.py:452
  55.5 3.7 %collective-permute-start.6 = (bf16[96,128]{1,0:T(8,128)(2,1)S(1)}, bf16[96,128]{1,0:T(8,128)(2,1)S(1)}, u32[]{:S(2)}, u32[]{:S(2)}) collective-permute-start(bf16[96,128]{1,0:T(8,128)(2,1)S(1)} %get-tuple-element.38.edge), channel_id=1, source_target_pairs={{16,1},{32,17},{48,33},{64,49},{80,65},{96,81},{112,97},{128,113},... | collective-permute-start | bytes 73736 | tf_op jit(solution)/shard_map/ppermute | solution.py:464
  59.2 1.3 %collective-permute-start.5 = (bf16[96,128]{1,0:T(8,128)(2,1)S(1)}, bf16[96,128]{1,0:T(8,128)(2,1)S(1)}, u32[]{:S(2)}, u32[]{:S(2)}) collective-permute-start(bf16[96,128]{1,0:T(8,128)(2,1)S(1)} %get-tuple-element.38.edge), channel_id=1, source_target_pairs={{0,16},{16,32},{32,48},{48,64},{64,80},{80,96},{96,112},{112,128},... | collective-permute-start | bytes 73736 | tf_op jit(solution)/shard_map/ppermute | solution.py:463
  60.5 0.0 copy-done.1
  60.5 0.0 copy-done.2
  60.5 1.1 %weights.1 = (bf16[2,288,864]{2,1,0:T(8,128)(2,1)S(1)}, bf16[288,864]{1,0:T(8,128)(2,1)S(1)}, bf16[288,864]{1,0:T(8,128)(2,1)S(1)}, f32[4,96,128]{2,1,0:T(8,128)S(1)}) custom-call(bf16[3,288,288]{2,1,0:T(8,128)(2,1)S(1)} %bitcast.13, bf16[3,288,288]{2,1,0:T(8,128)(2,1)S(1)} %bitcast.14, f32[4,1,96]{2,1,0:T(1,128)S(1)} %get-tuple-element.29.rows, ...), custom_call_target="tpu_custom_call" | custom-call | tf_op jit(solution)/shard_map/weights/pallas_call | solution.py:467
  61.6 0.0 collective-permute-done.z1
  61.6 1.3 %collective-permute-done.1.z2 = bf16[12,96,128]{2,1,0:T(8,128)(2,1)S(1)} collective-permute-done((bf16[12,96,128]{2,1,0:T(8,128)(2,1)S(1)}, bf16[12,96,128]{2,1,0:T(8,128)(2,1)S(1)}, u32[]{:S(2)}, u32[]{:S(2)}) %collective-permute-start.1) | collective-permute-done | bytes 294944 | tf_op jit(solution)/shard_map/ppermute | solution.py:452
  62.9 1.1 %lead.1 = (bf16[2,6,6,96,128]{4,3,2,1,0:T(8,128)(2,1)S(1)}, bf16[6,4,96,128]{3,2,1,0:T(8,128)(2,1)S(1)}, f32[2,2,2,288,256]{4,3,2,1,0:T(8,128)S(1)}) custom-call(bf16[12,96,128]{2,1,0:T(8,128)(2,1)S(1)} %get-tuple-element.27.m1, bf16[12,96,128]{2,1,0:T(8,128)(2,1)S(1)} %get-tuple-element.26.after.m2, bf16[2,4,96,128]{3,2,1,0:T(8,128)(2,1)S(1)} %get-tuple-element.28.oc, ...), custom_call_target="tpu_custom_call" | custom-call | tf_op jit(solution)/shard_map/lead/pallas_call | solution.py:485
  64.0 0.0 collective-permute-done.6.e2
  64.0 0.4 collective-permute-done.5.e1
  64.4 0.0 collective-permute-done.4.sp
  64.4 4.2 %block.1 = (bf16[2,6,6,96,128]{4,3,2,1,0:T(8,128)(2,1)S(1)}, bf16[6,4,96,128]{3,2,1,0:T(8,128)(2,1)S(1)}, f32[2,2,2,288,256]{4,3,2,1,0:T(8,128)S(1)}, bf16[6,4,9...) custom-call(bf16[2,6,6,96,128]{4,3,2,1,0:T(8,128)(2,1)S(1)} %get-tup, ...), custom_call_target="tpu_custom_call", output_to_operand_aliasing={{0}: (0, {}), {1}: (1, {}), {2}: (2, {})} | custom-call | tf_op jit(solution)/shard_map/block/pallas_call | solution.py:494
  68.6 2.0 %collective-permute-start.7 = (f32[2,2,2,96,128]{4,3,2,1,0:T(8,128)S(1)}, f32[2,2,2,96,128]{4,3,2,1,0:T(8,128)S(1)}, u32[]{:S(2)}, u32[]{:S(2)}) collective-permute-start(f32[2,2,2,96,128]{4,3,2,1,0:T(8,128)S(1)} %get-tuple-element.45), channel_id=1, source_target_pairs={{0,1},{1,0},{2,3},{3,2},{4,5},{5,4},{6,7},{7,6},{8,9},{9,8},{10,11... | collective-permute-start | bytes 1179656 | tf_op jit(solution)/shard_map/ppermute | solution.py:510
  70.6 0.9 %own.1.keep = f32[2,2,2,96,128]{4,3,2,1,0:T(8,128)S(1)} custom-call(bf16[12,96,128]{2,1,0:T(8,128)(2,1)S(1)} %get-tuple-element.26.after.m2, bf16[6,4,96,128]{3,2,1,0:T(8,128)(2,1)S(1)} %get-tuple-element.41.M, bf16[6,4,96,128]{3,2,1,0:T(8,128)(2,1)S(1)} %get-tuple-element.42.D, f32[96,128]{1,0:T(8,128)S(1)} %get-tuple-element.43.PA, ...), custom_call_target="tpu_custom_call" | custom-call | tf_op jit(solution)/shard_map/own/pallas_call | solution.py:511
  71.5 0.7 %collective-permute-done.7.got = f32[2,2,2,96,128]{4,3,2,1,0:T(8,128)S(1)} collective-permute-done((f32[2,2,2,96,128]{4,3,2,1,0:T(8,128)S(1)}, f32[2,2,2,96,128]{4,3,2,1,0:T(8,128)S(1)}, u32[]{:S(2)}, u32[]{:S(2)}) %collective-permute-start.7) | collective-permute-done | bytes 393248 | tf_op jit(solution)/shard_map/ppermute | solution.py:510
  72.3 0.9 %assemble.1 = (bf16[768,128]{1,0:T(8,128)(2,1)}, f32[768,128]{1,0:T(8,128)}) custom-call(f32[2,2,2,96,128]{4,3,2,1,0:T(8,128)S(1)} %own.1.keep, f32[2,2,2,96,128]{4,3,2,1,0:T(8,128)S(1)} %collective-permute-done.7.got), custom_call_target="tpu_custom_call" | custom-call | tf_op jit(solution)/shard_map/assemble/pallas_call | solution.py:519
  (1 shorter events, 0.0 us)
Async XLA Ops:
  0.6 59.9 %copy-start.1 = (bf16[3,3,96,288]{3,2,1,0:T(8,128)(2,1)S(1)}, bf16[3,3,96,288]{3,2,1,0:T(8,128)(2,1)}, u32[]{:S(2)}) copy-start(bf16[3,3,96,288]{3,2,1,0:T(8,128)(2,1)} %param.15) | copy-start | bytes 1492996
  2.4 8.6 %collective-permute-start.3 = (bf16[96,128]{1,0:T(8,128)(2,1)S(1)}, bf16[96,128]{1,0:T(8,128)(2,1)S(1)}, u32[]{:S(2)}, u32[]{:S(2)}) collective-permute-start(bf16[96,128]{1,0:T(8,128)(2,1)S(1)} %get-tuple-element.35), channel_id=1, source_target_pairs={{2,4},{4,2},{6,8},{8,6},{10,12},{12,10},{3,5},{5,3},{7,9},{9,7},{1... | collective-permute-start | bytes 73736 | tf_op jit(solution)/shard_map/ppermute | solution.py:449
  3.1 8.0 %collective-permute-start.2 = (bf16[96,128]{1,0:T(8,128)(2,1)S(1)}, bf16[96,128]{1,0:T(8,128)(2,1)S(1)}, u32[]{:S(2)}, u32[]{:S(2)}) collective-permute-start(bf16[96,128]{1,0:T(8,128)(2,1)S(1)} %get-tuple-element.35), channel_id=1, source_target_pairs={{0,2},{2,0},{4,6},{6,4},{8,10},{10,8},{12,14},{14,12},{1,3},{3,1},... | collective-permute-start | bytes 73736 | tf_op jit(solution)/shard_map/ppermute | solution.py:450
  9.8 1.1 %copy-start = (bf16[3,3,96,288]{3,2,1,0:T(8,128)(2,1)S(1)}, bf16[3,3,96,288]{3,2,1,0:T(8,128)(2,1)}, u32[]{:S(2)}) copy-start(bf16[3,3,96,288]{3,2,1,0:T(8,128)(2,1)} %param.15) | copy-start | bytes 1492996
  10.9 49.6 %copy-start.2 = (bf16[3,3,96,288]{3,2,1,0:T(8,128)(2,1)S(1)}, bf16[3,3,96,288]{3,2,1,0:T(8,128)(2,1)}, u32[]{:S(2)}) copy-start(bf16[3,3,96,288]{3,2,1,0:T(8,128)(2,1)} %param.17) | copy-start | bytes 1492996
  11.1 53.3 %collective-permute-start.4 = (bf16[17,96,128]{2,1,0:T(8,128)(2,1)S(1)}, bf16[17,96,128]{2,1,0:T(8,128)(2,1)S(1)}, u32[]{:S(2)}, u32[]{:S(2)}) collective-permute-start(bf16[17,96,128]{2,1,0:T(8,128)(2,1)S(1)} %get-tuple-element.37), channel_id=1, source_target_pairs={{0,1},{1,0},{2,3},{3,2},{4,5},{5,4},{6,7},{7,6},{8,9},{9,8},{10,11... | collective-permute-start | bytes 1253384 | tf_op jit(solution)/shard_map/ppermute | solution.py:462
  52.2 9.4 %collective-permute-start = (bf16[12,96,128]{2,1,0:T(8,128)(2,1)S(1)}, bf16[12,96,128]{2,1,0:T(8,128)(2,1)S(1)}, u32[]{:S(2)}, u32[]{:S(2)}) collective-permute-start(bf16[12,96,128]{2,1,0:T(8,128)(2,1)S(1)} %get-tuple-element.27.m1), channel_id=1, source_target_pairs={{0,16},{16,32},{32,48},{48,64},{64,80},{80,96},{96,112},{112,128},... | collective-permute-start | bytes 884744 | tf_op jit(solution)/shard_map/ppermute | solution.py:451
  53.6 9.3 %collective-permute-start.1 = (bf16[12,96,128]{2,1,0:T(8,128)(2,1)S(1)}, bf16[12,96,128]{2,1,0:T(8,128)(2,1)S(1)}, u32[]{:S(2)}, u32[]{:S(2)}) collective-permute-start(bf16[12,96,128]{2,1,0:T(8,128)(2,1)S(1)} %get-tuple-element.26.after.m2), channel_id=1, source_target_pairs={{16,1},{32,17},{48,33},{64,49},{80,65},{96,81},{112,97},{128,113},... | collective-permute-start | bytes 884744 | tf_op jit(solution)/shard_map/ppermute | solution.py:452
  55.5 8.5 %collective-permute-start.6 = (bf16[96,128]{1,0:T(8,128)(2,1)S(1)}, bf16[96,128]{1,0:T(8,128)(2,1)S(1)}, u32[]{:S(2)}, u32[]{:S(2)}) collective-permute-start(bf16[96,128]{1,0:T(8,128)(2,1)S(1)} %get-tuple-element.38.edge), channel_id=1, source_target_pairs={{16,1},{32,17},{48,33},{64,49},{80,65},{96,81},{112,97},{128,113},... | collective-permute-start | bytes 73736 | tf_op jit(solution)/shard_map/ppermute | solution.py:464
  59.2 5.2 %collective-permute-start.5 = (bf16[96,128]{1,0:T(8,128)(2,1)S(1)}, bf16[96,128]{1,0:T(8,128)(2,1)S(1)}, u32[]{:S(2)}, u32[]{:S(2)}) collective-permute-start(bf16[96,128]{1,0:T(8,128)(2,1)S(1)} %get-tuple-element.38.edge), channel_id=1, source_target_pairs={{0,16},{16,32},{32,48},{48,64},{64,80},{80,96},{96,112},{112,128},... | collective-permute-start | bytes 73736 | tf_op jit(solution)/shard_map/ppermute | solution.py:463
  68.6 3.6 %collective-permute-start.7 = (f32[2,2,2,96,128]{4,3,2,1,0:T(8,128)S(1)}, f32[2,2,2,96,128]{4,3,2,1,0:T(8,128)S(1)}, u32[]{:S(2)}, u32[]{:S(2)}) collective-permute-start(f32[2,2,2,96,128]{4,3,2,1,0:T(8,128)S(1)} %get-tuple-element.45), channel_id=1, source_target_pairs={{0,1},{1,0},{2,3},{3,2},{4,5},{5,4},{6,7},{7,6},{8,9},{9,8},{10,11... | collective-permute-start | bytes 1179656 | tf_op jit(solution)/shard_map/ppermute | solution.py:510

commit v8 on v7

--- a/solution.py
+++ b/solution.py
@@ -42,55 +42,61 @@
 
 
 def fetch_body(
-    fr_far, ct_far, ci_far, cm_far, gi, gm, bi, bm,
-    ed, scr, rows_of, inp, sems, others,
+    fr_far, ct_far, ci_far, cm_far, wm_far, gi, gm, bi, bm,
+    ed, scr, wm, rows_of, inp, sems, others,
 ):
     channels = ed.shape[0]
     rows = 4
     flat = channels * rows
-    quarter = inp.shape[1] // 4
+    half = flat // 2
+    ta = lax.axis_index("ta")
+    own = pl.multiple_of(ta * flat, flat)
+    other = pl.multiple_of((1 - ta) * flat, flat)
+    starts = [(fr_far, 0), (fr_far, flat), (ct_far, 0), (ct_far, flat)]
+    starts += [(ci_far, own), (cm_far, own), (ci_far, other), (cm_far, other)]
     copies = [
         [
             pltpu.make_async_copy(
-                source.at[pl.ds(k * quarter, quarter)],
-                inp.at[i, pl.ds(k * quarter, quarter)],
-                sems.at[4 * i + k],
+                source.at[pl.ds(start + k * half, half)],
+                inp.at[s, pl.ds(k * half, half)],
+                sems.at[2 * s + k],
             )
-            for k in range(4)
+            for k in range(2)
         ]
-        for i, source in enumerate((fr_far, ct_far, ci_far, cm_far))
+        for s, (source, start) in enumerate(starts)
     ]
-    rest = [
+    rest = [pltpu.make_async_copy(wm_far, wm, others.at[4])]
+    rest += [
         pltpu.make_async_copy(source, rows_of.at[k], others.at[k])
         for k, source in enumerate((gi, gm, bi, bm))
     ]
     for group in copies + [rest]:
         for copy in group:
             copy.start()
-    ta = lax.axis_index("ta")
-    starts = [(0, 0), (0, flat), (1, 0), (1, flat), (2, ta * flat), (3, ta * flat)]
-    starts += [(2, (1 - ta) * flat), (3, (1 - ta) * flat)]
     k = lax.broadcasted_iota(jnp.int32, (rows * 128, 128), 0)
     j = lanes_of((rows * 128, 128))
     column = jnp.where(j % 4 == 0, 1, jnp.where(j % 4 == 1, 0, jnp.where(j % 4 == 2, 127, 126)))
     chosen = (j < 4 * rows) & (k // 128 == j // 4) & (k % 128 == column)
     chosen = jnp.where(chosen, 1.0, 0.0).astype(bf16)
     edges = jnp.zeros((channels, 128), f32)
-    for s, (array, start) in enumerate(starts):
-        if s in (0, 2, 4, 5):
-            for copy in copies[array]:
-                copy.wait()
-        scr[s] = inp[array, pl.ds(start, flat), :].astype(f32)
+    for s in range(6):
+        for copy in copies[s]:
+            copy.wait()
+        scr[s] = inp[s].astype(f32)
     for s in range(6):
         tiles = [scr[s, pl.ds(r, channels, stride=rows), :].astype(bf16) for r in range(rows)]
         part = jnp.dot(jnp.concatenate(tiles, axis=1), chosen, preferred_element_type=f32)
         edges = edges + (pltpu.roll(part, 4 * rows * s, 1) if s else part)
     ed[...] = edges.astype(bf16)
+    for s in (6, 7):
+        for copy in copies[s]:
+            copy.wait()
+        scr[s] = inp[s].astype(f32)
     for copy in rest:
         copy.wait()
 
 
-def pack_body(scr, early_weight, m1, m2, oc, sw):
+def pack_body(scr, m1, m2, oc, sw):
     channels = m1.shape[1]
     ta = lax.axis_index("ta")
     tile_of = lambda s, r: scr[s, pl.ds(r, channels, stride=4), :].astype(bf16)
@@ -210,23 +216,23 @@
     return parts(product(w2[...], M, (), f, 0)), parts(product(w1f[...], D, (), f, 0))
 
 
-def second_layer(f, mine, slot, out, both, PA, PC, vec):
+def second_layer(f, mine, slot, out, both, PA, PC, vec, whole):
     pf, pb = both
     for i in range(2):
         q = f * 32 + i * 4
         frame = mine[2 * slot + i].astype(f32)
-        cot = mine[4 + 2 * slot + i].astype(f32)
+        cot = mine[4 + 2 * slot + i].astype(f32) if whole else None
         decoded = frame + (shifted_sum(pf[i], PA, q) + vec[3])
-        out[0, slot, i] = decoded.astype(bf16).astype(f32)
+        out[0, slot, i] = decoded.astype(bf16).astype(out.dtype)
         _, back = act_and_back(frame, vec[0], shifted_sum(pb[i], PC, q))
-        out[1, slot, i] = cot + back
+        out[1, slot, i] = cot + back if whole else back.astype(out.dtype)
 
 
 def own_body(m2, M, D, PA, PC, w2, w1f, vec, keep):
     ta = lax.axis_index("ta")
     for slot in range(2):
         f = 2 * ta + slot
-        second_layer(f, m2, slot, keep, second_products(f, M, D, w2, w1f), PA, PC, vec)
+        second_layer(f, m2, slot, keep, second_products(f, M, D, w2, w1f), PA, PC, vec, True)
 
 
 def main_body(
@@ -364,29 +370,21 @@
     PC[...] = edge_products(w1f, d, None, last=True)
 
     for slot in range(2):
-        second_layer(2 * other + slot, sp, slot, send, late[slot], PA, PC, vec)
-
-
-def assemble_body(keep, got, dec, grad, scr):
-    channels = got.shape[3]
+        second_layer(2 * other + slot, sp, slot, send, late[slot], PA, PC, vec, False)
+
+
+def assemble_body(keep, got, m1, dec, grad, scr):
+    channels = keep.shape[3]
     flat = 4 * channels
     ta = lax.axis_index("ta")
-
-    def write(at_keep, at_got):
-        for f in range(2):
-            for i in range(2):
-                for src, r in ((keep, at_keep + i), (got, at_got + i)):
-                    scr[pl.ds(f * flat + r, channels, stride=4), :] = src[0, f, i]
-                    grad[pl.ds(f * flat + r, channels, stride=4), :] = src[1, f, i]
-
-    @pl.when(ta == 0)
-    def _():
-        write(0, 2)
-
-    @pl.when(ta == 1)
-    def _():
-        write(2, 0)
-
+    for f in range(2):
+        for i in range(2):
+            mine = pl.ds(f * flat + 2 * ta + i, channels, stride=4)
+            yours = pl.ds(f * flat + 2 - 2 * ta + i, channels, stride=4)
+            scr[mine, :] = keep[0, f, i]
+            grad[mine, :] = keep[1, f, i]
+            scr[yours, :] = got[0, f, i].astype(f32)
+            grad[yours, :] = m1[4 + 2 * f + i].astype(f32) + got[1, f, i].astype(f32)
     dec[...] = scr[...].astype(bf16)
 
 
@@ -400,32 +398,32 @@
     limit = lambda mib: pltpu.CompilerParams(vmem_limit_bytes=mib << 20)
     row = lambda v: v.reshape(1, c)
     taps = lambda w: w.reshape(3, 3 * c, 3 * c)
-    ed, scr, rows = pl.pallas_call(
+    ed, scr, wm, rows = pl.pallas_call(
         fetch_body,
-        in_specs=[HB] * 8,
-        out_specs=(VM,) * 3,
+        in_specs=[HB] * 9,
+        out_specs=(VM,) * 4,
         out_shape=(
             pltpu.VMEM(tile, bf16),
             pltpu.VMEM((8, c * height, width), f32),
+            pltpu.VMEM((3, 3 * c, 3 * c), bf16),
             pltpu.VMEM((4, 1, c), f32),
         ),
         scratch_shapes=[
-            pltpu.VMEM((4, n * c * height, width), bf16),
+            pltpu.VMEM((8, c * height, width), bf16),
             pltpu.SemaphoreType.DMA((16,)),
-            pltpu.SemaphoreType.DMA((4,)),
+            pltpu.SemaphoreType.DMA((5,)),
         ],
         compiler_params=limit(6),
         name="fetch",
     )(
         *far(
             flat(frames), flat(cotangent), flat(cache_in), flat(cache_mid),
-            row(gain_in), row(gain_mid), row(bias_in), row(bias_mid),
+            taps(weight_mid), row(gain_in), row(gain_mid), row(bias_in), row(bias_mid),
         )
     )
-    wi, wm = near(taps(weight_in), taps(weight_mid))
     m1, m2, oc, sw = pl.pallas_call(
         pack_body,
-        in_specs=[VM] * 2,
+        in_specs=[VM],
         out_specs=(VM,) * 4,
         out_shape=(
             pltpu.VMEM((12,) + tile, bf16),
@@ -435,7 +433,7 @@
         ),
         compiler_params=limit(4),
         name="pack",
-    )(*near(scr, wi))
+    )(*near(scr))
 
     wide = lax.axis_size("wa")
     high = lax.axis_size("ha")
@@ -476,7 +474,7 @@
         ),
         compiler_params=limit(8),
         name="weights",
-    )(*near(wi, wm, rows), m2)
+    )(*near(taps(weight_in), wm, rows), m2)
     staged = (
         pltpu.VMEM((2, 6, 6) + tile, bf16),
         pltpu.VMEM((6, 4) + tile, bf16),
@@ -500,7 +498,7 @@
             pltpu.VMEM((6, 4) + tile, bf16),
             pltpu.VMEM(tile, f32),
             pltpu.VMEM(tile, f32),
-            half,
+            pltpu.VMEM((2, 2, 2) + tile, bf16),
         ),
         scratch_shapes=[pltpu.VMEM(tile, f32), pltpu.VMEM(tile, f32)],
         input_output_aliases={0: 0, 1: 1, 2: 2},
@@ -518,7 +516,7 @@
     )(*near(m2, M, D, PA, PC, w2, w1f, vec))
     decoded, grad = pl.pallas_call(
         assemble_body,
-        in_specs=[VM] * 2,
+        in_specs=[VM] * 3,
         out_shape=(
             jax.ShapeDtypeStruct((n * c * height, width), bf16),
             jax.ShapeDtypeStruct((n * c * height, width), f32),
@@ -526,7 +524,7 @@
         scratch_shapes=[pltpu.VMEM((n * c * height, width), f32)],
         compiler_params=limit(8),
         name="assemble",
-    )(*near(keep, got))
+    )(*near(keep, got, m1))
     return decoded.reshape(frames.shape), grad.reshape(frames.shape)
 
 

time: 73.5 us -> 73.3 us (level)
  local copies, waits for them, and re-layouts: 1.1 us -> 0.01 us
  waiting for transfers between devices: 2.45 us -> 3.23 us
    unnamed x6 -> x2, local copies, waits for them, and re-layouts: 1.1 us -> 0.01 us
    ppermute x1, waiting for transfers between devices: 0.01 us -> 1.05 us  [per_device(): first = lax.ppermute(ed, 'wa', pairs(0))]
  transfers between devices with their start and end apart: 8 -> 8, of which waited for: 3 -> 4; matrix products, arithmetic and copies ran while one was open for 0% -> 0% of each run, Pallas kernels for 4% -> 4%
where the time goes in v8:
time: 73.3 us; the launch traced here: 73 us
  starting transfers between devices  58.8 us (80%)
  Pallas kernels  10.2 us (14%)
  waiting for transfers between devices  3.23 us (4%)
  between operations  0.78 us (1%)
    ppermute x1, starting transfers between devices, per_device(): sp = lax.ppermute(sw, 'ta', [(0, 1), (1, 0)])  41.2 us
    ppermute x1, starting transfers between devices, per_device(): first = lax.ppermute(ed, 'wa', pairs(0))  6.73 us
    pallas_call x1, Pallas kernels, per_device(): pl.pallas_call(main_body, in_specs=[VM] * 11, out_specs=(VM,) * 7, out_sh...  4.14 us
    ppermute x1, starting transfers between devices, per_device(): e2 = lax.ppermute(edge, ('ha', 'ta'), two)  3.67 us
    ppermute x1, starting transfers between devices, per_device(): z2 = lax.ppermute(m2, ('ha', 'ta'), two)  1.95 us
    ppermute x1, starting transfers between devices, per_device(): got = lax.ppermute(send, 'ta', [(0, 1), (1, 0)])  1.95 us
    pallas_call x1, Pallas kernels, per_device(): pl.pallas_call(fetch_body, in_specs=[HB] * 9, out_specs=(VM,) * 4, out_sh...  1.9 us
  transfers between devices with their start and end apart: 8, of which 4 were waited for; matrix products, arithmetic and copies ran while one was open for 0% of the time, Pallas kernels for 4%

profile of v8, /device:TPU:65, one launch (start us, length us, event | category | flops | bytes accessed | tf_op | source)
XLA Modules:
  0.0 73.0 jit_solution(14107993726623214291)
XLA Ops:
  0.6 0.0 copy-start
  0.6 1.9 %fetch.1 = (bf16[96,128]{1,0:T(8,128)(2,1)S(1)}, f32[8,384,128]{2,1,0:T(8,128)S(1)}, bf16[3,288,288]{2,1,0:T(8,128)(2,1)S(1)}, f32[4,1,96]{2,1,0:T(1,128)S(1)}) custom-call(bf16[768,128]{1,0:T(8,128)(2,1)} %bitcast.14, bf16[768,128]{1,0:T(8,128)(2,1)} %bitcast.15, bf16[768,128]{1,0:T(8,128)(2,1)} %bitcast.16, bf16[768,128]{1,0:T(8,128)(2,1)} %bitcast.17, ...), custom_call_target="tpu_custom_call" | custom-call | tf_op jit(solution)/shard_map/fetch/pallas_call | solution.py:401
  2.6 0.7 collective-permute-start.3
  3.2 6.7 %collective-permute-start.2 = (bf16[96,128]{1,0:T(8,128)(2,1)S(1)}, bf16[96,128]{1,0:T(8,128)(2,1)S(1)}, u32[]{:S(2)}, u32[]{:S(2)}) collective-permute-start(bf16[96,128]{1,0:T(8,128)(2,1)S(1)} %get-tuple-element.37), channel_id=1, source_target_pairs={{0,2},{2,0},{4,6},{6,4},{8,10},{10,8},{12,14},{14,12},{1,3},{3,1},... | collective-permute-start | bytes 73736 | tf_op jit(solution)/shard_map/ppermute | solution.py:448
  10.0 0.1 pack.1
  10.1 0.0 collective-permute-done.3.second
  10.1 1.0 %collective-permute-done.2.first = bf16[96,128]{1,0:T(8,128)(2,1)S(1)} collective-permute-done((bf16[96,128]{1,0:T(8,128)(2,1)S(1)}, bf16[96,128]{1,0:T(8,128)(2,1)S(1)}, u32[]{:S(2)}, u32[]{:S(2)}) %collective-permute-start.2) | collective-permute-done | bytes 24608 | tf_op jit(solution)/shard_map/ppermute | solution.py:448
  11.2 41.2 %collective-permute-start.4 = (bf16[17,96,128]{2,1,0:T(8,128)(2,1)S(1)}, bf16[17,96,128]{2,1,0:T(8,128)(2,1)S(1)}, u32[]{:S(2)}, u32[]{:S(2)}) collective-permute-start(bf16[17,96,128]{2,1,0:T(8,128)(2,1)S(1)} %get-tuple-element.39), channel_id=1, source_target_pairs={{0,1},{1,0},{2,3},{3,2},{4,5},{5,4},{6,7},{7,6},{8,9},{9,8},{10,11... | collective-permute-start | bytes 1253384 | tf_op jit(solution)/shard_map/ppermute | solution.py:460
  52.4 1.3 %collective-permute-start = (bf16[12,96,128]{2,1,0:T(8,128)(2,1)S(1)}, bf16[12,96,128]{2,1,0:T(8,128)(2,1)S(1)}, u32[]{:S(2)}, u32[]{:S(2)}) collective-permute-start(bf16[12,96,128]{2,1,0:T(8,128)(2,1)S(1)} %get-tuple-element.28.m1), channel_id=1, source_target_pairs={{0,16},{16,32},{32,48},{48,64},{64,80},{80,96},{96,112},{112,128},... | collective-permute-start | bytes 884744 | tf_op jit(solution)/shard_map/ppermute | solution.py:449
  53.7 2.0 %collective-permute-start.1 = (bf16[12,96,128]{2,1,0:T(8,128)(2,1)S(1)}, bf16[12,96,128]{2,1,0:T(8,128)(2,1)S(1)}, u32[]{:S(2)}, u32[]{:S(2)}) collective-permute-start(bf16[12,96,128]{2,1,0:T(8,128)(2,1)S(1)} %get-tuple-element.27.after.m2), channel_id=1, source_target_pairs={{16,1},{32,17},{48,33},{64,49},{80,65},{96,81},{112,97},{128,113},... | collective-permute-start | bytes 884744 | tf_op jit(solution)/shard_map/ppermute | solution.py:450
  55.6 3.7 %collective-permute-start.6 = (bf16[96,128]{1,0:T(8,128)(2,1)S(1)}, bf16[96,128]{1,0:T(8,128)(2,1)S(1)}, u32[]{:S(2)}, u32[]{:S(2)}) collective-permute-start(bf16[96,128]{1,0:T(8,128)(2,1)S(1)} %get-tuple-element.40.edge), channel_id=1, source_target_pairs={{16,1},{32,17},{48,33},{64,49},{80,65},{96,81},{112,97},{128,113},... | collective-permute-start | bytes 73736 | tf_op jit(solution)/shard_map/ppermute | solution.py:462
  59.3 1.3 %collective-permute-start.5 = (bf16[96,128]{1,0:T(8,128)(2,1)S(1)}, bf16[96,128]{1,0:T(8,128)(2,1)S(1)}, u32[]{:S(2)}, u32[]{:S(2)}) collective-permute-start(bf16[96,128]{1,0:T(8,128)(2,1)S(1)} %get-tuple-element.40.edge), channel_id=1, source_target_pairs={{0,16},{16,32},{32,48},{48,64},{64,80},{80,96},{96,112},{112,128},... | collective-permute-start | bytes 73736 | tf_op jit(solution)/shard_map/ppermute | solution.py:461
  60.6 0.0 copy-done
  60.6 1.1 %weights.1 = (bf16[2,288,864]{2,1,0:T(8,128)(2,1)S(1)}, bf16[288,864]{1,0:T(8,128)(2,1)S(1)}, bf16[288,864]{1,0:T(8,128)(2,1)S(1)}, f32[4,96,128]{2,1,0:T(8,128)S(1)}) custom-call(bf16[3,288,288]{2,1,0:T(8,128)(2,1)S(1)} %bitcast.12, bf16[3,288,288]{2,1,0:T(8,128)(2,1)S(1)} %get-tuple-element.30.wmid, f32[4,1,96]{2,1,0:T(1,128)S(1)} %get-tuple-element.31.rows, ...), custom_call_target="tpu_custom_call" | custom-call | tf_op jit(solution)/shard_map/weights/pallas_call | solution.py:465
  61.7 0.0 collective-permute-done.z1
  61.7 1.3 %collective-permute-done.1.z2 = bf16[12,96,128]{2,1,0:T(8,128)(2,1)S(1)} collective-permute-done((bf16[12,96,128]{2,1,0:T(8,128)(2,1)S(1)}, bf16[12,96,128]{2,1,0:T(8,128)(2,1)S(1)}, u32[]{:S(2)}, u32[]{:S(2)}) %collective-permute-start.1) | collective-permute-done | bytes 294944 | tf_op jit(solution)/shard_map/ppermute | solution.py:450
  63.0 1.1 %lead.1 = (bf16[2,6,6,96,128]{4,3,2,1,0:T(8,128)(2,1)S(1)}, bf16[6,4,96,128]{3,2,1,0:T(8,128)(2,1)S(1)}, f32[2,2,2,288,256]{4,3,2,1,0:T(8,128)S(1)}) custom-call(bf16[12,96,128]{2,1,0:T(8,128)(2,1)S(1)} %get-tuple-element.28.m1, bf16[12,96,128]{2,1,0:T(8,128)(2,1)S(1)} %get-tuple-element.27.after.m2, bf16[2,4,96,128]{3,2,1,0:T(8,128)(2,1)S(1)} %get-tuple-element.29.oc, ...), custom_call_target="tpu_custom_call" | custom-call | tf_op jit(solution)/shard_map/lead/pallas_call | solution.py:483
  64.1 0.0 collective-permute-done.6.e2
  64.1 0.4 collective-permute-done.5.e1
  64.6 0.0 collective-permute-done.4.sp
  64.6 4.1 %block.1 = (bf16[2,6,6,96,128]{4,3,2,1,0:T(8,128)(2,1)S(1)}, bf16[6,4,96,128]{3,2,1,0:T(8,128)(2,1)S(1)}, f32[2,2,2,288,256]{4,3,2,1,0:T(8,128)S(1)}, bf16[6,4,9...) custom-call(bf16[2,6,6,96,128]{4,3,2,1,0:T(8,128)(2,1)S(1)} %get-tup, ...), custom_call_target="tpu_custom_call", output_to_operand_aliasing={{0}: (0, {}), {1}: (1, {}), {2}: (2, {})} | custom-call | tf_op jit(solution)/shard_map/block/pallas_call | solution.py:492
  68.7 2.0 %collective-permute-start.7 = (bf16[2,2,2,96,128]{4,3,2,1,0:T(8,128)(2,1)S(1)}, bf16[2,2,2,96,128]{4,3,2,1,0:T(8,128)(2,1)S(1)}, u32[]{:S(2)}, u32[]{:S(2)}) collective-permute-start(bf16[2,2,2,96,128]{4,3,2,1,0:T(8,128)(2,1)S(1)} %get-tuple-element.47), channel_id=1, source_target_pairs={{0,1},{1,0},{2,3},{3,2},{4,5},{5,4},{6,7},{7,6},{8,9},{9,8},{10,11... | collective-permute-start | bytes 589832 | tf_op jit(solution)/shard_map/ppermute | solution.py:508
  70.7 1.0 %own.1.keep = f32[2,2,2,96,128]{4,3,2,1,0:T(8,128)S(1)} custom-call(bf16[12,96,128]{2,1,0:T(8,128)(2,1)S(1)} %get-tuple-element.27.after.m2, bf16[6,4,96,128]{3,2,1,0:T(8,128)(2,1)S(1)} %get-tuple-element.43.M, bf16[6,4,96,128]{3,2,1,0:T(8,128)(2,1)S(1)} %get-tuple-element.44.D, f32[96,128]{1,0:T(8,128)S(1)} %get-tuple-element.45.PA, ...), custom_call_target="tpu_custom_call" | custom-call | tf_op jit(solution)/shard_map/own/pallas_call | solution.py:509
  71.6 0.4 collective-permute-done.7.got
  72.1 0.9 %assemble.1 = (bf16[768,128]{1,0:T(8,128)(2,1)}, f32[768,128]{1,0:T(8,128)}) custom-call(f32[2,2,2,96,128]{4,3,2,1,0:T(8,128)S(1)} %own.1.keep, bf16[2,2,2,96,128]{4,3,2,1,0:T(8,128)(2,1)S(1)} %collective-permute-done.7.got, bf16[12,96,128]{2,1,0:T(8,128)(2,1)S(1)} %get-tuple-element.28.m1), custom_call_target="tpu_custom_call" | custom-call | tf_op jit(solution)/shard_map/assemble/pallas_call | solution.py:517
  (1 shorter events, 0.0 us)
Async XLA Ops:
  0.6 60.0 %copy-start = (bf16[3,3,96,288]{3,2,1,0:T(8,128)(2,1)S(1)}, bf16[3,3,96,288]{3,2,1,0:T(8,128)(2,1)}, u32[]{:S(2)}) copy-start(bf16[3,3,96,288]{3,2,1,0:T(8,128)(2,1)} %param.15) | copy-start | bytes 1492996
  2.6 7.6 %collective-permute-start.3 = (bf16[96,128]{1,0:T(8,128)(2,1)S(1)}, bf16[96,128]{1,0:T(8,128)(2,1)S(1)}, u32[]{:S(2)}, u32[]{:S(2)}) collective-permute-start(bf16[96,128]{1,0:T(8,128)(2,1)S(1)} %get-tuple-element.37), channel_id=1, source_target_pairs={{2,4},{4,2},{6,8},{8,6},{10,12},{12,10},{3,5},{5,3},{7,9},{9,7},{1... | collective-permute-start | bytes 73736 | tf_op jit(solution)/shard_map/ppermute | solution.py:447
  3.2 7.9 %collective-permute-start.2 = (bf16[96,128]{1,0:T(8,128)(2,1)S(1)}, bf16[96,128]{1,0:T(8,128)(2,1)S(1)}, u32[]{:S(2)}, u32[]{:S(2)}) collective-permute-start(bf16[96,128]{1,0:T(8,128)(2,1)S(1)} %get-tuple-element.37), channel_id=1, source_target_pairs={{0,2},{2,0},{4,6},{6,4},{8,10},{10,8},{12,14},{14,12},{1,3},{3,1},... | collective-permute-start | bytes 73736 | tf_op jit(solution)/shard_map/ppermute | solution.py:448
  11.2 53.4 %collective-permute-start.4 = (bf16[17,96,128]{2,1,0:T(8,128)(2,1)S(1)}, bf16[17,96,128]{2,1,0:T(8,128)(2,1)S(1)}, u32[]{:S(2)}, u32[]{:S(2)}) collective-permute-start(bf16[17,96,128]{2,1,0:T(8,128)(2,1)S(1)} %get-tuple-element.39), channel_id=1, source_target_pairs={{0,1},{1,0},{2,3},{3,2},{4,5},{5,4},{6,7},{7,6},{8,9},{9,8},{10,11... | collective-permute-start | bytes 1253384 | tf_op jit(solution)/shard_map/ppermute | solution.py:460
  52.4 9.4 %collective-permute-start = (bf16[12,96,128]{2,1,0:T(8,128)(2,1)S(1)}, bf16[12,96,128]{2,1,0:T(8,128)(2,1)S(1)}, u32[]{:S(2)}, u32[]{:S(2)}) collective-permute-start(bf16[12,96,128]{2,1,0:T(8,128)(2,1)S(1)} %get-tuple-element.28.m1), channel_id=1, source_target_pairs={{0,16},{16,32},{32,48},{48,64},{64,80},{80,96},{96,112},{112,128},... | collective-permute-start | bytes 884744 | tf_op jit(solution)/shard_map/ppermute | solution.py:449
  53.7 9.3 %collective-permute-start.1 = (bf16[12,96,128]{2,1,0:T(8,128)(2,1)S(1)}, bf16[12,96,128]{2,1,0:T(8,128)(2,1)S(1)}, u32[]{:S(2)}, u32[]{:S(2)}) collective-permute-start(bf16[12,96,128]{2,1,0:T(8,128)(2,1)S(1)} %get-tuple-element.27.after.m2), channel_id=1, source_target_pairs={{16,1},{32,17},{48,33},{64,49},{80,65},{96,81},{112,97},{128,113},... | collective-permute-start | bytes 884744 | tf_op jit(solution)/shard_map/ppermute | solution.py:450
  55.6 8.5 %collective-permute-start.6 = (bf16[96,128]{1,0:T(8,128)(2,1)S(1)}, bf16[96,128]{1,0:T(8,128)(2,1)S(1)}, u32[]{:S(2)}, u32[]{:S(2)}) collective-permute-start(bf16[96,128]{1,0:T(8,128)(2,1)S(1)} %get-tuple-element.40.edge), channel_id=1, source_target_pairs={{16,1},{32,17},{48,33},{64,49},{80,65},{96,81},{112,97},{128,113},... | collective-permute-start | bytes 73736 | tf_op jit(solution)/shard_map/ppermute | solution.py:462
  59.3 5.2 %collective-permute-start.5 = (bf16[96,128]{1,0:T(8,128)(2,1)S(1)}, bf16[96,128]{1,0:T(8,128)(2,1)S(1)}, u32[]{:S(2)}, u32[]{:S(2)}) collective-permute-start(bf16[96,128]{1,0:T(8,128)(2,1)S(1)} %get-tuple-element.40.edge), channel_id=1, source_target_pairs={{0,16},{16,32},{32,48},{48,64},{64,80},{80,96},{96,112},{112,128},... | collective-permute-start | bytes 73736 | tf_op jit(solution)/shard_map/ppermute | solution.py:461
  68.7 3.4 %collective-permute-start.7 = (bf16[2,2,2,96,128]{4,3,2,1,0:T(8,128)(2,1)S(1)}, bf16[2,2,2,96,128]{4,3,2,1,0:T(8,128)(2,1)S(1)}, u32[]{:S(2)}, u32[]{:S(2)}) collective-permute-start(bf16[2,2,2,96,128]{4,3,2,1,0:T(8,128)(2,1)S(1)} %get-tuple-element.47), channel_id=1, source_target_pairs={{0,1},{1,0},{2,3},{3,2},{4,5},{5,4},{6,7},{7,6},{8,9},{9,8},{10,11... | collective-permute-start | bytes 589832 | tf_op jit(solution)/shard_map/ppermute | solution.py:508

commit v9 on v8

--- a/solution.py
+++ b/solution.py
@@ -134,7 +134,7 @@
                 for a in range(3)
             ]
             blocks = [
-                flat[a][(2 - t) * channels : (3 - t) * channels] for a in range(3) for t in range(3)
+                flat[a][(2 - t) * channels : (3 - t) * channels] for t in range(3) for a in range(3)
             ]
             turned[b * channels : (b + 1) * channels, :] = jnp.concatenate(blocks, axis=1).astype(
                 bf16
@@ -143,19 +143,33 @@
         vec[k] = jnp.transpose(jnp.broadcast_to(rows[k], (128, channels)))
 
 
-def offsets():
-    ta = lax.axis_index("ta")
+def per_core(body):
+    def run(*refs):
+        index = lax.axis_index("ta")
+        for core in range(2):
+            pl.when(index == core)(lambda: body(core, *refs))
+
+    return run
+
+
+def offsets(ta):
     return ta, 1 - ta, 4 * ta, 4 - 4 * ta
 
 
-taps_order = [(t, a) for a in range(3) for t in range(3)]
-
-
-def product(weights, ref, lead, f, row):
+forward_order = [(t, a) for a in range(3) for t in range(3)]
+gradient_order = [(t, a) for t in range(3) for a in range(3)]
+
+
+def gradient_taps(f):
+    return gradient_order[: 3 * min(3, 4 - f)]
+
+
+def product(weights, ref, lead, f, row, order):
     cols = [
-        jnp.concatenate([ref[lead + (f + t, row + i + a)] for t, a in taps_order], axis=0)
+        jnp.concatenate([ref[lead + (f + t, row + i + a)] for t, a in order], axis=0)
         for i in range(2)
     ]
+    weights = weights[:, : cols[0].shape[0]]
     return jnp.dot(weights, jnp.concatenate(cols, axis=1), preferred_element_type=f32)
 
 
@@ -167,12 +181,14 @@
 def partial_products(ws, AC, PV, which):
     for k in range(2):
         for pair in range(2):
-            PV[which, k, pair] = product(ws[which], AC, (which,), 2 * which + k, 2 * pair)
-
-
-def lead_body(m1, m2, oc, z1, z2, vec, ws, AC, M, PV):
+            f = 2 * which + k
+            order = gradient_taps(f) if which else forward_order
+            PV[which, k, pair] = product(ws[which], AC, (which,), f, 2 * pair, order)
+
+
+def lead_body(core, m1, m2, oc, z1, z2, vec, ws, AC, M, PV):
     A, C = AC.at[0], AC.at[1]
-    ta, other, zb, mb = offsets()
+    ta, other, zb, mb = offsets(core)
     gin = vec[0]
     for i in range(2):
         for r in range(2):
@@ -198,9 +214,6 @@
         A[other, r + 2 - 2 * ta] = oc[0, r]
     for k in range(3):
         M[other, k + 1 - ta] = oc[1, k + ta]
-    for e in range(6):
-        C[4, e] = jnp.zeros(m1.shape[1:], bf16)
-        C[5, e] = jnp.zeros(m1.shape[1:], bf16)
     partial_products(ws, AC, PV, ta)
 
 
@@ -213,7 +226,8 @@
 
 
 def second_products(f, M, D, w2, w1f):
-    return parts(product(w2[...], M, (), f, 0)), parts(product(w1f[...], D, (), f, 0))
+    forward = product(w2[...], M, (), f, 0, forward_order)
+    return parts(forward), parts(product(w1f[...], D, (), f, 0, gradient_taps(f)))
 
 
 def second_layer(f, mine, slot, out, both, PA, PC, vec, whole):
@@ -228,21 +242,21 @@
         out[1, slot, i] = cot + back if whole else back.astype(out.dtype)
 
 
-def own_body(m2, M, D, PA, PC, w2, w1f, vec, keep):
-    ta = lax.axis_index("ta")
+def own_body(core, m2, M, D, PA, PC, w2, w1f, vec, keep):
+    ta = core
     for slot in range(2):
         f = 2 * ta + slot
         second_layer(f, m2, slot, keep, second_products(f, M, D, w2, w1f), PA, PC, vec, True)
 
 
 def main_body(
-    AC_in, M_in, PV_in, sp, edge, e1, e2, ws, w2, w1f, vec,
+    core, AC_in, M_in, PV_in, sp, edge, e1, e2, ws, w2, w1f, vec,
     AC, M, PV, D, PA, PC, send, EA, EC,
 ):
     A, C, w1, w2f = AC.at[0], AC.at[1], ws.at[0], ws.at[1]
     channels = sp.shape[1]
     tile = (channels, 128)
-    ta, other, _, mb = offsets()
+    ta, other, _, mb = offsets(core)
     ha = lax.axis_index("ha")
     wa = lax.axis_index("wa")
     first_row = (ta == 1) | (ha > 0)
@@ -261,10 +275,6 @@
             ):
                 A[2 + frame, row] = act(src[at].astype(f32), gin).astype(bf16)
                 C[frame, row] = src[at + 4]
-    for e in range(4):
-        D[4, e] = jnp.zeros(tile, bf16)
-        D[5, e] = jnp.zeros(tile, bf16)
-
     own, par, zo, zp = (t[...].astype(f32) for t in (edge, sp.at[16], e1, e2))
 
     def placed(t, slot, start, rows_from, rows, to):
@@ -279,8 +289,7 @@
             mine += placed(zo, first + i, 32 * i, 2 - 2 * ta, 2, 4 * ta)
             yours += placed(par, first + i, 32 * i, 0, 4, 2 - 2 * ta)
             yours += placed(zp, first + i, 32 * i, 2 - 2 * ta, 2, 4 * ta)
-        g0 = jnp.where(ta == 0, mine, yours)
-        g1 = jnp.where(ta == 0, yours, mine)
+        g0, g1 = (mine, yours) if ta == 0 else (yours, mine)
         return g0 + pltpu.roll(g1, 64, 1)
 
     def caches(slot):
@@ -289,16 +298,15 @@
         out += placed(par, slot, 32 * other, 0, 4, 2 - 2 * ta)
         return out + placed(zp, slot, 32 * other, 2 - 2 * ta, 2, 4 * ta)
 
-    def edge_products(w, low, high, last=False):
+    def edge_products(w, low, high, order, last=False):
         pieces = []
-        for t, a in taps_order:
+        for t, a in order:
             s = 32 * t + 4 * a
             if s == 0:
                 pieces.append(low.astype(bf16))
                 continue
-            moved = pltpu.roll(low, 128 - s, 1)
-            beyond = 0.0 if high is None else pltpu.roll(high, 128 - s, 1)
-            pieces.append(jnp.where(lane < 128 - s, moved, beyond).astype(bf16))
+            joined = jnp.where(lane < s, 0.0 if high is None else high, low)
+            pieces.append(pltpu.roll(joined, 128 - s, 1).astype(bf16))
         stacked = jnp.concatenate(pieces, axis=0)
         if last:
             outer = jnp.concatenate([w[:channels, :], w[2 * channels :, :]], axis=0)
@@ -316,19 +324,20 @@
         edge_ref[...] = edge_ref[...] + jnp.where(here, moved, 0.0)
 
     def first_products(f, pair):
-        forward = PV[0, f, pair] if f < 2 else product(w1[...], A, (), f, 2 * pair)
-        gradient = PV[1, f - 2, pair] if f > 1 else product(w2f[...], C, (), f, 2 * pair)
+        forward = PV[0, f, pair] if f < 2 else product(w1[...], A, (), f, 2 * pair, forward_order)
+        gradient = PV[1, f - 2, pair] if f > 1 else product(w2f[...], C, (), f, 2 * pair, gradient_taps(f))
         return parts(forward), parts(gradient)
 
     partial_products(ws, AC, PV, other)
     act_edges = pltpu.roll(act(group(0), gin), 64, 1)
     cin_edges = caches(4)
     across, own_part = edge_products(
-        w1, jnp.where(lane < 64, cin_edges, act_edges), jnp.where(lane < 64, act_edges, 0.0)
+        w1, jnp.where(lane < 64, cin_edges, act_edges), jnp.where(lane < 64, act_edges, 0.0),
+        forward_order,
     )
     PA[...] = across
     EA[...] = own_part
-    across, own_part = edge_products(w2f, group(2), None)
+    across, own_part = edge_products(w2f, group(2), None, gradient_order)
     PC[...] = across
     EC[...] = own_part
     cmid_edges = pltpu.roll(caches(5), 124, 1)
@@ -356,7 +365,7 @@
     for f in range(4):
         first_layer(f)
 
-    late = [second_products(2 * other + slot, M, D, w2, w1f) for slot in range(2)]
+    late = [second_products(2 * other, M, D, w2, w1f)]
     hidden = (EA[...] + bin_).astype(bf16).astype(f32)
     a, d = act_and_back(hidden, gmid, EC[...])
     row = (lane % 32) // 4
@@ -366,8 +375,9 @@
     d = jnp.where(inside, d, 0.0).astype(bf16).astype(f32)
     a = pltpu.roll(a, 64, 1)
     low = jnp.where(lane < 64, cmid_edges, a)
-    PA[...] = edge_products(w2, low, jnp.where(lane < 64, a, 0.0), last=True)
-    PC[...] = edge_products(w1f, d, None, last=True)
+    PA[...] = edge_products(w2, low, jnp.where(lane < 64, a, 0.0), forward_order, last=True)
+    PC[...] = edge_products(w1f, d, None, gradient_order, last=True)
+    late.append(second_products(2 * other + 1, M, D, w2, w1f))
 
     for slot in range(2):
         second_layer(2 * other + slot, sp, slot, send, late[slot], PA, PC, vec, False)
@@ -481,7 +491,7 @@
         pltpu.VMEM((2, 2, 2, 3 * c, 2 * width), f32),
     )
     AC, M, PV = pl.pallas_call(
-        lead_body,
+        per_core(lead_body),
         in_specs=[VM] * 7,
         out_specs=(VM,) * 3,
         out_shape=staged,
@@ -490,7 +500,7 @@
     )(*near(m1, m2, oc, z1, z2, vec, ws))
     half = pltpu.VMEM((2, 2, 2) + tile, f32)
     AC, M, PV, D, PA, PC, send = pl.pallas_call(
-        main_body,
+        per_core(main_body),
         in_specs=[VM] * 11,
         out_specs=(VM,) * 7,
         out_shape=staged
@@ -507,7 +517,7 @@
     )(*near(AC, M, PV, sp, edge, e1, e2, ws, w2, w1f, vec))
     got = lax.ppermute(send, "ta", [(0, 1), (1, 0)])
     keep = pl.pallas_call(
-        own_body,
+        per_core(own_body),
         in_specs=[VM] * 8,
         out_specs=VM,
         out_shape=half,

time: 73.3 us -> 73 us (level)
  Pallas kernels: 10.2 us -> 9.28 us
    pallas_call x3, Pallas kernels: 6.18 us -> 5.27 us  [the longest x1 3.85 us: per_device(): pl.pallas_call(per_core(main_body), in_specs=[VM] * 11, out_specs=(VM,) *...]
where the time goes in v9:
time: 73 us; the launch traced here: 72.7 us
  starting transfers between devices  58.8 us (81%)
  Pallas kernels  9.28 us (13%)
  waiting for transfers between devices  3.84 us (5%)
  between operations  0.78 us (1%)
    ppermute x1, starting transfers between devices, per_device(): sp = lax.ppermute(sw, 'ta', [(0, 1), (1, 0)])  41.2 us
    ppermute x1, starting transfers between devices, per_device(): first = lax.ppermute(ed, 'wa', pairs(0))  6.73 us
    pallas_call x1, Pallas kernels, per_device(): pl.pallas_call(per_core(main_body), in_specs=[VM] * 11, out_specs=(VM,) *...  3.85 us
    ppermute x1, starting transfers between devices, per_device(): e2 = lax.ppermute(edge, ('ha', 'ta'), two)  3.67 us
    ppermute x1, starting transfers between devices, per_device(): got = lax.ppermute(send, 'ta', [(0, 1), (1, 0)])  1.95 us
    ppermute x1, starting transfers between devices, per_device(): z2 = lax.ppermute(m2, ('ha', 'ta'), two)  1.95 us
    pallas_call x1, Pallas kernels, per_device(): pl.pallas_call(fetch_body, in_specs=[HB] * 9, out_specs=(VM,) * 4, out_sh...  1.9 us
  transfers between devices with their start and end apart: 8, of which 4 were waited for; matrix products, arithmetic and copies ran while one was open for 0% of the time, Pallas kernels for 4%

profile of v9, /device:TPU:65, one launch (start us, length us, event | category | flops | bytes accessed | tf_op | source)
XLA Modules:
  0.0 72.7 jit_solution(16356541271516242646)
XLA Ops:
  0.6 0.0 copy-start
  0.6 1.9 %fetch.1 = (bf16[96,128]{1,0:T(8,128)(2,1)S(1)}, f32[8,384,128]{2,1,0:T(8,128)S(1)}, bf16[3,288,288]{2,1,0:T(8,128)(2,1)S(1)}, f32[4,1,96]{2,1,0:T(1,128)S(1)}) custom-call(bf16[768,128]{1,0:T(8,128)(2,1)} %bitcast.14, bf16[768,128]{1,0:T(8,128)(2,1)} %bitcast.15, bf16[768,128]{1,0:T(8,128)(2,1)} %bitcast.16, bf16[768,128]{1,0:T(8,128)(2,1)} %bitcast.17, ...), custom_call_target="tpu_custom_call" | custom-call | tf_op jit(solution)/shard_map/fetch/pallas_call | solution.py:411
  2.6 0.7 collective-permute-start.3
  3.2 6.7 %collective-permute-start.2 = (bf16[96,128]{1,0:T(8,128)(2,1)S(1)}, bf16[96,128]{1,0:T(8,128)(2,1)S(1)}, u32[]{:S(2)}, u32[]{:S(2)}) collective-permute-start(bf16[96,128]{1,0:T(8,128)(2,1)S(1)} %get-tuple-element.37), channel_id=1, source_target_pairs={{0,2},{2,0},{4,6},{6,4},{8,10},{10,8},{12,14},{14,12},{1,3},{3,1},... | collective-permute-start | bytes 73736 | tf_op jit(solution)/shard_map/ppermute | solution.py:458
  10.0 0.1 pack.1
  10.1 0.0 collective-permute-done.3.second
  10.1 1.0 %collective-permute-done.2.first = bf16[96,128]{1,0:T(8,128)(2,1)S(1)} collective-permute-done((bf16[96,128]{1,0:T(8,128)(2,1)S(1)}, bf16[96,128]{1,0:T(8,128)(2,1)S(1)}, u32[]{:S(2)}, u32[]{:S(2)}) %collective-permute-start.2) | collective-permute-done | bytes 24608 | tf_op jit(solution)/shard_map/ppermute | solution.py:458
  11.2 41.2 %collective-permute-start.4 = (bf16[17,96,128]{2,1,0:T(8,128)(2,1)S(1)}, bf16[17,96,128]{2,1,0:T(8,128)(2,1)S(1)}, u32[]{:S(2)}, u32[]{:S(2)}) collective-permute-start(bf16[17,96,128]{2,1,0:T(8,128)(2,1)S(1)} %get-tuple-element.39), channel_id=1, source_target_pairs={{0,1},{1,0},{2,3},{3,2},{4,5},{5,4},{6,7},{7,6},{8,9},{9,8},{10,11... | collective-permute-start | bytes 1253384 | tf_op jit(solution)/shard_map/ppermute | solution.py:470
  52.4 1.3 %collective-permute-start = (bf16[12,96,128]{2,1,0:T(8,128)(2,1)S(1)}, bf16[12,96,128]{2,1,0:T(8,128)(2,1)S(1)}, u32[]{:S(2)}, u32[]{:S(2)}) collective-permute-start(bf16[12,96,128]{2,1,0:T(8,128)(2,1)S(1)} %get-tuple-element.28.refs_0_.m1), channel_id=1, source_target_pairs={{0,16},{16,32},{32,48},{48,64},{64,80},{80,96},{96,112},{112,128},... | collective-permute-start | bytes 884744 | tf_op jit(solution)/shard_map/ppermute | solution.py:459
  53.7 2.0 %collective-permute-start.1 = (bf16[12,96,128]{2,1,0:T(8,128)(2,1)S(1)}, bf16[12,96,128]{2,1,0:T(8,128)(2,1)S(1)}, u32[]{:S(2)}, u32[]{:S(2)}) collective-permute-start(bf16[12,96,128]{2,1,0:T(8,128)(2,1)S(1)} %get-tuple-element.27.after.refs_1_.refs_0_), channel_id=1, source_target_pairs={{16,1},{32,17},{48,33},{64,49},{80,65},{96,81},{112,97},{128,113},... | collective-permute-start | bytes 884744 | tf_op jit(solution)/shard_map/ppermute | solution.py:460
  55.6 3.7 %collective-permute-start.6 = (bf16[96,128]{1,0:T(8,128)(2,1)S(1)}, bf16[96,128]{1,0:T(8,128)(2,1)S(1)}, u32[]{:S(2)}, u32[]{:S(2)}) collective-permute-start(bf16[96,128]{1,0:T(8,128)(2,1)S(1)} %get-tuple-element.40.refs_4_), channel_id=1, source_target_pairs={{16,1},{32,17},{48,33},{64,49},{80,65},{96,81},{112,97},{128,113},... | collective-permute-start | bytes 73736 | tf_op jit(solution)/shard_map/ppermute | solution.py:472
  59.3 1.3 %collective-permute-start.5 = (bf16[96,128]{1,0:T(8,128)(2,1)S(1)}, bf16[96,128]{1,0:T(8,128)(2,1)S(1)}, u32[]{:S(2)}, u32[]{:S(2)}) collective-permute-start(bf16[96,128]{1,0:T(8,128)(2,1)S(1)} %get-tuple-element.40.refs_4_), channel_id=1, source_target_pairs={{0,16},{16,32},{32,48},{48,64},{64,80},{80,96},{96,112},{112,128},... | collective-permute-start | bytes 73736 | tf_op jit(solution)/shard_map/ppermute | solution.py:471
  60.6 0.0 copy-done
  60.6 1.1 %weights.1 = (bf16[2,288,864]{2,1,0:T(8,128)(2,1)S(1)}, bf16[288,864]{1,0:T(8,128)(2,1)S(1)}, bf16[288,864]{1,0:T(8,128)(2,1)S(1)}, f32[4,96,128]{2,1,0:T(8,128)S(1)}) custom-call(bf16[3,288,288]{2,1,0:T(8,128)(2,1)S(1)} %bitcast.12, bf16[3,288,288]{2,1,0:T(8,128)(2,1)S(1)} %get-tuple-element.30.wmid, f32[4,1,96]{2,1,0:T(1,128)S(1)} %get-tuple-element.31.rows, ...), custom_call_target="tpu_custom_call" | custom-call | tf_op jit(solution)/shard_map/weights/pallas_call | solution.py:475
  61.7 0.0 collective-permute-done.refs_3_
  61.7 1.3 %collective-permute-done.1.refs_4_ = bf16[12,96,128]{2,1,0:T(8,128)(2,1)S(1)} collective-permute-done((bf16[12,96,128]{2,1,0:T(8,128)(2,1)S(1)}, bf16[12,96,128]{2,1,0:T(8,128)(2,1)S(1)}, u32[]{:S(2)}, u32[]{:S(2)}) %collective-permute-start.1) | collective-permute-done | bytes 294944 | tf_op jit(solution)/shard_map/ppermute | solution.py:460
  63.0 0.6 lead.1
  63.6 0.0 collective-permute-done.6.refs_6_
  63.6 0.9 %collective-permute-done.5.refs_5_ = bf16[96,128]{1,0:T(8,128)(2,1)S(1)} collective-permute-done((bf16[96,128]{1,0:T(8,128)(2,1)S(1)}, bf16[96,128]{1,0:T(8,128)(2,1)S(1)}, u32[]{:S(2)}, u32[]{:S(2)}) %collective-permute-start.5) | collective-permute-done | bytes 24608 | tf_op jit(solution)/shard_map/ppermute | solution.py:471
  64.6 0.0 collective-permute-done.4.refs_3_
  64.6 3.8 %block.1 = (bf16[2,6,6,96,128]{4,3,2,1,0:T(8,128)(2,1)S(1)}, bf16[6,4,96,128]{3,2,1,0:T(8,128)(2,1)S(1)}, f32[2,2,2,288,256]{4,3,2,1,0:T(8,128)S(1)}, bf16[6,4,9...) custom-call(bf16[2,6,6,96,128]{4,3,2,1,0:T(8,128)(2,1)S(1)} %get-tup, ...), custom_call_target="tpu_custom_call", output_to_operand_aliasing={{0}: (0, {}), {1}: (1, {}), {2}: (2, {})} | custom-call | tf_op jit(solution)/shard_map/block/pallas_call | solution.py:502
  68.4 2.0 %collective-permute-start.7 = (bf16[2,2,2,96,128]{4,3,2,1,0:T(8,128)(2,1)S(1)}, bf16[2,2,2,96,128]{4,3,2,1,0:T(8,128)(2,1)S(1)}, u32[]{:S(2)}, u32[]{:S(2)}) collective-permute-start(bf16[2,2,2,96,128]{4,3,2,1,0:T(8,128)(2,1)S(1)} %get-tuple-element.47), channel_id=1, source_target_pairs={{0,1},{1,0},{2,3},{3,2},{4,5},{5,4},{6,7},{7,6},{8,9},{9,8},{10,11... | collective-permute-start | bytes 589832 | tf_op jit(solution)/shard_map/ppermute | solution.py:518
  70.4 0.8 %own.1.keep = f32[2,2,2,96,128]{4,3,2,1,0:T(8,128)S(1)} custom-call(bf16[12,96,128]{2,1,0:T(8,128)(2,1)S(1)} %get-tuple-element.27.after.refs_1_.refs_0_, bf16[6,4,96,128]{3,2,1,0:T(8,128)(2,1)S(1)} %get-tuple-element.43.refs_1_, bf16[6,4,96,128]{3,2,1,0:T(8,128)(2,1)S(1)} %get-tuple-element.44.refs_2_, f32[96,128]{1,0:T(8,128)S(1)} %get-tuple-element.45.refs_3_, ...), custom_call_target="tpu_custom_call" | custom-call | tf_op jit(solution)/shard_map/own/pallas_call | solution.py:519
  71.2 0.6 collective-permute-done.7.got
  71.8 0.9 %assemble.1 = (bf16[768,128]{1,0:T(8,128)(2,1)}, f32[768,128]{1,0:T(8,128)}) custom-call(f32[2,2,2,96,128]{4,3,2,1,0:T(8,128)S(1)} %own.1.keep, bf16[2,2,2,96,128]{4,3,2,1,0:T(8,128)(2,1)S(1)} %collective-permute-done.7.got, bf16[12,96,128]{2,1,0:T(8,128)(2,1)S(1)} %get-tuple-element.28.refs_0_.m1), custom_call_target="tpu_custom_call" | custom-call | tf_op jit(solution)/shard_map/assemble/pallas_call | solution.py:527
  (1 shorter events, 0.0 us)
Async XLA Ops:
  0.6 60.0 %copy-start = (bf16[3,3,96,288]{3,2,1,0:T(8,128)(2,1)S(1)}, bf16[3,3,96,288]{3,2,1,0:T(8,128)(2,1)}, u32[]{:S(2)}) copy-start(bf16[3,3,96,288]{3,2,1,0:T(8,128)(2,1)} %param.15) | copy-start | bytes 1492996
  2.6 7.6 %collective-permute-start.3 = (bf16[96,128]{1,0:T(8,128)(2,1)S(1)}, bf16[96,128]{1,0:T(8,128)(2,1)S(1)}, u32[]{:S(2)}, u32[]{:S(2)}) collective-permute-start(bf16[96,128]{1,0:T(8,128)(2,1)S(1)} %get-tuple-element.37), channel_id=1, source_target_pairs={{2,4},{4,2},{6,8},{8,6},{10,12},{12,10},{3,5},{5,3},{7,9},{9,7},{1... | collective-permute-start | bytes 73736 | tf_op jit(solution)/shard_map/ppermute | solution.py:457
  3.2 7.9 %collective-permute-start.2 = (bf16[96,128]{1,0:T(8,128)(2,1)S(1)}, bf16[96,128]{1,0:T(8,128)(2,1)S(1)}, u32[]{:S(2)}, u32[]{:S(2)}) collective-permute-start(bf16[96,128]{1,0:T(8,128)(2,1)S(1)} %get-tuple-element.37), channel_id=1, source_target_pairs={{0,2},{2,0},{4,6},{6,4},{8,10},{10,8},{12,14},{14,12},{1,3},{3,1},... | collective-permute-start | bytes 73736 | tf_op jit(solution)/shard_map/ppermute | solution.py:458
  11.2 53.4 %collective-permute-start.4 = (bf16[17,96,128]{2,1,0:T(8,128)(2,1)S(1)}, bf16[17,96,128]{2,1,0:T(8,128)(2,1)S(1)}, u32[]{:S(2)}, u32[]{:S(2)}) collective-permute-start(bf16[17,96,128]{2,1,0:T(8,128)(2,1)S(1)} %get-tuple-element.39), channel_id=1, source_target_pairs={{0,1},{1,0},{2,3},{3,2},{4,5},{5,4},{6,7},{7,6},{8,9},{9,8},{10,11... | collective-permute-start | bytes 1253384 | tf_op jit(solution)/shard_map/ppermute | solution.py:470
  52.4 9.4 %collective-permute-start = (bf16[12,96,128]{2,1,0:T(8,128)(2,1)S(1)}, bf16[12,96,128]{2,1,0:T(8,128)(2,1)S(1)}, u32[]{:S(2)}, u32[]{:S(2)}) collective-permute-start(bf16[12,96,128]{2,1,0:T(8,128)(2,1)S(1)} %get-tuple-element.28.refs_0_.m1), channel_id=1, source_target_pairs={{0,16},{16,32},{32,48},{48,64},{64,80},{80,96},{96,112},{112,128},... | collective-permute-start | bytes 884744 | tf_op jit(solution)/shard_map/ppermute | solution.py:459
  53.7 9.3 %collective-permute-start.1 = (bf16[12,96,128]{2,1,0:T(8,128)(2,1)S(1)}, bf16[12,96,128]{2,1,0:T(8,128)(2,1)S(1)}, u32[]{:S(2)}, u32[]{:S(2)}) collective-permute-start(bf16[12,96,128]{2,1,0:T(8,128)(2,1)S(1)} %get-tuple-element.27.after.refs_1_.refs_0_), channel_id=1, source_target_pairs={{16,1},{32,17},{48,33},{64,49},{80,65},{96,81},{112,97},{128,113},... | collective-permute-start | bytes 884744 | tf_op jit(solution)/shard_map/ppermute | solution.py:460
  55.6 8.0 %collective-permute-start.6 = (bf16[96,128]{1,0:T(8,128)(2,1)S(1)}, bf16[96,128]{1,0:T(8,128)(2,1)S(1)}, u32[]{:S(2)}, u32[]{:S(2)}) collective-permute-start(bf16[96,128]{1,0:T(8,128)(2,1)S(1)} %get-tuple-element.40.refs_4_), channel_id=1, source_target_pairs={{16,1},{32,17},{48,33},{64,49},{80,65},{96,81},{112,97},{128,113},... | collective-permute-start | bytes 73736 | tf_op jit(solution)/shard_map/ppermute | solution.py:472
  59.3 5.2 %collective-permute-start.5 = (bf16[96,128]{1,0:T(8,128)(2,1)S(1)}, bf16[96,128]{1,0:T(8,128)(2,1)S(1)}, u32[]{:S(2)}, u32[]{:S(2)}) collective-permute-start(bf16[96,128]{1,0:T(8,128)(2,1)S(1)} %get-tuple-element.40.refs_4_), channel_id=1, source_target_pairs={{0,16},{16,32},{32,48},{48,64},{64,80},{80,96},{96,112},{112,128},... | collective-permute-start | bytes 73736 | tf_op jit(solution)/shard_map/ppermute | solution.py:471
  68.4 3.4 %collective-permute-start.7 = (bf16[2,2,2,96,128]{4,3,2,1,0:T(8,128)(2,1)S(1)}, bf16[2,2,2,96,128]{4,3,2,1,0:T(8,128)(2,1)S(1)}, u32[]{:S(2)}, u32[]{:S(2)}) collective-permute-start(bf16[2,2,2,96,128]{4,3,2,1,0:T(8,128)(2,1)S(1)} %get-tuple-element.47), channel_id=1, source_target_pairs={{0,1},{1,0},{2,3},{3,2},{4,5},{5,4},{6,7},{7,6},{8,9},{9,8},{10,11... | collective-permute-start | bytes 589832 | tf_op jit(solution)/shard_map/ppermute | solution.py:518
